TPU v7x, 16 devices: a whole 2x2x2 slice. The times are simulated.
16 devices in a mesh: tp: 2 (over z), dp: 8 (over y, x, core).
Axes of the slice: x: 2, y: 2, z: 2, core: 2. Of those that a mesh axis runs over, the one named last changes fastest.
Arguments:
- h_main: bfloat16 [8, 512, 2048], P('dp')
- h_mtp: bfloat16 [8, 512, 2048], P('dp')
- labels_main: int32 [8, 512], P('dp')
- labels_mtp: int32 [8, 512], P('dp')
- weight_main: float32 [8, 512], P('dp')
- weight_mtp: float32 [8, 512], P('dp')
- gain_final: float32 [2048], replicated
- gain_mtp: float32 [2048], replicated
- w_out: bfloat16 [2048, 32256], P(None, 'tp')
Outputs:
- output 1: float32 [], replicated
- output 2: bfloat16 [8, 512, 2048], P('dp')
- output 3: bfloat16 [8, 512, 2048], P('dp')
- output 4: float32 [2048, 32256], P('dp', 'tp')
- output 5: float32 [2048], replicated
- output 6: float32 [2048], replicated
All inputs are finite; a program needn't handle non-finite values.
Results may differ from a plain program's by a relative error of at most 0.00844002.
Values sent between devices are 32-bit elements.
A program may use at most 1 GiB of HBM per device.

v0:
```python
import jax
import jax.numpy as jnp
from jax import lax
from jax.sharding import PartitionSpec as P

NORM_EPS = 1e-6
MTP_LAMBDA = 0.3


def solution(mesh):
    def local_step(h_main, h_mtp, labels_main, labels_mtp, weight_main, weight_mtp, gain_final, gain_mtp, w_out):
        batch_loc, seq_len, d_model = h_main.shape
        shard_vocab = w_out.shape[1]
        rows = batch_loc * seq_len
        weight_sums = lax.psum(jnp.stack([jnp.sum(weight_main), jnp.sum(weight_mtp)]), 'dp')
        loss_coefs = jnp.stack([1.0 / weight_sums[0], MTP_LAMBDA / weight_sums[1]])
        row_w = (jnp.stack([weight_main, weight_mtp]).reshape(2, rows) * loss_coefs[:, None]).reshape(2 * rows)
        x_rows = jnp.stack([h_main, h_mtp]).reshape(2, rows, d_model).astype(jnp.float32)
        gain_rows = jnp.stack([gain_final, gain_mtp])[:, None, :]
        inv_rms = lax.rsqrt(jnp.mean(x_rows * x_rows, axis=-1, keepdims=True) + NORM_EPS)
        normed = x_rows * inv_rms
        u_rows = (normed * gain_rows).astype(jnp.bfloat16).reshape(2 * rows, d_model)
        logits = jnp.dot(u_rows, w_out, preferred_element_type=jnp.float32)
        vocab_start = lax.axis_index('tp') * shard_vocab
        local_labels = jnp.stack([labels_main, labels_mtp]).reshape(2 * rows) - vocab_start
        is_target = jnp.arange(shard_vocab, dtype=jnp.int32)[None, :] == local_labels[:, None]
        row_max = lax.pmax(jnp.max(logits, axis=-1), 'tp')
        shifted = jnp.exp(logits - row_max[:, None])
        row_stats = lax.psum(jnp.stack([jnp.sum(shifted, axis=-1), jnp.sum(jnp.where(is_target, logits, 0.0), axis=-1)]), 'tp')
        log_norm = row_max + jnp.log(row_stats[0])
        loss_total = lax.psum(jnp.sum(row_w * (log_norm - row_stats[1])), 'dp')
        soft_probs = shifted * (1.0 / row_stats[0])[:, None]
        grad_z = (row_w[:, None] * jnp.where(is_target, soft_probs - 1.0, soft_probs)).astype(jnp.bfloat16)
        grad_w = lax.dot_general(u_rows, grad_z, (((0,), (0,)), ((), ())), preferred_element_type=jnp.float32)
        grad_w = lax.psum_scatter(grad_w, 'dp', scatter_dimension=0, tiled=True)
        grad_part = lax.dot_general(grad_z, w_out, (((1,), (1,)), ((), ())), preferred_element_type=jnp.float32).astype(jnp.bfloat16)
        grad_u = lax.psum(grad_part.astype(jnp.float32), 'tp').reshape(2, rows, d_model)
        grad_normed = grad_u * gain_rows
        grad_gain = lax.psum(jnp.sum(grad_u * normed, axis=1), 'dp')
        grad_x = inv_rms * (grad_normed - normed * jnp.mean(grad_normed * normed, axis=-1, keepdims=True))
        grad_h = grad_x.astype(jnp.bfloat16).reshape(2, batch_loc, seq_len, d_model)
        return loss_total, grad_h[0], grad_h[1], grad_w, grad_gain[0], grad_gain[1]

    row_spec = P('dp', None)
    return jax.shard_map(local_step, mesh=mesh, in_specs=(P('dp', None, None), P('dp', None, None), row_spec, row_spec, row_spec, row_spec, P(None), P(None), P(None, 'tp')), out_specs=(P(), P('dp', None, None), P('dp', None, None), P('dp', 'tp'), P(None), P(None)), check_vma=False)
```

profile of v0, /device:TPU:0, one launch (start us, length us, event | category | flops | bytes accessed | tf_op | source)
XLA Modules:
  0.0 1075.9 jit_solution(1824271877807530826)
XLA Ops:
  8.0 0.0 all-reduce.3.cloned.1.call-start
  8.0 1.3 reduce_sum.73
  9.3 1.3 reduce_sum.72
  10.6 1.4 pad_maximum_fusion.4
  12.0 15.4 %psum.35 = f32[2]{0:T(128)S(1)} all-reduce(f32[2]{0:T(128)S(1)} %pad_maximum_fusion.4), channel_id=1, replica_groups=mesh['tp'=2,'dp'=8] {'dp'}, use_global_device_ids=true, to_apply=%region_2.0 | all-reduce | flops 2 | bytes 16 | tf_op jit(solution)/shard_map/psum | solution.py:15
  27.4 0.6 fusion.10
  29.4 0.1 pad_maximum_fusion.5
  29.4 0.1 broadcast_bitcast_fusion
  29.5 0.6 copy.15
  30.1 2.7 fusion.6
  32.8 0.6 add_rsqrt_fusion
  33.4 0.7 pad_maximum_fusion.1
  34.1 0.6 copy-done.2
  34.7 2.7 fusion.3
  37.5 78.9 %fusion.11 = (f32[1024]{0:T(1024)S(1)}, f32[1024,16128]{1,0:T(8,128)}) fusion(bf16[1024,2048]{1,0:T(8,128)(2,1)S(1)} %fusion.3, bf16[2048,16128]{1,0:T(8,128)(2,1)} %param.17), kind=kOutput, calls=%fused_computation.36 | convolution fusion | flops 67662249984 | bytes 136318976 | tf_op jit(solution)/shard_map/dot_general | solution.py:23
  116.4 4.9 pmax.7
  121.4 25.2 %fusion.2 = (f32[1024]{0:T(1024)S(1)}, f32[1024]{0:T(1024)S(1)}) fusion(f32[1024,16128]{1,0:T(8,128)} %get-tuple-element.26, f32[1024]{0:T(1024)S(1)} %pmax.7, s32[1024]{0:T(1024)S(1)} %bitcast.68), kind=kLoop, calls=%fused_computation.6 | loop fusion | flops 82573312 | bytes 66076672 | tf_op jit(solution)/shard_map/reduce_sum | solution.py:29
  146.6 5.0 psum.36
  151.6 0.6 multiply_reduce_fusion.1
  152.2 33.1 %fusion.1 = bf16[1024,16128]{1,0:T(8,128)(2,1)} fusion(f32[1024,16128]{1,0:T(8,128)} %get-tuple-element.26, f32[1024]{0:T(1024)S(1)} %bitcast.70, f32[1024]{0:T(1024)S(1)} %get-tuple-element.11, s32[1024]{0:T(1024)S(1)} %bitcast.69, f32[1024]{0:T(1024)S(1)} %pmax.7), kind=kLoop, calls=%fused_computation.2 | loop fusion | flops 115605504 | bytes 99106816 | tf_op jit(solution)/shard_map/convert_element_type | solution.py:33
  185.3 78.2 %convert_convert_fusion = f32[1024,2048]{1,0:T(8,128)} fusion(bf16[1024,16128]{1,0:T(8,128)(2,1)} %fusion.1, bf16[2048,16128]{1,0:T(8,128)(2,1)} %param.17), kind=kOutput, calls=%fused_computation.19 | convolution fusion | flops 67649929216 | bytes 107479040 | tf_op jit(solution)/shard_map/dot_general | solution.py:36
  263.5 0.0 all-reduce.3.cloned.1.call-update
  263.6 0.3 reduce-scatter.2.cloned.1.call-start
  263.8 80.3 %fusion.12 = f32[2048,16128]{1,0:T(8,128)} fusion(bf16[1024,2048]{1,0:T(8,128)(2,1)} %copy-done.1, bf16[1024,16128]{1,0:T(8,128)(2,1)} %fusion.1), kind=kOutput, calls=%fused_computation.37 | convolution fusion | flops 67645734912 | bytes 169345024 | tf_op jit(solution)/shard_map/dot_general | solution.py:34
  344.1 0.0 reduce-scatter.2.cloned.1.call-update
  344.2 112.8 %all-reduce.3.cloned.1.call-done = f32[1024,2048]{1,0:T(8,128)} async-done(((f32[1024,2048]{1,0:T(8,128)}), f32[1024,2048]{1,0:T(8,128)}) %all-reduce.3.cloned.1.call-update) | async-done | bytes 8388624 | tf_op jit(solution)/shard_map/psum | solution.py:37
  457.0 4.9 fusion.5
  461.9 6.8 multiply_convert_fusion
  468.7 24.9 %all-reduce = (f32[]{:T(128)}, f32[2,2048]{1,0:T(2,128)S(1)}) all-reduce(f32[]{:T(128)} %get-tuple-element.10, f32[2,2048]{1,0:T(2,128)S(1)} %get-tuple-element.13), channel_id=1, replica_groups=mesh['tp'=2,'dp'=8] {'dp'}, use_global_device_ids=true, to_apply=%region_10.11 | all-reduce | flops 4097 | bytes 32776 | tf_op jit(solution)/shard_map/psum | solution.py:31
  493.6 0.6 fusion.9
  494.2 4.8 fusion.8
  499.0 569.4 %reduce-scatter.2.cloned.1.call-done = f32[256,16128]{1,0:T(8,128)} async-done(((f32[2048,16128]{1,0:T(8,128)}), f32[256,16128]{1,0:T(8,128)}) %reduce-scatter.2.cloned.1.call-update) | async-done | bytes 16515088 | tf_op jit(solution)/shard_map/reduce_scatter | solution.py:35
  (30 shorter events, 0.1 us)
Async XLA Ops:
  8.0 449.0 %all-reduce.3.cloned.1.call-start = ((), (), s32[]{:S(2)}) async-start(), calls=%async_computation.1 | async-start | bytes 16777216 | tf_op jit(solution)/shard_map/psum | solution.py:37
  33.4 0.8 copy-start.4
  34.1 0.6 copy-start.2
  37.5 79.0 %copy-start.1 = (bf16[1024,2048]{1,0:T(8,128)(2,1)}, bf16[1024,2048]{1,0:T(8,128)(2,1)S(1)}, u32[]{:S(2)}) copy-start(bf16[1024,2048]{1,0:T(8,128)(2,1)S(1)} %fusion.3) | copy-start | bytes 12582916
  37.5 83.9 %copy-start.10 = (s32[1,512]{1,0:T(1,128)S(1)}, s32[1,512]{1,0:T(1,128)}, u32[]{:S(2)}) copy-start(s32[1,512]{1,0:T(1,128)} %param.12) | copy-start | bytes 6148
  37.5 83.8 %copy-start.11 = (s32[1,512]{1,0:T(1,128)S(1)}, s32[1,512]{1,0:T(1,128)}, u32[]{:S(2)}) copy-start(s32[1,512]{1,0:T(1,128)} %param.11) | copy-start | bytes 6148
  121.3 30.2 %copy-start.8 = (f32[1,512]{1,0:T(1,128)S(1)}, f32[1,512]{1,0:T(1,128)}, u32[]{:S(2)}) copy-start(f32[1,512]{1,0:T(1,128)} %param.14) | copy-start | bytes 6148
  121.3 30.2 %copy-start.9 = (f32[1,512]{1,0:T(1,128)S(1)}, f32[1,512]{1,0:T(1,128)}, u32[]{:S(2)}) copy-start(f32[1,512]{1,0:T(1,128)} %param.13) | copy-start | bytes 6148
  121.4 30.3 %copy-start.6 = (f32[1,4,2,128]{3,1,2,0:T(4,128)S(1)}, f32[1,4,2,128]{3,1,2,0:T(4,128)}, u32[]{:S(2)}) copy-start(f32[1,4,2,128]{3,1,2,0:T(4,128)} %copy.15) | copy-start | bytes 12292
  263.6 804.9 %reduce-scatter.2.cloned.1.call-start = ((), (), s32[]{:S(2)}) async-start(), calls=%async_computation.2 | async-start | bytes 148635648 | tf_op jit(solution)/shard_map/reduce_scatter | solution.py:35
  344.1 112.8 %copy-start = (bf16[1,512,2048]{2,1,0:T(8,128)(2,1)S(1)}, bf16[1,512,2048]{2,1,0:T(8,128)(2,1)}, u32[]{:S(2)}) copy-start(bf16[1,512,2048]{2,1,0:T(8,128)(2,1)} %param.10) | copy-start | bytes 6291460
  344.1 112.8 %copy-start.3 = (f32[2,2048]{1,0:T(2,128)S(1)}, f32[2,2048]{1,0:T(2,128)}, u32[]{:S(2)}) copy-start(f32[2,2048]{1,0:T(2,128)} %copy-done.2) | copy-start | bytes 49156
  344.1 112.8 %copy-start.5 = (f32[1,4,2,128]{3,1,2,0:T(4,128)S(1)}, f32[1,4,2,128]{3,1,2,0:T(4,128)}, u32[]{:S(2)}) copy-start(f32[1,4,2,128]{3,1,2,0:T(4,128)} %copy-done.4) | copy-start | bytes 12292
  344.2 117.7 %copy-start.7 = (f32[2,512]{1,0:T(2,128)S(1)}, f32[2,512]{1,0:T(2,128)}, u32[]{:S(2)}) copy-start(f32[2,512]{1,0:T(2,128)} %get-tuple-element.21) | copy-start | bytes 12292
Sparse Core Ops, SparseCore 0:
  263.7 193.2 all-reduce.2
Sparse Core Ops, SparseCore 1:
  344.2 724.2 reduce-scatter.1
where the time goes:
time: 1080 us
  waiting for transfers between devices  682 us (63%)
  matrix products  237 us (22%)
  other arithmetic  81.4 us (8%)
  blocking collectives  50.2 us (5%)
  between operations  17 us (2%)
    reduce_scatter x1, waiting for transfers between devices, local_step(): grad_w = lax.psum_scatter(grad_w, 'dp', scatter_dimension=0, tiled=True)  569 us
    psum x1, waiting for transfers between devices, local_step(): lax.psum(grad_part.astype(jnp.float32), 'tp').reshape(2, rows, d_model)  113 us
    dot_general x1, matrix products, local_step(): lax.dot_general(u_rows, grad_z, (((0,), (0,)), ((), ())), preferred_eleme...  80.3 us
    dot_general x1, matrix products, local_step(): logits = jnp.dot(u_rows, w_out, preferred_element_type=jnp.float32)  78.9 us
    dot_general x1, matrix products, local_step(): lax.dot_general(grad_z, w_out, (((1,), (1,)), ((), ())), preferred_elemen...  78.2 us
    convert_element_type x1, other arithmetic, local_step(): (row_w[:, None] * jnp.where(is_target, soft_probs - 1.0, soft_probs)).ast...  33.1 us
    reduce_sum x1, other arithmetic, local_step(): jnp.sum(shifted, axis=-1)  25.2 us
    psum x1, blocking collectives, local_step(): loss_total = lax.psum(jnp.sum(row_w * (log_norm - row_stats[1])), 'dp')  24.9 us
  transfers between devices with their start and end apart: 2, of which 2 were waited for; matrix products, arithmetic and copies ran while one was open for 9% of the time, Pallas kernels for 0%

commit v1 on v0

v1 whole, which is shorter than its diff:
```python
import functools

import jax
import jax.numpy as jnp
from jax import lax
from jax.experimental import pallas as pl
from jax.experimental.pallas import tpu as pltpu
from jax.sharding import PartitionSpec as P


NORM_EPS = 1e-6
MTP_LAMBDA = 0.3
BLOCK_COLS = 4096
TILE = 2304
NARROW = 256
VMEM_LIMIT = 60 * 1024 * 1024
NN = (((1,), (0,)), ((), ()))
NT = (((1,), (1,)), ((), ()))


def params(*semantics):
    return pltpu.CompilerParams(dimension_semantics=semantics, vmem_limit_bytes=VMEM_LIMIT)


HBM = pl.BlockSpec(memory_space=pl.ANY)


def norm_kernel(tp_ref, h0_ref, h1_ref, gain_ref, _, u_ref, near_ref, c0_ref, c1a_ref, c1b_ref):
    head, b = pl.program_id(0), pl.program_id(1)

    def rows_of(h_ref):
        x = h_ref[0].astype(jnp.float32)
        return x * lax.rsqrt(jnp.mean(x * x, axis=-1, keepdims=True) + NORM_EPS)

    for i, h_ref in enumerate((h0_ref, h1_ref)):
        @pl.when(head == i)
        def _():
            u = rows_of(h_ref) * gain_ref[i:i + 1, :]
            u_ref[...] = u.astype(jnp.bfloat16)

            @pl.when(b == tp_ref[0])
            def _():
                near_ref[...] = u

            if i == 0:
                @pl.when(b >= 2)
                def _():
                    c0_ref[...] = u
            else:
                @pl.when(b == 2)
                def _():
                    c1a_ref[...] = u

                @pl.when(b == 3)
                def _():
                    c1b_ref[...] = u


def run_norm(tp, h0, h1, gains, dep):
    _, rows, d = h0.shape
    q = rows // 4
    f32 = jnp.float32
    blk = lambda f: pl.BlockSpec((q, d), f)
    return pl.pallas_call(
        norm_kernel,
        out_shape=(jax.ShapeDtypeStruct((2 * rows, d), jnp.bfloat16), jax.ShapeDtypeStruct((2 * q, d), f32), jax.ShapeDtypeStruct((2 * q, d), f32), jax.ShapeDtypeStruct((q, d), f32), jax.ShapeDtypeStruct((q, d), f32)),
        grid_spec=pltpu.PrefetchScalarGridSpec(
            num_scalar_prefetch=1, grid=(2, 4),
            in_specs=[pl.BlockSpec((1, q, d), lambda h, b, s: (0, jnp.where(h == 0, b, 3), 0)), pl.BlockSpec((1, q, d), lambda h, b, s: (0, jnp.where(h == 0, 0, b), 0)), pl.BlockSpec((2, d), lambda h, b, s: (0, 0)), HBM],
            out_specs=(blk(lambda h, b, s: (4 * h + b, 0)), blk(lambda h, b, s: (h, 0)), blk(lambda h, b, s: (jnp.where(h == 0, jnp.maximum(b - 2, 0), 1), 0)), blk(lambda h, b, s: (0, 0)), blk(lambda h, b, s: (0, 0)))),
        compiler_params=params("arbitrary", "arbitrary"),
        cost_estimate=pl.CostEstimate(flops=8 * rows * d * 1000, bytes_accessed=14 * rows * d, transcendentals=rows),
        name="norm",
    )(tp, h0, h1, gains, dep)


def norm_back_kernel(h_ref, a_ref, b_ref, gain_ref, _, out_ref, gg_ref):
    @pl.when(pl.program_id(0) == 0)
    def _():
        gg_ref[...] = jnp.zeros_like(gg_ref)

    x = h_ref[0].astype(jnp.float32)
    inv = lax.rsqrt(jnp.mean(x * x, axis=-1, keepdims=True) + NORM_EPS)
    normed = x * inv
    gu = a_ref[...] + b_ref[...]
    gn = gu * gain_ref[...]
    prod = gu * normed
    gg_ref[...] += jnp.sum(prod, axis=0, keepdims=True)
    gx = inv * (gn - normed * jnp.mean(gn * normed, axis=-1, keepdims=True))
    out_ref[0] = gx.astype(jnp.bfloat16)


def run_norm_back(h, a, b, gain, dep):
    _, rows, d = h.shape
    q = 128
    row = pl.BlockSpec((q, d), lambda i: (i, 0))
    row3 = pl.BlockSpec((1, q, d), lambda i: (0, i, 0))
    one = pl.BlockSpec((1, d), lambda i: (0, 0))
    return pl.pallas_call(
        norm_back_kernel,
        out_shape=(jax.ShapeDtypeStruct(h.shape, jnp.bfloat16), jax.ShapeDtypeStruct((1, d), jnp.float32)),
        grid=(rows // q,),
        in_specs=[row3, row, row, one, HBM],
        out_specs=(row3, one),
        compiler_params=params("arbitrary"),
        cost_estimate=pl.CostEstimate(flops=8 * rows * d * 1000, bytes_accessed=12 * rows * d, transcendentals=rows),
        name="norm_back",
    )(h, a, b, gain, dep)


def logits_kernel(start_ref, u_ref, w_ref, lab_ref, _, z_ref, stat_ref, m_ref, s_ref, t_ref, *, sub):
    j = pl.program_id(0)
    rows, tile = z_ref.shape
    lanes = 128

    @pl.when(j == 0)
    def _():
        m_ref[...] = jnp.full_like(m_ref, -jnp.inf)
        s_ref[...] = jnp.zeros_like(s_ref)
        t_ref[...] = jnp.zeros_like(t_ref)

    base = start_ref[0] + j * tile
    z_ref[...] = lax.dot_general(u_ref[...], w_ref[...], NN, preferred_element_type=jnp.float32)
    for i in range(rows // sub):
        r = pl.ds(i * sub, sub)
        z = z_ref[r, :]
        lab = lab_ref[r, :] - base
        parts = [z[:, k * lanes:(k + 1) * lanes] for k in range(tile // lanes)]
        m_old = m_ref[r, :]
        m_new = m_old
        for p in parts:
            m_new = jnp.maximum(m_new, p)
        lane = lax.broadcasted_iota(jnp.int32, (sub, lanes), 1)
        off = lab - lane
        total = s_ref[r, :] * jnp.exp(m_old - m_new)
        target = t_ref[r, :]
        for k, p in enumerate(parts):
            total += jnp.exp(p - m_new)
            target = jnp.where(off == k * lanes, p, target)
        m_ref[r, :] = m_new
        s_ref[r, :] = total
        t_ref[r, :] = target

    @pl.when(j == pl.num_programs(0) - 1)
    def _():
        m = m_ref[...]
        top = jnp.max(m, axis=1, keepdims=True)
        stat_ref[0] = top
        stat_ref[1] = jnp.sum(s_ref[...] * jnp.exp(m - top), axis=1, keepdims=True)
        stat_ref[2] = jnp.sum(t_ref[...], axis=1, keepdims=True)


def run_logits(start, u, w, lab, dep, head, rows):
    d, cols = w.shape
    return pl.pallas_call(
        functools.partial(logits_kernel, sub=128),
        out_shape=(jax.ShapeDtypeStruct((rows, cols), jnp.float32), jax.ShapeDtypeStruct((3, rows, 1), jnp.float32)),
        grid_spec=pltpu.PrefetchScalarGridSpec(
            num_scalar_prefetch=1, grid=(cols // TILE,),
            in_specs=[pl.BlockSpec((rows, d), lambda j, s: (head, 0)), pl.BlockSpec((d, TILE), lambda j, s: (0, j)), pl.BlockSpec((rows, 1), lambda j, s: (head, 0)), HBM],
            out_specs=(pl.BlockSpec((rows, TILE), lambda j, s: (0, j)), pl.BlockSpec((3, rows, 1), lambda j, s: (0, 0, 0))),
            scratch_shapes=[pltpu.VMEM((rows, 128), jnp.float32)] * 3),
        compiler_params=params("arbitrary"),
        cost_estimate=pl.CostEstimate(flops=2 * rows * d * cols, bytes_accessed=cols * (2 * d + 4 * rows), transcendentals=rows * cols),
        name="logits",
    )(start, u, w, lab, dep)


def e_tile(z, shift, weight, off):
    parts = []
    for k in range(z.shape[1] // 128):
        p = jnp.exp(z[:, k * 128:(k + 1) * 128] - shift)
        parts.append(jnp.where(off == k * 128, p - weight, p))
    return jnp.concatenate(parts, axis=1).astype(jnp.bfloat16)


def fill_rows(vals_ref, norm_ref, wt_ref, lab_ref, shift_ref, weight_ref, off_ref):
    shape = shift_ref.shape
    wt = wt_ref[...]
    shift_ref[...] = jnp.broadcast_to(norm_ref[...] - jnp.log(wt), shape)
    weight_ref[...] = jnp.broadcast_to(wt, shape)
    off_ref[...] = lab_ref[...] - vals_ref[0] - lax.broadcasted_iota(jnp.int32, shape, 1)


def row_scratch(rows):
    return [pltpu.VMEM((rows, 128), jnp.float32), pltpu.VMEM((rows, 128), jnp.float32), pltpu.VMEM((rows, 128), jnp.int32)]


def du_kernel(start_ref, z_ref, w_ref, norm_ref, wt_ref, lab_ref, _, out_ref, acc_ref, shift_ref, weight_ref, off_ref):
    j = pl.program_id(0)

    @pl.when(j == 0)
    def _():
        acc_ref[...] = jnp.zeros_like(acc_ref)
        fill_rows(start_ref, norm_ref, wt_ref, lab_ref, shift_ref, weight_ref, off_ref)

    e = e_tile(z_ref[...], shift_ref[...], weight_ref[...], off_ref[...] - j * z_ref.shape[1])
    acc_ref[...] += lax.dot_general(e, w_ref[...], NT, preferred_element_type=jnp.float32)

    @pl.when(j == pl.num_programs(0) - 1)
    def _():
        out_ref[...] = acc_ref[...].astype(jnp.bfloat16).astype(jnp.float32)


def run_du(start, z, w, norm, wt, lab, dep, head, rows):
    d, cols = w.shape
    steps = cols // TILE
    vec = pl.BlockSpec((rows, 1), lambda j, s: (head, 0))
    return pl.pallas_call(
        du_kernel,
        out_shape=jax.ShapeDtypeStruct((rows, d), jnp.float32),
        grid_spec=pltpu.PrefetchScalarGridSpec(
            num_scalar_prefetch=1, grid=(steps,),
            in_specs=[pl.BlockSpec((rows, TILE), lambda j, s: (0, j)), pl.BlockSpec((d, TILE), lambda j, s: (0, j)), vec, vec, vec, HBM],
            out_specs=pl.BlockSpec((rows, d), lambda j, s: (0, 0)),
            scratch_shapes=[pltpu.VMEM((rows, d), jnp.float32)] + row_scratch(rows)),
        compiler_params=params("arbitrary"),
        cost_estimate=pl.CostEstimate(flops=2 * rows * d * cols, bytes_accessed=cols * (2 * d + 4 * rows), transcendentals=rows * cols),
        name="du",
    )(start, z, w, norm, wt, lab, dep)


def own_e_kernel(start_ref, z0_ref, z1_ref, u_ref, norm_ref, wt_ref, lab_ref, e_ref, uo_ref, shift_ref, weight_ref, off_ref):
    j = pl.program_id(0)

    @pl.when(j == 0)
    def _():
        fill_rows(start_ref, norm_ref, wt_ref, lab_ref, shift_ref, weight_ref, off_ref)

    uo_ref[...] = u_ref[...]
    rows = z0_ref.shape[0]
    at = (start_ref[1] + j) * NARROW
    for i, z_ref in enumerate((z0_ref, z1_ref)):
        r = slice(i * rows, (i + 1) * rows)
        e_ref[r, :] = e_tile(z_ref[...], shift_ref[r, :], weight_ref[r, :], off_ref[r, :] - at)


def run_own_e(start, z0, z1, u, norm, wt, lab):
    rows, d = u.shape
    steps = BLOCK_COLS // NARROW
    vec = pl.BlockSpec((rows, 1), lambda j, s: (0, 0))
    u_spec = pl.BlockSpec((rows // steps, d), lambda j, s: (j, 0))
    z_spec = pl.BlockSpec((rows // 2, NARROW), lambda j, s: (0, s[1] + j))
    return pl.pallas_call(
        own_e_kernel,
        out_shape=(jax.ShapeDtypeStruct((4 * rows, BLOCK_COLS), jnp.bfloat16), jax.ShapeDtypeStruct((4 * rows, d), jnp.bfloat16)),
        grid_spec=pltpu.PrefetchScalarGridSpec(
            num_scalar_prefetch=1, grid=(steps,),
            in_specs=[z_spec, z_spec, u_spec, vec, vec, vec],
            out_specs=(pl.BlockSpec((rows, NARROW), lambda j, s: (0, j)), u_spec),
            scratch_shapes=row_scratch(rows)),
        compiler_params=params("arbitrary"),
        cost_estimate=pl.CostEstimate(flops=rows * BLOCK_COLS * 2048, bytes_accessed=rows * (6 * BLOCK_COLS + 4 * d), transcendentals=rows * BLOCK_COLS),
        name="own_e",
    )(start, z0, z1, u, norm, wt, lab)


def class_e_kernel(start_ref, *refs):
    n = len(refs) - 12
    pieces, (w0_ref, w1_ref, norm_ref, wt_ref, lab_ref, _, _, e_ref, u_ref, shift_ref, weight_ref, off_ref) = refs[:n], refs[n:]
    j = pl.program_id(0)

    @pl.when(j == 0)
    def _():
        at = 0
        for p in pieces:
            u_ref[at:at + p.shape[0], :] = p[...].astype(jnp.bfloat16)
            at += p.shape[0]
        fill_rows(start_ref, norm_ref, wt_ref, lab_ref, shift_ref, weight_ref, off_ref)

    for i, w_ref in enumerate((w0_ref, w1_ref)):
        z = lax.dot_general(u_ref[...], w_ref[...], NN, preferred_element_type=jnp.float32)
        at = (start_ref[1] + 2 * j + i) * NARROW
        e_ref[:, i * NARROW:(i + 1) * NARROW] = e_tile(z, shift_ref[...], weight_ref[...], off_ref[...] - at)


def run_class_e(start, pieces, w, norm, wt, lab, e_all, u_all, slot):
    d = w.shape[0]
    rows = sum(p.shape[0] for p in pieces)
    full = lambda j, s: (0, 0)
    once = pl.Buffered(1)
    vec = pl.BlockSpec((rows, 1), full)
    n = len(pieces)
    return pl.pallas_call(
        class_e_kernel,
        out_shape=(jax.ShapeDtypeStruct(e_all.shape, e_all.dtype), jax.ShapeDtypeStruct(u_all.shape, u_all.dtype)),
        grid_spec=pltpu.PrefetchScalarGridSpec(
            num_scalar_prefetch=1, grid=(BLOCK_COLS // (2 * NARROW),),
            in_specs=[pl.BlockSpec(p.shape, full, pipeline_mode=once) for p in pieces] + [pl.BlockSpec((d, NARROW), lambda j, s: (0, s[1] + 2 * j)), pl.BlockSpec((d, NARROW), lambda j, s: (0, s[1] + 2 * j + 1)), vec, vec, vec, HBM, HBM],
            out_specs=(pl.BlockSpec((rows, 2 * NARROW), lambda j, s: (slot, j)), pl.BlockSpec((rows, d), lambda j, s: (slot, 0))),
            scratch_shapes=row_scratch(rows)),
        input_output_aliases={1 + n + 5: 0, 1 + n + 6: 1},
        compiler_params=params("arbitrary"),
        cost_estimate=pl.CostEstimate(flops=2 * rows * d * BLOCK_COLS, bytes_accessed=BLOCK_COLS * 2 * (d + rows) + 6 * rows * d, transcendentals=rows * BLOCK_COLS),
        name="class_e",
    )(start, *pieces, w, w, norm, wt, lab, e_all, u_all)


def grad_w_kernel(start_ref, u_ref, e_ref, _, keep_ref, give_ref, ut_ref):
    @pl.when(pl.program_id(0) == 0)
    def _():
        ut_ref[...] = u_ref[...].T

    g = lax.dot_general(ut_ref[...], e_ref[...], NN, preferred_element_type=jnp.float32)
    half = g.shape[0] // 2

    @pl.when(start_ref[0] == 0)
    def _():
        keep_ref[...] = g[:half]
        give_ref[...] = g[half:]

    @pl.when(start_ref[0] == 1)
    def _():
        keep_ref[...] = g[half:]
        give_ref[...] = g[:half]


def run_grad_w(where, u_all, e_all, dep):
    rows, cols = e_all.shape
    blk, tn = 512, 512
    out = pl.BlockSpec((blk // 2, tn), lambda j, s: (0, j))
    return pl.pallas_call(
        grad_w_kernel,
        out_shape=(jax.ShapeDtypeStruct((blk // 2, cols), jnp.float32),) * 2,
        grid_spec=pltpu.PrefetchScalarGridSpec(
            num_scalar_prefetch=1, grid=(cols // tn,),
            in_specs=[pl.BlockSpec((rows, blk), lambda j, s: (0, s[1])), pl.BlockSpec((rows, tn), lambda j, s: (0, j)), HBM],
            out_specs=(out, out),
            scratch_shapes=[pltpu.VMEM((blk, rows), jnp.bfloat16)]),
        compiler_params=params("arbitrary"),
        cost_estimate=pl.CostEstimate(flops=2 * rows * blk * cols, bytes_accessed=2 * rows * (blk + cols) + 4 * blk * cols, transcendentals=0),
        name="grad_w",
    )(where, u_all, e_all, dep)


def place_kernel(at_ref, *refs, n, chunks):
    blocks, out_ref, bufs, in_sem, out_sem = refs[:n], refs[-n - 3], refs[-n - 2:-2], refs[-2], refs[-1]
    _, cols = blocks[0].shape
    width = cols // chunks
    at = at_ref[0] * NARROW

    def load(i, k):
        c = pl.ds(k * width, width)
        return pltpu.make_async_copy(blocks[i].at[:, c], bufs[i].at[:, c], in_sem.at[i, k])

    def store(k):
        to = pl.ds(pl.multiple_of(at + k * width, NARROW), width)
        return pltpu.make_async_copy(bufs[0].at[:, pl.ds(k * width, width)], out_ref.at[:, to], out_sem.at[k])

    for k in range(chunks):
        for i in range(n):
            load(i, k).start()
    for k in range(chunks):
        for i in range(n):
            load(i, k).wait()
        if n == 2:
            c = pl.ds(k * width, width)
            bufs[0][:, c] += bufs[1][:, c]
        store(k).start()
    for k in range(chunks):
        store(k).wait()


def run_place(at, blocks, out, dep, shape):
    rows, cols = blocks[0].shape
    n, chunks = len(blocks), 4
    extra = [dep] if out is None else [out, dep]
    return pl.pallas_call(
        functools.partial(place_kernel, n=n, chunks=chunks),
        out_shape=jax.ShapeDtypeStruct(shape, jnp.float32),
        grid_spec=pltpu.PrefetchScalarGridSpec(
            num_scalar_prefetch=1, grid=(),
            in_specs=[HBM] * (n + len(extra)),
            out_specs=HBM,
            scratch_shapes=[pltpu.VMEM((rows, cols), jnp.float32)] * n + [pltpu.SemaphoreType.DMA((n, chunks)), pltpu.SemaphoreType.DMA((chunks,))]),
        input_output_aliases={} if out is None else {1 + n: 0},
        compiler_params=pltpu.CompilerParams(vmem_limit_bytes=VMEM_LIMIT),
        cost_estimate=pl.CostEstimate(flops=rows * cols * 200, bytes_accessed=8 * rows * cols, transcendentals=0),
        name="place",
    )(at, *blocks, *extra)


def solution(mesh):
    n_dp = mesh.shape['dp']

    def hop(x, bit):
        return lax.ppermute(x, 'dp', [(i, i ^ bit) for i in range(n_dp)])

    def hop_tp(x):
        return lax.ppermute(x, 'tp', [(0, 1), (1, 0)])

    CORE, X, Y = 1, 2, 4

    def local_step(h_main, h_mtp, labels_main, labels_mtp, weight_main, weight_mtp, gain_final, gain_mtp, w_out):
        rows, d_model = h_main.shape[1:]
        shard_vocab = w_out.shape[1]
        q = rows // 4
        tp = lax.axis_index('tp')
        dp = lax.axis_index('dp')
        core = dp % 2
        chip = dp // 2
        vocab_start = tp * shard_vocab
        col_tile = jnp.minimum(chip * BLOCK_COLS, shard_vocab - BLOCK_COLS) // NARROW
        start = jnp.stack([vocab_start, col_tile]).astype(jnp.int32)
        gains = jnp.stack([gain_final, gain_mtp])

        labels = jnp.concatenate([labels_main, labels_mtp])
        weights = jnp.concatenate([weight_main, weight_mtp])
        small_all = lax.all_gather(jnp.stack([labels.astype(jnp.float32), weights]), 'dp')
        weight_sums = jnp.sum(small_all[:, 1], axis=(0, 2))
        loss_coefs = jnp.stack([1.0 / weight_sums[0], MTP_LAMBDA / weight_sums[1]])
        row_w_all = small_all[:, 1] * loss_coefs[None, :, None]
        labels_all = small_all[:, 0].astype(jnp.int32)
        row_w = (weights * loss_coefs[:, None]).reshape(2 * rows)
        labels = labels.reshape(2 * rows, 1)

        u_own, near, c0, c1a, c1b = run_norm(tp.reshape(1).astype(jnp.int32), h_main, h_mtp, gains, small_all)
        nx, ny = hop(near, X), hop(near, Y)
        c0x, c0y = hop(c0, X), hop(c0, Y)
        c1ax, c1ay = hop(c1a, X), hop(c1a, Y)
        c1bx, c1by = hop(c1b, X), hop(c1b, Y)
        nd = hop(ny, X)
        c0d = hop(c0x, Y)
        c1ad = hop(c1ay, X)
        c1bd = hop(c1bx, Y)
        zx, zy, zd = hop_tp(nx), hop_tp(ny), hop_tp(nd)
        pieces = {X: (nx, c0x, c1ax, c1bx, zx), Y: (ny, c0y, c1ay, c1by, zy), X | Y: (nd, c0d, c1ad, c1bd, zd)}

        z0, stats0 = run_logits(start, u_own, w_out, labels, u_own, 0, rows)
        z1, stats1 = run_logits(start, u_own, w_out, labels, stats0, 1, rows)
        stats = jnp.concatenate([stats0, stats1], axis=1).reshape(3, 2 * rows)
        other = hop_tp(stats)
        row_max = jnp.maximum(stats[0], other[0])
        row_sum = stats[1] * jnp.exp(stats[0] - row_max) + other[1] * jnp.exp(other[0] - row_max)
        log_norm = row_max + jnp.log(row_sum)
        loss_part = jnp.sum(row_w * (log_norm - (stats[2] + other[2])))
        norms = {d: hop(log_norm, d) for d in (X, Y, X | Y)}

        norm_col, w_col = log_norm.reshape(2 * rows, 1), row_w.reshape(2 * rows, 1)
        e_cls, u_cls = run_own_e(start, z0, z1, u_own, norm_col, w_col, labels)
        part0 = run_du(start, z0, w_out, norm_col, w_col, labels, stats1, 0, rows)
        other0 = hop_tp(part0)

        def order(v):
            v = v.reshape(2, rows)
            a, b = v[:, :q].reshape(2 * q), v[:, q:2 * q].reshape(2 * q)
            first, last = jnp.where(tp == 0, a, b), jnp.where(tp == 0, b, a)
            return jnp.concatenate([first, v[:, 2 * q:].reshape(2 * rows - 4 * q), last]).reshape(2 * rows, 1)

        dep = e_cls
        for slot, d in enumerate((X, Y, X | Y)):
            pick = lambda v: order(lax.dynamic_index_in_dim(v, dp ^ d, 0, keepdims=False))
            e_cls, u_cls = run_class_e(start, pieces[d], w_out, order(norms[d]), pick(row_w_all), pick(labels_all), e_cls, u_cls, slot + 1)

        blk = d_model // n_dp
        recv = []
        for d in (X | Y, X, Y, 0):
            where = jnp.stack([core, chip ^ (d // 2)]).astype(jnp.int32)
            keep, give = run_grad_w(where, u_cls, e_cls, dep)
            got = hop(give, CORE)
            if d == 0:
                recv.append((keep, got))
                break
            dep = keep + got
            recv.append((hop(dep, d),))
            if d == X:
                part1 = run_du(start, z1, w_out, norm_col, w_col, labels, keep, 1, rows)
                other1 = hop_tp(part1)
        gh0, gg0 = run_norm_back(h_main, part0, other0, gains[:1], keep)
        out, after = None, gg0
        for d, blocks in zip((0, X | Y, X, Y), (recv[3], recv[0], recv[1], recv[2])):
            src = chip ^ (d // 2)
            at = (jnp.minimum(src * BLOCK_COLS, shard_vocab - BLOCK_COLS) // NARROW).reshape(1).astype(jnp.int32)
            out = run_place(at, blocks, out, after, (blk, shard_vocab))
            if d == X:
                gh1, gg1 = run_norm_back(h_mtp, part1, other1, gains[1:], gg0)
                loss_total, grad_gain = lax.psum((loss_part, jnp.concatenate([gg0, gg1])), 'dp')
                after = grad_gain
        return loss_total, gh0, gh1, out, grad_gain[0], grad_gain[1]


    row_spec = P('dp', None)
    return jax.shard_map(local_step, mesh=mesh, in_specs=(P('dp', None, None), P('dp', None, None), row_spec, row_spec, row_spec, row_spec, P(None), P(None), P(None, 'tp')), out_specs=(P(), P('dp', None, None), P('dp', None, None), P('dp', 'tp'), P(None), P(None)), check_vma=False)
```

time: 1080 us -> 841 us (0.78)
  waiting for transfers between devices: 682 us -> 192 us
  Pallas kernels: 0 us -> 435 us
  matrix products: 237 us -> 0 us
  other arithmetic: 81.4 us -> 28.4 us
  blocking collectives: 50.2 us -> 103 us
  local copies, waits for them, and re-layouts: 7.35 us -> 42 us
  starting transfers between devices: 0.3 us -> 27.3 us
  between operations: 17 us -> 2.67 us
    reduce_scatter x1 -> x0, waiting for transfers between devices: 569 us -> none  [local_step(): grad_w = lax.psum_scatter(grad_w, 'dp', scatter_dimension=0, tiled=True)]
    pallas_call x0 -> x19, Pallas kernels: none -> 435 us  [the longest x4 105 us: run_grad_w(): pl.pallas_call(grad_w_kernel, out_shape=(jax.ShapeDtypeStruct((blk // 2,...]
    dot_general x3 -> x0, matrix products: 237 us -> none  [the longest x1 80.3 us: local_step(): lax.dot_general(u_rows, grad_z, (((0,), (0,)), ((), ())), preferred_eleme...]
    ppermute x0 -> x28, waiting for transfers between devices: none -> 192 us  [the longest x22 99.9 us: hop(): return lax.ppermute(x, 'dp', [(i, i ^ bit) for i in range(n_dp)])]
    psum x1 -> x0, waiting for transfers between devices: 113 us -> none  [local_step(): lax.psum(grad_part.astype(jnp.float32), 'tp').reshape(2, rows, d_model)]
    psum x3 -> x1, blocking collectives: 45.3 us -> 91 us  [local_step(): lax.psum((loss_part, jnp.concatenate([gg0, gg1])), 'dp')]
    convert_element_type x3 -> x2, other arithmetic: 42.7 us -> 0.86 us  [the longest x1 0.71 us: local_step(): labels.astype(jnp.float32)]
    reduce_sum x6 -> x1, other arithmetic: 35.9 us -> 0.64 us  [local_step(): loss_part = jnp.sum(row_w * (log_norm - (stats[2] + other[2])))]
  transfers between devices with their start and end apart: 2 -> 28, of which waited for: 2 -> 8; matrix products, arithmetic and copies ran while one was open for 9% -> 7% of each run, Pallas kernels for 0% -> 38%
where the time goes in v1:
time: 841 us; the launch traced here: 831 us
  Pallas kernels  435 us (52%)
  waiting for transfers between devices  192 us (23%)
  blocking collectives  103 us (12%)
  local copies, waits for them, and re-layouts  42 us (5%)
  other arithmetic  28.4 us (3%)
  starting transfers between devices  27.3 us (3%)
    pallas_call x4, Pallas kernels, run_grad_w(): pl.pallas_call(grad_w_kernel, out_shape=(jax.ShapeDtypeStruct((blk // 2,...  105 us
    ppermute x22, waiting for transfers between devices, hop(): return lax.ppermute(x, 'dp', [(i, i ^ bit) for i in range(n_dp)])  99.9 us
    pallas_call x2, Pallas kernels, run_logits(): pl.pallas_call(functools.partial(logits_kernel, sub=128), out_shape=(jax....  97.8 us
    ppermute x6, waiting for transfers between devices, hop_tp(): return lax.ppermute(x, 'tp', [(0, 1), (1, 0)])  92.4 us
    psum x1, blocking collectives, local_step(): lax.psum((loss_part, jnp.concatenate([gg0, gg1])), 'dp')  91 us
    pallas_call x2, Pallas kernels, run_du(): pl.pallas_call(du_kernel, out_shape=jax.ShapeDtypeStruct((rows, d), jnp.f...  89.6 us
    pallas_call x3, Pallas kernels, run_class_e(): pl.pallas_call(class_e_kernel, out_shape=(jax.ShapeDtypeStruct(e_all.shap...  85.3 us
    unnamed x40, local copies, waits for them, and re-layouts  25.1 us
  transfers between devices with their start and end apart: 28, of which 8 were waited for; matrix products, arithmetic and copies ran while one was open for 7% of the time, Pallas kernels for 38%

profile of v1, /device:TPU:0, one launch (start us, length us, event | category | flops | bytes accessed | tf_op | source)
XLA Modules:
  0.0 830.9 jit_solution(5782633385181532708)
XLA Ops:
  2.1 11.9 %all-gather = f32[16,2,512]{2,1,0:T(2,128)} all-gather(f32[2,2,512]{2,1,0:T(2,128)S(1)} %pad_maximum_fusion.2), channel_id=2, replica_groups=mesh['tp'=2,'dp'=8] {'dp'}, dimensions={0}, use_global_device_ids=true | all-gather | bytes 73728 | tf_op jit(solution)/shard_map/all_gather | solution.py:409
  15.3 9.3 %norm.1 = (bf16[1024,2048]{1,0:T(8,128)(2,1)}, f32[256,2048]{1,0:T(8,128)}, f32[256,2048]{1,0:T(8,128)}, f32[128,2048]{1,0:T(8,128)}, f32[128,2048]{1,0:T(8,128)}) custom-call(s32[1]{0:T(128)} %bitcast.6.tp_ref, bf16[1,512,2048]{2,1,0:T(8,128)(2,1)} %h_ref.2, bf16[1,512,2048]{2,1,0:T(8,128)(2,1)} %h_ref.3, f32[2,2048]{1,0:T(2,128)} %pad_maximum_fusion.gain_ref, ...), custom_call_target="tpu_custom_call" | custom-call | flops 8388608000 | bytes 14680064 | tf_op jit(solution)/shard_map/norm/pallas_call | solution.py:64
  30.5 48.6 %logits.2 = (f32[512,16128]{1,0:T(8,128)}, f32[3,512,1]{2,1,0:T(8,128)}) custom-call(s32[2]{0:T(128)} %pad_add_fusion.3.start_ref, bf16[1024,2048]{1,0:T(8,128)(2,1)} %get-tuple-element.35.u_ref._, bf16[2048,16128]{1,0:T(8,128)(2,1)} %w_ref.7, s32[1024,1]{1,0:T(8,128)} %bitcast.170, bf16[1024,2048]{1,0:T(8,128)(2,1)} %get-tuple-element.35.u_ref._), custom_call_target="tpu_custom_call" | custom-call | flops 33822867456 | bytes 99090432 | tf_op jit(solution)/shard_map/logits/pallas_call | solution.py:155
  80.5 49.1 %logits.3 = (f32[512,16128]{1,0:T(8,128)}, f32[3,512,1]{2,1,0:T(8,128)}) custom-call(s32[2]{0:T(128)} %pad_add_fusion.3.start_ref, bf16[1024,2048]{1,0:T(8,128)(2,1)} %get-tuple-element.35.u_ref._, bf16[2048,16128]{1,0:T(8,128)(2,1)} %w_ref.7, s32[1024,1]{1,0:T(8,128)} %bitcast.171, f32[3,512,1]{2,1,0:T(8,128)} %get-tuple-element.36._), custom_call_target="tpu_custom_call" | custom-call | flops 33822867456 | bytes 99090432 | tf_op jit(solution)/shard_map/logits/pallas_call | solution.py:155
  150.7 19.0 %own_e.1 = (bf16[4096,4096]{1,0:T(8,128)(2,1)}, bf16[4096,2048]{1,0:T(8,128)(2,1)}) custom-call(s32[2]{0:T(128)} %pad_add_fusion.3.start_ref, f32[512,16128]{1,0:T(8,128)} %get-tuple-element.38.z_ref.z0_ref, f32[512,16128]{1,0:T(8,128)} %get-tuple-element.43.z1_ref.z_ref, bf16[1024,2048]{1,0:T(8,128)(2,1)} %get-tuple-element.35.u_ref._, ...), custom_call_target="tpu_custom_call" | custom-call | flops 8589934592 | bytes 33554432 | tf_op jit(solution)/shard_map/own_e/pallas_call | solution.py:244
  169.7 22.9 %copy.138.refs_10_ = bf16[4096,4096]{1,0:T(8,128)(2,1)} copy(bf16[4096,4096]{1,0:T(8,128)(2,1)} %get-tuple-element.44._) | data formatting | bytes 67108864
  198.4 21.1 %collective-permute-done.6.refs_2_ = f32[128,2048]{1,0:T(8,128)S(1)} collective-permute-done((f32[128,2048]{1,0:T(8,128)}, f32[128,2048]{1,0:T(8,128)S(1)}, u32[]{:S(2)}, u32[]{:S(2)}) %collective-permute-start.6) | collective-permute-done | bytes 1048608 | tf_op jit(solution)/shard_map/ppermute | solution.py:387
  231.3 28.4 %class_e.3 = (bf16[4096,4096]{1,0:T(8,128)(2,1)}, bf16[4096,2048]{1,0:T(8,128)(2,1)}) custom-call(s32[2]{0:T(128)} %pad_add_fusion.3.start_ref, f32[256,2048]{1,0:T(8,128)} %collective-permute-done.16.refs_0_, f32[256,2048]{1,0:T(8,128)} %copy-done, f32[128,2048]{1,0:T(8,128)} %collective-permute-done.17.refs_2_, ...), custom_call_target="tpu_custom_call", output_to_operand_aliasing={{0}: (11, {}), {1}: (12, {})} | custom-call | flops 17179869184 | bytes 37748736 | tf_op jit(solution)/shard_map/class_e/pallas_call | solution.py:284
  259.7 31.1 %collective-permute-done.13.refs_3_ = f32[128,2048]{1,0:T(8,128)} collective-permute-done((f32[128,2048]{1,0:T(8,128)}, f32[128,2048]{1,0:T(8,128)}, u32[]{:S(2)}, u32[]{:S(2)}) %collective-permute-start.13) | collective-permute-done | bytes 1048608 | tf_op jit(solution)/shard_map/ppermute | solution.py:387
  292.8 28.4 %class_e.4 = (bf16[4096,4096]{1,0:T(8,128)(2,1)}, bf16[4096,2048]{1,0:T(8,128)(2,1)}) custom-call(s32[2]{0:T(128)} %pad_add_fusion.3.start_ref, f32[256,2048]{1,0:T(8,128)} %collective-permute-done.2.refs_0_, f32[256,2048]{1,0:T(8,128)} %collective-permute-done.12.refs_1_, f32[128,2048]{1,0:T(8,128)} %copy-done.1, ...), custom_call_target="tpu_custom_call", output_to_operand_aliasing={{0}: (11, {}), {1}: (12, {})} | custom-call | flops 17179869184 | bytes 37748736 | tf_op jit(solution)/shard_map/class_e/pallas_call | solution.py:284
  321.2 32.5 %collective-permute-done.9.refs_3_ = f32[128,2048]{1,0:T(8,128)} collective-permute-done((f32[128,2048]{1,0:T(8,128)}, f32[128,2048]{1,0:T(8,128)}, u32[]{:S(2)}, u32[]{:S(2)}) %collective-permute-start.9) | collective-permute-done | bytes 1048608 | tf_op jit(solution)/shard_map/ppermute | solution.py:387
  353.7 28.5 %class_e.5 = (bf16[4096,4096]{1,0:T(8,128)(2,1)}, bf16[4096,2048]{1,0:T(8,128)(2,1)}) custom-call(s32[2]{0:T(128)} %pad_add_fusion.3.start_ref, f32[256,2048]{1,0:T(8,128)} %collective-permute-done.3.refs_0_, f32[256,2048]{1,0:T(8,128)} %collective-permute-done.5.refs_1_, ...), custom_call_target="tpu_custom_call", output_to_operand_aliasing={{0}: (11, {}), {1}: (12, {})} | custom-call | flops 17179869184 | bytes 37748736 | tf_op jit(solution)/shard_map/class_e/pallas_call | solution.py:284
  382.2 26.3 %grad_w.4 = (f32[256,4096]{1,0:T(8,128)}, f32[256,4096]{1,0:T(8,128)}) custom-call(s32[2]{0:T(128)} %pad_add_fusion.7.start_ref, bf16[4096,2048]{1,0:T(8,128)(2,1)} %get-tuple-element.50.u_ref, bf16[4096,4096]{1,0:T(8,128)(2,1)} %get-tuple-element.51.e_ref, bf16[4096,4096]{1,0:T(8,128)(2,1)} %get-tuple-element.44._), custom_call_target="tpu_custom_call" | custom-call | flops 17179869184 | bytes 46137344 | tf_op jit(solution)/shard_map/grad_w/pallas_call | solution.py:322
  409.1 6.9 collective-permute-done.20
  416.0 6.1 add.84._
  422.1 26.1 %grad_w.5 = (f32[256,4096]{1,0:T(8,128)}, f32[256,4096]{1,0:T(8,128)}) custom-call(s32[2]{0:T(128)} %pad_add_fusion.6.start_ref, bf16[4096,2048]{1,0:T(8,128)(2,1)} %get-tuple-element.50.u_ref, bf16[4096,4096]{1,0:T(8,128)(2,1)} %get-tuple-element.51.e_ref, f32[256,4096]{1,0:T(8,128)} %add.84._), custom_call_target="tpu_custom_call" | custom-call | flops 17179869184 | bytes 46137344 | tf_op jit(solution)/shard_map/grad_w/pallas_call | solution.py:322
  449.6 6.1 collective-permute-done.21
  455.8 6.1 add.85._
  461.9 26.3 %grad_w.6 = (f32[256,4096]{1,0:T(8,128)}, f32[256,4096]{1,0:T(8,128)}) custom-call(s32[2]{0:T(128)} %pad_add_fusion.5.start_ref, bf16[4096,2048]{1,0:T(8,128)(2,1)} %get-tuple-element.50.u_ref, bf16[4096,4096]{1,0:T(8,128)(2,1)} %get-tuple-element.51.e_ref, f32[256,4096]{1,0:T(8,128)} %add.85._), custom_call_target="tpu_custom_call" | custom-call | flops 17179869184 | bytes 46137344 | tf_op jit(solution)/shard_map/grad_w/pallas_call | solution.py:322
  488.5 44.5 %du.2.a_ref = f32[512,2048]{1,0:T(8,128)} custom-call(s32[2]{0:T(128)} %pad_add_fusion.3.start_ref, f32[512,16128]{1,0:T(8,128)} %get-tuple-element.38.z_ref.z0_ref, bf16[2048,16128]{1,0:T(8,128)(2,1)} %w_ref.7, f32[1024,1]{1,0:T(8,128)} %log_add_fusion.norm_ref, f32[1024,1]{1,0:T(8,128)} %bitcast.176, s32[1024,1]{1,0:T(8,128)} %bitcast.173, ...), custom_call_target="tpu_custom_call" | custom-call | flops 33822867456 | bytes 99090432 | tf_op jit(solution)/shard_map/du/pallas_call | solution.py:209
  534.5 45.0 %du.3.a_ref = f32[512,2048]{1,0:T(8,128)} custom-call(s32[2]{0:T(128)} %pad_add_fusion.3.start_ref, f32[512,16128]{1,0:T(8,128)} %get-tuple-element.43.z1_ref.z_ref, bf16[2048,16128]{1,0:T(8,128)(2,1)} %w_ref.7, f32[1024,1]{1,0:T(8,128)} %log_add_fusion.norm_ref, f32[1024,1]{1,0:T(8,128)} %bitcast.177, s32[1024,1]{1,0:T(8,128)} %bitcast.174, ...), custom_call_target="tpu_custom_call" | custom-call | flops 33822867456 | bytes 99090432 | tf_op jit(solution)/shard_map/du/pallas_call | solution.py:209
  580.1 6.2 add.86._
  586.3 26.1 %grad_w.7 = (f32[256,4096]{1,0:T(8,128)}, f32[256,4096]{1,0:T(8,128)}) custom-call(s32[2]{0:T(128)} %pad_add_fusion.4.start_ref, bf16[4096,2048]{1,0:T(8,128)(2,1)} %get-tuple-element.50.u_ref, bf16[4096,4096]{1,0:T(8,128)(2,1)} %get-tuple-element.51.e_ref, f32[256,4096]{1,0:T(8,128)} %add.86._), custom_call_target="tpu_custom_call" | custom-call | flops 17179869184 | bytes 46137344 | tf_op jit(solution)/shard_map/grad_w/pallas_call | solution.py:322
  615.1 11.7 %collective-permute-done.1.b_ref = f32[512,2048]{1,0:T(8,128)} collective-permute-done((f32[512,2048]{1,0:T(8,128)}, f32[512,2048]{1,0:T(8,128)}, u32[]{:S(2)}, u32[]{:S(2)}) %collective-permute-start.1) | collective-permute-done | bytes 4194336 | tf_op jit(solution)/shard_map/ppermute | solution.py:390
  628.0 7.1 norm_back.2
  635.2 80.7 %collective-permute-done.23.b_ref = f32[512,2048]{1,0:T(8,128)} collective-permute-done((f32[512,2048]{1,0:T(8,128)}, f32[512,2048]{1,0:T(8,128)}, u32[]{:S(2)}, u32[]{:S(2)}) %collective-permute-start.23) | collective-permute-done | bytes 4194336 | tf_op jit(solution)/shard_map/ppermute | solution.py:390
  715.9 7.1 norm_back.3
  723.7 91.0 %all-reduce = (f32[]{:T(128)}, f32[2,2048]{1,0:T(2,128)S(1)}) all-reduce(f32[]{:T(128)} %get-tuple-element.68, f32[2,2048]{1,0:T(2,128)S(1)} %pad_maximum_fusion.1), channel_id=1, replica_groups=mesh['tp'=2,'dp'=8] {'dp'}, use_global_device_ids=true, to_apply=%region_2.3 | all-reduce | flops 4097 | bytes 32776 | tf_op jit(solution)/shard_map/psum | solution.py:477
  815.3 5.4 place.4.refs_1_
  820.7 3.3 place.5.refs_1_
  824.0 3.3 place.6.refs_1_
  827.4 3.3 place.7
  (148 shorter events, 58.6 us)
Async XLA Ops:
  24.7 125.0 %collective-permute-start.16 = (f32[256,2048]{1,0:T(8,128)}, f32[256,2048]{1,0:T(8,128)}, u32[]{:S(2)}, u32[]{:S(2)}) collective-permute-start(f32[256,2048]{1,0:T(8,128)} %get-tuple-element.39), channel_id=1, source_target_pairs={{0,2},{1,3},{2,0},{3,1},{4,6},{5,7},{6,4},{7,5},{8,10},{9,11},{10,... | collective-permute-start | bytes 6291464 | tf_op jit(solution)/shard_map/ppermute | solution.py:387
  26.2 123.9 %collective-permute-start.2 = (f32[256,2048]{1,0:T(8,128)}, f32[256,2048]{1,0:T(8,128)}, u32[]{:S(2)}, u32[]{:S(2)}) collective-permute-start(f32[256,2048]{1,0:T(8,128)} %get-tuple-element.39), channel_id=1, source_target_pairs={{0,4},{1,5},{2,6},{3,7},{4,0},{5,1},{6,2},{7,3},{8,12},{9,13},{10,... | collective-permute-start | bytes 6291464 | tf_op jit(solution)/shard_map/ppermute | solution.py:387
  26.8 171.0 %collective-permute-start.17 = (f32[128,2048]{1,0:T(8,128)}, f32[128,2048]{1,0:T(8,128)}, u32[]{:S(2)}, u32[]{:S(2)}) collective-permute-start(f32[128,2048]{1,0:T(8,128)} %get-tuple-element.41), channel_id=1, source_target_pairs={{0,2},{1,3},{2,0},{3,1},{4,6},{5,7},{6,4},{7,5},{8,10},{9,11},{10,... | collective-permute-start | bytes 3145736 | tf_op jit(solution)/shard_map/ppermute | solution.py:387
  28.2 200.6 %collective-permute-start.4 = (f32[256,2048]{1,0:T(8,128)}, f32[256,2048]{1,0:T(8,128)S(1)}, u32[]{:S(2)}, u32[]{:S(2)}) collective-permute-start(f32[256,2048]{1,0:T(8,128)} %get-tuple-element.40), channel_id=1, source_target_pairs={{0,2},{1,3},{2,0},{3,1},{4,6},{5,7},{6,4},{7,5},{8,10},{9,11},{10,... | collective-permute-start | bytes 6291464 | tf_op jit(solution)/shard_map/ppermute | solution.py:387
  80.5 52.2 %copy-start.2 = (f32[16,2,512]{2,1,0:T(2,128)S(1)}, f32[16,2,512]{2,1,0:T(2,128)}, u32[]{:S(2)}) copy-start(f32[16,2,512]{2,1,0:T(2,128)} %all-gather) | copy-start | bytes 196612
  80.5 54.6 %copy-start.5 = (f32[1,512]{1,0:T(1,128)S(1)}, f32[1,512]{1,0:T(1,128)}, u32[]{:S(2)}) copy-start(f32[1,512]{1,0:T(1,128)} %param.14) | copy-start | bytes 6148
  80.5 54.7 %copy-start.6 = (f32[1,512]{1,0:T(1,128)S(1)}, f32[1,512]{1,0:T(1,128)}, u32[]{:S(2)}) copy-start(f32[1,512]{1,0:T(1,128)} %param.13) | copy-start | bytes 6148
  131.1 9.0 %collective-permute-start = (f32[3,1024]{1,0:T(4,128)S(1)}, f32[3,1024]{1,0:T(4,128)S(1)}, u32[]{:S(2)}, u32[]{:S(2)}) collective-permute-start(f32[3,1024]{1,0:T(4,128)S(1)} %bitcast.196), channel_id=1, source_target_pairs={{0,8},{8,0},{1,9},{9,1},{2,10},{10,2},{3,11},{11,3},{4,12},{12,4},... | collective-permute-start | bytes 36872 | tf_op jit(solution)/shard_map/ppermute | solution.py:390
  140.8 7.4 collective-permute-start.15
  148.2 44.4 %collective-permute-start.11 = (f32[1024]{0:T(1024)S(1)}, f32[1024]{0:T(1024)S(1)}, u32[]{:S(2)}, u32[]{:S(2)}) collective-permute-start(f32[1024]{0:T(1024)S(1)} %log_add_fusion.1), channel_id=1, source_target_pairs={{0,6},{1,7},{2,4},{3,5},{4,2},{5,3},{6,0},{7,1},{8,14},{9,15},{10,... | collective-permute-start | bytes 12296 | tf_op jit(solution)/shard_map/ppermute | solution.py:387
  149.6 79.7 %collective-permute-start.18 = (f32[256,2048]{1,0:T(8,128)}, f32[256,2048]{1,0:T(8,128)}, u32[]{:S(2)}, u32[]{:S(2)}) collective-permute-start(f32[256,2048]{1,0:T(8,128)} %collective-permute-done.16.refs_0_), channel_id=1, source_target_pairs={{0,8},{8,0},{1,9},{9,1},{2,10},{10,2},{3,11},{11,3},{4,12},{12,4},... | collective-permute-start | bytes 6291464 | tf_op jit(solution)/shard_map/ppermute | solution.py:390
  150.1 80.8 %collective-permute-start.3 = (f32[256,2048]{1,0:T(8,128)}, f32[256,2048]{1,0:T(8,128)}, u32[]{:S(2)}, u32[]{:S(2)}) collective-permute-start(f32[256,2048]{1,0:T(8,128)} %collective-permute-done.2.refs_0_), channel_id=1, source_target_pairs={{0,2},{1,3},{2,0},{3,1},{4,6},{5,7},{6,4},{7,5},{8,10},{9,11},{10,... | collective-permute-start | bytes 6291464 | tf_op jit(solution)/shard_map/ppermute | solution.py:387
  192.6 3.6 collective-permute-start.19
  196.3 23.2 %collective-permute-start.6 = (f32[128,2048]{1,0:T(8,128)}, f32[128,2048]{1,0:T(8,128)S(1)}, u32[]{:S(2)}, u32[]{:S(2)}) collective-permute-start(f32[128,2048]{1,0:T(8,128)} %get-tuple-element.41), channel_id=1, source_target_pairs={{0,4},{1,5},{2,6},{3,7},{4,0},{5,1},{6,2},{7,3},{8,12},{9,13},{10,... | collective-permute-start | bytes 3145736 | tf_op jit(solution)/shard_map/ppermute | solution.py:387
  197.8 23.2 %collective-permute-start.8 = (f32[128,2048]{1,0:T(8,128)}, f32[128,2048]{1,0:T(8,128)}, u32[]{:S(2)}, u32[]{:S(2)}) collective-permute-start(f32[128,2048]{1,0:T(8,128)} %get-tuple-element.42), channel_id=1, source_target_pairs={{0,2},{1,3},{2,0},{3,1},{4,6},{5,7},{6,4},{7,5},{8,10},{9,11},{10,... | collective-permute-start | bytes 3145736 | tf_op jit(solution)/shard_map/ppermute | solution.py:387
  219.5 72.8 %copy-start.1 = (f32[128,2048]{1,0:T(8,128)}, f32[128,2048]{1,0:T(8,128)S(1)}, u32[]{:S(2)}) copy-start(f32[128,2048]{1,0:T(8,128)S(1)} %collective-permute-done.6.refs_2_) | copy-start | bytes 3145732
  219.5 72.8 %collective-permute-start.12 = (f32[256,2048]{1,0:T(8,128)}, f32[256,2048]{1,0:T(8,128)}, u32[]{:S(2)}, u32[]{:S(2)}) collective-permute-start(f32[256,2048]{1,0:T(8,128)} %get-tuple-element.40), channel_id=1, source_target_pairs={{0,4},{1,5},{2,6},{3,7},{4,0},{5,1},{6,2},{7,3},{8,12},{9,13},{10,... | collective-permute-start | bytes 6291464 | tf_op jit(solution)/shard_map/ppermute | solution.py:387
  221.0 71.8 %collective-permute-start.14 = (f32[256,2048]{1,0:T(8,128)}, f32[256,2048]{1,0:T(8,128)}, u32[]{:S(2)}, u32[]{:S(2)}) collective-permute-start(f32[256,2048]{1,0:T(8,128)} %collective-permute-done.2.refs_0_), channel_id=1, source_target_pairs={{0,8},{8,0},{1,9},{9,1},{2,10},{10,2},{3,11},{11,3},{4,12},{12,4},... | collective-permute-start | bytes 6291464 | tf_op jit(solution)/shard_map/ppermute | solution.py:390
  228.8 62.0 %collective-permute-start.13 = (f32[128,2048]{1,0:T(8,128)}, f32[128,2048]{1,0:T(8,128)}, u32[]{:S(2)}, u32[]{:S(2)}) collective-permute-start(f32[128,2048]{1,0:T(8,128)} %get-tuple-element.42), channel_id=1, source_target_pairs={{0,4},{1,5},{2,6},{3,7},{4,0},{5,1},{6,2},{7,3},{8,12},{9,13},{10,... | collective-permute-start | bytes 3145736 | tf_op jit(solution)/shard_map/ppermute | solution.py:387
  229.4 124.3 %collective-permute-start.5 = (f32[256,2048]{1,0:T(8,128)S(1)}, f32[256,2048]{1,0:T(8,128)}, u32[]{:S(2)}, u32[]{:S(2)}) collective-permute-start(f32[256,2048]{1,0:T(8,128)S(1)} %collective-permute-done.4.refs_1_), channel_id=1, source_target_pairs={{0,4},{1,5},{2,6},{3,7},{4,0},{5,1},{6,2},{7,3},{8,12},{9,13},{10,... | collective-permute-start | bytes 6291464 | tf_op jit(solution)/shard_map/ppermute | solution.py:387
  230.9 122.8 %collective-permute-start.10 = (f32[256,2048]{1,0:T(8,128)}, f32[256,2048]{1,0:T(8,128)}, u32[]{:S(2)}, u32[]{:S(2)}) collective-permute-start(f32[256,2048]{1,0:T(8,128)} %collective-permute-done.3.refs_0_), channel_id=1, source_target_pairs={{0,8},{8,0},{1,9},{9,1},{2,10},{10,2},{3,11},{11,3},{4,12},{12,4},... | collective-permute-start | bytes 6291464 | tf_op jit(solution)/shard_map/ppermute | solution.py:390
  290.8 62.9 %collective-permute-start.9 = (f32[128,2048]{1,0:T(8,128)}, f32[128,2048]{1,0:T(8,128)}, u32[]{:S(2)}, u32[]{:S(2)}) collective-permute-start(f32[128,2048]{1,0:T(8,128)} %collective-permute-done.8.refs_3_), channel_id=1, source_target_pairs={{0,4},{1,5},{2,6},{3,7},{4,0},{5,1},{6,2},{7,3},{8,12},{9,13},{10,... | collective-permute-start | bytes 3145736 | tf_op jit(solution)/shard_map/ppermute | solution.py:387
  292.3 29.0 %collective-permute-start.7 = (f32[128,2048]{1,0:T(8,128)S(1)}, f32[128,2048]{1,0:T(8,128)}, u32[]{:S(2)}, u32[]{:S(2)}) collective-permute-start(f32[128,2048]{1,0:T(8,128)S(1)} %collective-permute-done.6.refs_2_), channel_id=1, source_target_pairs={{0,2},{1,3},{2,0},{3,1},{4,6},{5,7},{6,4},{7,5},{8,10},{9,11},{10,... | collective-permute-start | bytes 3145736 | tf_op jit(solution)/shard_map/ppermute | solution.py:387
  408.5 7.5 collective-permute-start.20
  448.3 7.5 collective-permute-start.21
  488.1 91.9 %collective-permute-start.22 = (f32[256,4096]{1,0:T(8,128)}, f32[256,4096]{1,0:T(8,128)}, u32[]{:S(2)}, u32[]{:S(2)}) collective-permute-start(f32[256,4096]{1,0:T(8,128)} %get-tuple-element.57), channel_id=1, source_target_pairs={{0,1},{1,0},{2,3},{3,2},{4,5},{5,4},{6,7},{7,6},{8,9},{9,8},{10,11... | collective-permute-start | bytes 12582920 | tf_op jit(solution)/shard_map/ppermute | solution.py:387
  533.0 93.8 %collective-permute-start.1 = (f32[512,2048]{1,0:T(8,128)}, f32[512,2048]{1,0:T(8,128)}, u32[]{:S(2)}, u32[]{:S(2)}) collective-permute-start(f32[512,2048]{1,0:T(8,128)} %du.2.a_ref), channel_id=1, source_target_pairs={{0,8},{8,0},{1,9},{9,1},{2,10},{10,2},{3,11},{11,3},{4,12},{12,4},... | collective-permute-start | bytes 12582920 | tf_op jit(solution)/shard_map/ppermute | solution.py:390
  579.6 136.3 %collective-permute-start.23 = (f32[512,2048]{1,0:T(8,128)}, f32[512,2048]{1,0:T(8,128)}, u32[]{:S(2)}, u32[]{:S(2)}) collective-permute-start(f32[512,2048]{1,0:T(8,128)} %du.3.a_ref), channel_id=1, source_target_pairs={{0,8},{8,0},{1,9},{9,1},{2,10},{10,2},{3,11},{11,3},{4,12},{12,4},... | collective-permute-start | bytes 12582920 | tf_op jit(solution)/shard_map/ppermute | solution.py:390
  612.4 203.0 %collective-permute-start.27 = (f32[256,4096]{1,0:T(8,128)}, f32[256,4096]{1,0:T(8,128)}, u32[]{:S(2)}, u32[]{:S(2)}) collective-permute-start(f32[256,4096]{1,0:T(8,128)} %get-tuple-element.62), channel_id=1, source_target_pairs={{0,1},{1,0},{2,3},{3,2},{4,5},{5,4},{6,7},{7,6},{8,9},{9,8},{10,11... | collective-permute-start | bytes 12582920 | tf_op jit(solution)/shard_map/ppermute | solution.py:387
  612.4 208.3 %collective-permute-start.26 = (f32[256,4096]{1,0:T(8,128)}, f32[256,4096]{1,0:T(8,128)}, u32[]{:S(2)}, u32[]{:S(2)}) collective-permute-start(f32[256,4096]{1,0:T(8,128)} %add.84._), channel_id=1, source_target_pairs={{0,6},{1,7},{2,4},{3,5},{4,2},{5,3},{6,0},{7,1},{8,14},{9,15},{10,... | collective-permute-start | bytes 12582920 | tf_op jit(solution)/shard_map/ppermute | solution.py:387
  613.7 210.3 %collective-permute-start.25 = (f32[256,4096]{1,0:T(8,128)}, f32[256,4096]{1,0:T(8,128)}, u32[]{:S(2)}, u32[]{:S(2)}) collective-permute-start(f32[256,4096]{1,0:T(8,128)} %add.85._), channel_id=1, source_target_pairs={{0,2},{1,3},{2,0},{3,1},{4,6},{5,7},{6,4},{7,5},{8,10},{9,11},{10,... | collective-permute-start | bytes 12582920 | tf_op jit(solution)/shard_map/ppermute | solution.py:387
  626.8 200.6 %collective-permute-start.24 = (f32[256,4096]{1,0:T(8,128)}, f32[256,4096]{1,0:T(8,128)}, u32[]{:S(2)}, u32[]{:S(2)}) collective-permute-start(f32[256,4096]{1,0:T(8,128)} %add.86._), channel_id=1, source_target_pairs={{0,4},{1,5},{2,6},{3,7},{4,0},{5,1},{6,2},{7,3},{8,12},{9,13},{10,... | collective-permute-start | bytes 12582920 | tf_op jit(solution)/shard_map/ppermute | solution.py:387
  (5 other events, 42.5 us)

commit v2 on v1

v2 whole, which is shorter than its diff:
```python
import functools

import jax
import jax.numpy as jnp
from jax import lax
from jax.experimental import pallas as pl
from jax.experimental.pallas import tpu as pltpu
from jax.sharding import PartitionSpec as P


NORM_EPS = 1e-6
MTP_LAMBDA = 0.3
BLOCK_COLS = 4096
TILE = 2304
L_TILE = 768
NARROW = 256
VMEM_LIMIT = 60 * 1024 * 1024
CHAIN = ("60", "61", "20", "40", "21", "41", "00")
DU1_AFTER = "20"
NN = (((1,), (0,)), ((), ()))
NT = (((1,), (1,)), ((), ()))


def params(*semantics):
    return pltpu.CompilerParams(dimension_semantics=semantics, vmem_limit_bytes=VMEM_LIMIT)


HBM = pl.BlockSpec(memory_space=pl.ANY)


def norm_kernel(tp_ref, h0_ref, h1_ref, gain_ref, u_ref, near_ref, third_ref, *last_refs):
    head, b = pl.program_id(0), pl.program_id(1)

    def rows_of(h_ref):
        x = h_ref[0].astype(jnp.float32)
        return x * lax.rsqrt(jnp.mean(x * x, axis=-1, keepdims=True) + NORM_EPS)

    for i, h_ref in enumerate((h0_ref, h1_ref)):
        @pl.when(head == i)
        def _():
            u = rows_of(h_ref) * gain_ref[i:i + 1, :]
            u_ref[...] = u.astype(jnp.bfloat16)

            @pl.when(b == tp_ref[0])
            def _():
                near_ref[...] = u

            @pl.when(b == 2)
            def _():
                third_ref[...] = u

            @pl.when(b == 3)
            def _():
                last_refs[i][...] = u


def run_norm(tp, h0, h1, gains):
    _, rows, d = h0.shape
    q = rows // 4
    f32 = jnp.float32
    blk = lambda f: pl.BlockSpec((q, d), f)
    return pl.pallas_call(
        norm_kernel,
        out_shape=(jax.ShapeDtypeStruct((8 * rows, d), jnp.bfloat16), jax.ShapeDtypeStruct((2 * q, d), f32), jax.ShapeDtypeStruct((2 * q, d), f32), jax.ShapeDtypeStruct((q, d), f32), jax.ShapeDtypeStruct((q, d), f32)),
        grid_spec=pltpu.PrefetchScalarGridSpec(
            num_scalar_prefetch=1, grid=(2, 4),
            in_specs=[pl.BlockSpec((1, q, d), lambda h, b, s: (0, jnp.where(h == 0, b, 3), 0)), pl.BlockSpec((1, q, d), lambda h, b, s: (0, jnp.where(h == 0, 0, b), 0)), pl.BlockSpec((2, d), lambda h, b, s: (0, 0))],
            out_specs=(blk(lambda h, b, s: (4 * h + b, 0)), blk(lambda h, b, s: (h, 0)), blk(lambda h, b, s: (h, 0)), blk(lambda h, b, s: (0, 0)), blk(lambda h, b, s: (0, 0)))),
        compiler_params=params("arbitrary", "arbitrary"),
        cost_estimate=pl.CostEstimate(flops=8 * rows * d * 1000, bytes_accessed=14 * rows * d, transcendentals=rows),
        name="norm",
    )(tp, h0, h1, gains)


def norm_back_kernel(h_ref, a_ref, b_ref, gain_ref, _, out_ref, gg_ref):
    @pl.when(pl.program_id(0) == 0)
    def _():
        gg_ref[...] = jnp.zeros_like(gg_ref)

    x = h_ref[0].astype(jnp.float32)
    inv = lax.rsqrt(jnp.mean(x * x, axis=-1, keepdims=True) + NORM_EPS)
    normed = x * inv
    gu = a_ref[...] + b_ref[...]
    gn = gu * gain_ref[...]
    prod = gu * normed
    gg_ref[...] += jnp.sum(prod, axis=0, keepdims=True)
    gx = inv * (gn - normed * jnp.mean(gn * normed, axis=-1, keepdims=True))
    out_ref[0] = gx.astype(jnp.bfloat16)


def run_norm_back(h, a, b, gain, dep):
    _, rows, d = h.shape
    q = 128
    row = pl.BlockSpec((q, d), lambda i: (i, 0))
    row3 = pl.BlockSpec((1, q, d), lambda i: (0, i, 0))
    one = pl.BlockSpec((1, d), lambda i: (0, 0))
    return pl.pallas_call(
        norm_back_kernel,
        out_shape=(jax.ShapeDtypeStruct(h.shape, jnp.bfloat16), jax.ShapeDtypeStruct((1, d), jnp.float32)),
        grid=(rows // q,),
        in_specs=[row3, row, row, one, HBM],
        out_specs=(row3, one),
        compiler_params=params("arbitrary"),
        cost_estimate=pl.CostEstimate(flops=8 * rows * d * 1000, bytes_accessed=12 * rows * d, transcendentals=rows),
        name="norm_back",
    )(h, a, b, gain, dep)


def logits_kernel(start_ref, u_ref, w_ref, lab_ref, z_ref, stat_ref, m_ref, s_ref, t_ref, off_ref, *, sub):
    j = pl.program_id(0)
    rows, tile = z_ref.shape
    lanes = 128

    @pl.when(j == 0)
    def _():
        m_ref[...] = jnp.full_like(m_ref, -jnp.inf)
        s_ref[...] = jnp.zeros_like(s_ref)
        t_ref[...] = jnp.zeros_like(t_ref)
        off_ref[...] = label_offset(lab_ref[...], start_ref[0])

    base = j * tile
    z_ref[...] = lax.dot_general(u_ref[...], w_ref[...], NN, preferred_element_type=jnp.float32)
    for i in range(rows // sub):
        r = pl.ds(i * sub, sub)
        z = z_ref[r, :]
        parts = [z[:, k * lanes:(k + 1) * lanes] for k in range(tile // lanes)]
        m_old = m_ref[r, :]
        m_new = m_old
        for p in parts:
            m_new = jnp.maximum(m_new, p)
        off = off_ref[r, :] - base
        total = s_ref[r, :] * jnp.exp(m_old - m_new)
        target = t_ref[r, :]
        for k, p in enumerate(parts):
            total += jnp.exp(p - m_new)
            target = jnp.where(off == k * lanes, p, target)
        m_ref[r, :] = m_new
        s_ref[r, :] = total
        t_ref[r, :] = target

    @pl.when(j == pl.num_programs(0) - 1)
    def _():
        for i in range(0, rows, 128):
            r = pl.ds(i, 128)
            m = m_ref[r, :].T
            top = jnp.max(m, axis=0, keepdims=True)
            stat_ref[0:1, r] = top
            stat_ref[1:2, r] = jnp.sum(s_ref[r, :].T * jnp.exp(m - top), axis=0, keepdims=True)
            stat_ref[2:3, r] = jnp.sum(t_ref[r, :].T, axis=0, keepdims=True)


def run_logits(start, u, w, lab, rows):
    d, cols = w.shape
    full = lambda j, s: (0, 0)
    return pl.pallas_call(
        functools.partial(logits_kernel, sub=128),
        out_shape=(jax.ShapeDtypeStruct((rows, cols), jnp.float32), jax.ShapeDtypeStruct((3, rows), jnp.float32)),
        grid_spec=pltpu.PrefetchScalarGridSpec(
            num_scalar_prefetch=1, grid=(cols // L_TILE,),
            in_specs=[pl.BlockSpec((rows, d), full), pl.BlockSpec((d, L_TILE), lambda j, s: (0, j)), pl.BlockSpec((1, rows), full)],
            out_specs=(pl.BlockSpec((rows, L_TILE), lambda j, s: (0, j)), pl.BlockSpec((3, rows), full)),
            scratch_shapes=[pltpu.VMEM((rows, 128), jnp.float32)] * 3 + [pltpu.VMEM((rows, 128), jnp.int32)]),
        compiler_params=params("arbitrary"),
        cost_estimate=pl.CostEstimate(flops=2 * rows * d * cols, bytes_accessed=cols * (2 * d + 4 * rows), transcendentals=rows * cols),
        name="logits",
    )(start, u, w, lab)


def e_tile(z, shift, weight, off):
    parts = []
    for k in range(z.shape[1] // 128):
        p = jnp.exp(z[:, k * 128:(k + 1) * 128] - shift)
        parts.append(jnp.where(off == k * 128, p - weight, p))
    return jnp.concatenate(parts, axis=1).astype(jnp.bfloat16)


def spread(row):
    parts = [jnp.broadcast_to(row[:, i:i + 128], (128, 128)).T for i in range(0, row.shape[1], 128)]
    return jnp.concatenate(parts, axis=0)


def label_offset(row, vocab_start):
    lab = spread(row).astype(jnp.int32)
    return lab - vocab_start - lax.broadcasted_iota(jnp.int32, lab.shape, 1)


def fill_rows(start_ref, info_ref, shift_ref, weight_ref, off_ref):
    shift_ref[...] = spread(info_ref[0:1, :] - jnp.log(info_ref[1:2, :]))
    weight_ref[...] = spread(info_ref[1:2, :])
    off_ref[...] = label_offset(info_ref[2:3, :], start_ref[0])


def row_scratch(rows):
    return [pltpu.VMEM((rows, 128), jnp.float32), pltpu.VMEM((rows, 128), jnp.float32), pltpu.VMEM((rows, 128), jnp.int32)]


def du_kernel(start_ref, z_ref, w_ref, info_ref, _, out_ref, acc_ref, shift_ref, weight_ref, off_ref):
    j = pl.program_id(0)

    @pl.when(j == 0)
    def _():
        acc_ref[...] = jnp.zeros_like(acc_ref)
        fill_rows(start_ref, info_ref, shift_ref, weight_ref, off_ref)

    e = e_tile(z_ref[...], shift_ref[...], weight_ref[...], off_ref[...] - j * z_ref.shape[1])
    acc_ref[...] += lax.dot_general(e, w_ref[...], NT, preferred_element_type=jnp.float32)

    @pl.when(j == pl.num_programs(0) - 1)
    def _():
        out_ref[...] = acc_ref[...].astype(jnp.bfloat16).astype(jnp.float32)


def run_du(start, z, w, info, dep, head, rows):
    d, cols = w.shape
    steps = cols // TILE
    vec = pl.BlockSpec((info.shape[0], rows), lambda j, s: (0, head))
    return pl.pallas_call(
        du_kernel,
        out_shape=jax.ShapeDtypeStruct((rows, d), jnp.float32),
        grid_spec=pltpu.PrefetchScalarGridSpec(
            num_scalar_prefetch=1, grid=(steps,),
            in_specs=[pl.BlockSpec((rows, TILE), lambda j, s: (head, j)), pl.BlockSpec((d, TILE), lambda j, s: (0, j)), vec, HBM],
            out_specs=pl.BlockSpec((rows, d), lambda j, s: (0, 0)),
            scratch_shapes=[pltpu.VMEM((rows, d), jnp.float32)] + row_scratch(rows)),
        compiler_params=params("arbitrary"),
        cost_estimate=pl.CostEstimate(flops=2 * rows * d * cols, bytes_accessed=cols * (2 * d + 4 * rows), transcendentals=rows * cols),
        name="du",
    )(start, z, w, info, dep)


def own_e_kernel(start_ref, z0_ref, z1_ref, info_ref, _, e_ref, shift_ref, weight_ref, off_ref):
    j = pl.program_id(0)

    @pl.when(j == 0)
    def _():
        fill_rows(start_ref, info_ref, shift_ref, weight_ref, off_ref)

    for k, z_ref in enumerate((z0_ref, z1_ref)):
        at = (start_ref[1] + 2 * j + k) * NARROW
        e_ref[:, k * NARROW:(k + 1) * NARROW] = e_tile(z_ref[...], shift_ref[...], weight_ref[...], off_ref[...] - at)


def run_own_e(start, z, info, dep):
    rows = info.shape[1]
    vec = pl.BlockSpec(info.shape, lambda j, s: (0, 0))
    z_even = pl.BlockSpec((rows, NARROW), lambda j, s: (0, s[1] + 2 * j))
    z_odd = pl.BlockSpec((rows, NARROW), lambda j, s: (0, s[1] + 2 * j + 1))
    return pl.pallas_call(
        own_e_kernel,
        out_shape=jax.ShapeDtypeStruct((4 * rows, BLOCK_COLS), jnp.bfloat16),
        grid_spec=pltpu.PrefetchScalarGridSpec(
            num_scalar_prefetch=1, grid=(BLOCK_COLS // (2 * NARROW),),
            in_specs=[z_even, z_odd, vec, HBM],
            out_specs=pl.BlockSpec((rows, 2 * NARROW), lambda j, s: (0, j)),
            scratch_shapes=row_scratch(rows)),
        compiler_params=params("arbitrary"),
        cost_estimate=pl.CostEstimate(flops=rows * BLOCK_COLS * 2048, bytes_accessed=rows * 6 * BLOCK_COLS, transcendentals=rows * BLOCK_COLS),
        name="own_e",
    )(start, z, z, info, dep)


def class_e_kernel(start_ref, *refs, quarter, slot):
    n = len(refs) - 11
    pieces, (w_ref, info_ref, _, _, _, e_ref, u_ref, token_ref, shift_ref, weight_ref, off_ref) = refs[:n], refs[n:]
    j = pl.program_id(0)
    rows = e_ref.shape[0]

    @pl.when(j == 0)
    def _():
        at = 0
        for p in pieces:
            u_ref[at:at + p.shape[0], :] = p[...].astype(jnp.bfloat16)
            at += p.shape[0]
        fill_rows(start_ref, info_ref, shift_ref, weight_ref, off_ref)
        token_ref[...] = jnp.zeros_like(token_ref)

    used = start_ref[1 + slot]
    at = (start_ref[1] + 2 * j) * NARROW
    for count in (2, 3, 4):
        @pl.when(used == count)
        def _():
            r = slice(0, count * quarter)
            z = lax.dot_general(u_ref[r, :], w_ref[...], NN, preferred_element_type=jnp.float32)
            e_ref[r, :] = e_tile(z, shift_ref[r, :], weight_ref[r, :], off_ref[r, :] - at)
            if count < 4:
                e_ref[count * quarter:, :] = jnp.zeros((rows - count * quarter, e_ref.shape[1]), e_ref.dtype)


def run_class_e(start, pieces, w, info, e_all, u_all, dep, slot):
    d = w.shape[0]
    rows = sum(p.shape[0] for p in pieces)
    full = lambda j, s: (0, 0)
    once = pl.Buffered(1)
    n = len(pieces)
    return pl.pallas_call(
        functools.partial(class_e_kernel, quarter=rows // 4, slot=slot),
        out_shape=(jax.ShapeDtypeStruct(e_all.shape, e_all.dtype), jax.ShapeDtypeStruct(u_all.shape, u_all.dtype), jax.ShapeDtypeStruct((8, 128), jnp.float32)),
        grid_spec=pltpu.PrefetchScalarGridSpec(
            num_scalar_prefetch=1, grid=(BLOCK_COLS // (2 * NARROW),),
            in_specs=[pl.BlockSpec(p.shape, full, pipeline_mode=once) for p in pieces] + [pl.BlockSpec((pl.Element(d), pl.Element(2 * NARROW)), lambda j, s: (0, pl.multiple_of((s[1] + 2 * j) * NARROW, NARROW))), pl.BlockSpec(info.shape, full), HBM, HBM, HBM],
            out_specs=(pl.BlockSpec((rows, 2 * NARROW), lambda j, s: (slot, j)), pl.BlockSpec((rows, d), lambda j, s: (slot, 0)), pl.BlockSpec((8, 128), full)),
            scratch_shapes=row_scratch(rows)),
        input_output_aliases={1 + n + 2: 0, 1 + n + 3: 1},
        compiler_params=params("arbitrary"),
        cost_estimate=pl.CostEstimate(flops=2 * rows * d * BLOCK_COLS, bytes_accessed=BLOCK_COLS * 2 * (d + rows) + 6 * rows * d, transcendentals=rows * BLOCK_COLS),
        name="class_e",
    )(start, *pieces, w, info, e_all, u_all, dep)


def grad_w_kernel(start_ref, u_ref, e_ref, _, *refs):
    *before, ut_ref = refs
    if len(before) == 5:
        mine_ref, got_ref, keep_ref, give_ref, total_ref = before
        total_ref[...] = mine_ref[...] + got_ref[...]
    else:
        keep_ref, give_ref = before

    @pl.when(pl.program_id(0) == 0)
    def _():
        ut_ref[...] = u_ref[...].T

    g = lax.dot_general(ut_ref[...], e_ref[...], NN, preferred_element_type=jnp.float32)
    half = g.shape[0] // 2

    @pl.when(start_ref[0] == 0)
    def _():
        keep_ref[...] = g[:half]
        give_ref[...] = g[half:]

    @pl.when(start_ref[0] == 1)
    def _():
        keep_ref[...] = g[half:]
        give_ref[...] = g[:half]


def run_grad_w(where, u_all, e_all, dep, part, parts, previous=()):
    rows, cols = e_all.shape
    cols //= parts
    blk, tn = 512, 512
    first = part * (cols // tn)
    out = pl.BlockSpec((blk // 2, tn), lambda j, s: (0, j))
    n_out = 3 if previous else 2
    return pl.pallas_call(
        grad_w_kernel,
        out_shape=(jax.ShapeDtypeStruct((blk // 2, cols), jnp.float32),) * n_out,
        grid_spec=pltpu.PrefetchScalarGridSpec(
            num_scalar_prefetch=1, grid=(cols // tn,),
            in_specs=[pl.BlockSpec((rows, blk), lambda j, s: (0, s[1])), pl.BlockSpec((rows, tn), lambda j, s: (0, first + j)), HBM] + [out] * len(previous),
            out_specs=(out,) * n_out,
            scratch_shapes=[pltpu.VMEM((blk, rows), jnp.bfloat16)]),
        compiler_params=params("arbitrary"),
        cost_estimate=pl.CostEstimate(flops=2 * rows * blk * cols, bytes_accessed=2 * rows * (blk + cols) + 4 * blk * cols, transcendentals=0),
        name="grad_w",
    )(where, u_all, e_all, dep, *previous)


def place_kernel(at_ref, *refs, sizes, chunks):
    n = sum(sizes)
    blocks, (out_ref, *bufs, in_sem, out_sem) = refs[:n], refs[len(refs) - n - 3:]

    def load(i, k):
        width = blocks[i].shape[1] // chunks
        c = pl.ds(k * width, width)
        return pltpu.make_async_copy(blocks[i].at[:, c], bufs[i].at[:, c], in_sem.at[i, k])

    def store(g, i, k):
        width = blocks[i].shape[1] // chunks
        to = pl.ds(pl.multiple_of(at_ref[g] * NARROW + k * width, NARROW), width)
        return pltpu.make_async_copy(bufs[i].at[:, pl.ds(k * width, width)], out_ref.at[:, to], out_sem.at[i, k])

    for i in range(n):
        for k in range(chunks):
            load(i, k).start()
    i = 0
    for g, size in enumerate(sizes):
        for k in range(chunks):
            for m in range(size):
                load(i + m, k).wait()
            if size == 2:
                width = blocks[i].shape[1] // chunks
                c = slice(k * width, (k + 1) * width)
                bufs[i][:, c] += bufs[i + 1][:, c]
            store(g, i, k).start()
        i += size
    i = 0
    for g, size in enumerate(sizes):
        for k in range(chunks):
            store(g, i, k).wait()
        i += size


def run_place(at, groups, out, dep, shape):
    blocks = [b for g in groups for b in g]
    n, chunks = len(blocks), 2
    extra = [dep] if out is None else [out, dep]
    words = sum(b.size for b in blocks)
    return pl.pallas_call(
        functools.partial(place_kernel, sizes=tuple(len(g) for g in groups), chunks=chunks),
        out_shape=jax.ShapeDtypeStruct(shape, jnp.float32),
        grid_spec=pltpu.PrefetchScalarGridSpec(
            num_scalar_prefetch=1, grid=(),
            in_specs=[HBM] * (n + len(extra)),
            out_specs=HBM,
            scratch_shapes=[pltpu.VMEM(b.shape, jnp.float32) for b in blocks] + [pltpu.SemaphoreType.DMA((n, chunks)), pltpu.SemaphoreType.DMA((n, chunks))]),
        input_output_aliases={} if out is None else {1 + n: 0},
        compiler_params=pltpu.CompilerParams(vmem_limit_bytes=VMEM_LIMIT),
        cost_estimate=pl.CostEstimate(flops=words * 200, bytes_accessed=8 * words, transcendentals=0),
        name="place",
    )(at, *blocks, *extra)


def solution(mesh):
    n_dp = mesh.shape['dp']

    def hop(x, bit):
        return lax.ppermute(x, 'dp', [(i, i ^ bit) for i in range(n_dp)])

    def hop_tp(x):
        return lax.ppermute(x, 'tp', [(0, 1), (1, 0)])

    CORE, X, Y = 1, 2, 4

    def local_step(h_main, h_mtp, labels_main, labels_mtp, weight_main, weight_mtp, gain_final, gain_mtp, w_out):
        rows, d_model = h_main.shape[1:]
        shard_vocab = w_out.shape[1]
        q = rows // 4
        tp = lax.axis_index('tp')
        dp = lax.axis_index('dp')
        core = dp % 2
        chip = dp // 2
        vocab_start = tp * shard_vocab
        col_tile = jnp.minimum(chip * BLOCK_COLS, shard_vocab - BLOCK_COLS) // NARROW
        start = jnp.stack([vocab_start, col_tile]).astype(jnp.int32)
        gains = jnp.stack([gain_final, gain_mtp])

        labels = jnp.concatenate([labels_main, labels_mtp])
        weights = jnp.concatenate([weight_main, weight_mtp])
        weight_sums = jnp.sum(weights, axis=1)
        weight_sums = weight_sums + hop(weight_sums, CORE)
        weight_sums = weight_sums + hop(weight_sums, X) + hop(weight_sums, Y) + hop(weight_sums, X | Y)
        loss_coefs = jnp.stack([1.0 / weight_sums[0], MTP_LAMBDA / weight_sums[1]])
        row_w = (weights * loss_coefs[:, None]).reshape(2 * rows)
        labels = labels.reshape(2 * rows).astype(jnp.float32)

        u_cls, near, c0, c1a, c1b = run_norm(tp.reshape(1).astype(jnp.int32), h_main, h_mtp, gains)
        nx, ny = hop(near, X), hop(near, Y)
        c0x, c0y = hop(c0, X), hop(c0, Y)
        c1ax, c1ay = hop(c1a, X), hop(c1a, Y)
        c1bx, c1by = hop(c1b, X), hop(c1b, Y)
        nd = hop(ny, X)
        c0d = hop(c0x, Y)
        c1ad = hop(c1ay, X)
        c1bd = hop(c1bx, Y)
        zx, zy, zd = hop_tp(nx), hop_tp(ny), hop_tp(nd)
        pieces = {X: (nx, zx, c0x, c1ax, c1bx), Y: (ny, zy, c0y, c1ay, c1by), X | Y: (nd, zd, c0d, c1ad, c1bd)}

        z, stats = run_logits(start, u_cls, w_out, labels[None], 2 * rows)
        other = hop_tp(stats)
        row_max = jnp.maximum(stats[0], other[0])
        row_sum = stats[1] * jnp.exp(stats[0] - row_max) + other[1] * jnp.exp(other[0] - row_max)
        log_norm = row_max + jnp.log(row_sum)
        loss_part = jnp.sum(row_w * (log_norm - (stats[2] + other[2])))

        live = jnp.any(weights.reshape(2, 4, q) > 0, axis=(0, 2))
        used = jnp.where(live[3], 4.0, jnp.where(live[2], 3.0, 2.0))
        info = jnp.stack([log_norm, row_w, labels, jnp.broadcast_to(used, row_w.shape)])
        v = info.reshape(4, 2, 4, q)
        a, b = v[:, :, 0], v[:, :, 1]
        near_far = jnp.stack([jnp.where(tp == 0, a, b), jnp.where(tp == 0, b, a)], axis=1)
        info_sent = jnp.concatenate([near_far, jnp.swapaxes(v[:, :, 2:], 1, 2)], axis=1).reshape(4, 2 * rows)
        infos = {d: hop(info_sent, d) for d in (X, Y, X | Y)}
        start_all = jnp.concatenate([start, jnp.stack([infos[d][3, 0] for d in (X, Y, X | Y)]).astype(jnp.int32)])

        part0 = run_du(start, z, w_out, info, stats, 0, rows)
        other0 = hop_tp(part0)
        e_cls = run_own_e(start, z, info, part0)

        token = part0
        for slot, d in enumerate((X, Y, X | Y)):
            e_cls, u_cls, token = run_class_e(start_all, pieces[d], w_out, infos[d], e_cls, u_cls, token, slot + 1)

        blk = d_model // n_dp
        recv = {}
        dep, previous, send = token, (), None
        for tag in CHAIN:
            d, part = int(tag[0]), int(tag[1])
            where = jnp.stack([core, chip ^ (d // 2)]).astype(jnp.int32)
            last = d == 0
            keep, give, *total = run_grad_w(where, u_cls, e_cls, dep, part, 1 if last else 2, previous)
            if send:
                recv[send] = (hop(total[0], int(send[0])),)
            got = hop(give, CORE)
            previous, send, dep = (keep, got), tag, keep
            if last:
                recv[tag] = (keep, got)
            elif tag == CHAIN[-2]:
                dep = keep + got
                recv[tag] = (hop(dep, d),)
                previous, send = (), None
            elif tag == DU1_AFTER:
                part1 = run_du(start, z, w_out, info, keep, 1, rows)
                other1 = hop_tp(part1)
                dep = part1
        gh0, gg0 = run_norm_back(h_main, part0, other0, gains[:1], keep)
        gh1, gg1 = run_norm_back(h_mtp, part1, other1, gains[1:], gg0)
        sums = jnp.concatenate([gg0.reshape(-1), gg1.reshape(-1), jnp.broadcast_to(loss_part, (128,))])
        for bit in (CORE, X, Y):
            sums = sums + hop(sums, bit)
        loss_total, grad_gain = sums[2 * d_model], sums[:2 * d_model].reshape(2, d_model)

        def place(tags, out, after):
            at = []
            for tag in tags:
                src = chip ^ (int(tag[0]) // 2)
                at.append((jnp.minimum(src * BLOCK_COLS, shard_vocab - BLOCK_COLS) + int(tag[1]) * (BLOCK_COLS // 2)) // NARROW)
            return run_place(jnp.stack(at).astype(jnp.int32), [recv[t] for t in tags], out, after, (blk, shard_vocab))

        out = place(("00", "60", "61", "20", "40"), None, gg1)
        out = place(CHAIN[-3:-1], out, gg1)
        return loss_total, gh0, gh1, out, grad_gain[0], grad_gain[1]


    row_spec = P('dp', None)
    return jax.shard_map(local_step, mesh=mesh, in_specs=(P('dp', None, None), P('dp', None, None), row_spec, row_spec, row_spec, row_spec, P(None), P(None), P(None, 'tp')), out_specs=(P(), P('dp', None, None), P('dp', None, None), P('dp', 'tp'), P(None), P(None)), check_vma=False)
```

time: 841 us -> 815 us (0.969)
  blocking collectives: 103 us -> 0 us
  waiting for transfers between devices: 192 us -> 292 us
  local copies, waits for them, and re-layouts: 42 us -> 12.5 us
  starting transfers between devices: 27.3 us -> 51.8 us
  other arithmetic: 28.4 us -> 14.9 us
    psum x1 -> x0, blocking collectives: 91 us -> none  [local_step(): lax.psum((loss_part, jnp.concatenate([gg0, gg1])), 'dp')]
    ppermute x22 -> x35, waiting for transfers between devices: 99.9 us -> 180 us  [hop(): return lax.ppermute(x, 'dp', [(i, i ^ bit) for i in range(n_dp)])]
    pallas_call x4 -> x7, Pallas kernels: 105 us -> 131 us  [run_grad_w(): pl.pallas_call(grad_w_kernel, out_shape=(jax.ShapeDtypeStruct((blk // 2,...]
    ppermute x22 -> x35, starting transfers between devices: 21.2 us -> 44.8 us  [hop(): return lax.ppermute(x, 'dp', [(i, i ^ bit) for i in range(n_dp)])]
    pallas_call x9 -> x7, Pallas kernels: 129 us -> 108 us  [the longest x3 69.9 us: run_class_e(): pl.pallas_call(functools.partial(class_e_kernel, quarter=rows // 4, slot=...]
    ppermute x6, waiting for transfers between devices: 92.4 us -> 112 us  [hop_tp(): return lax.ppermute(x, 'tp', [(0, 1), (1, 0)])]
    unnamed x40 -> x38, local copies, waits for them, and re-layouts: 25.1 us -> 7.24 us
    add x3 -> x1, other arithmetic: 18.4 us -> 3.18 us  [local_step(): dep = keep + got]
  transfers between devices with their start and end apart: 28 -> 41, of which waited for: 8 -> 19; matrix products, arithmetic and copies ran while one was open for 7% -> 2% of each run, Pallas kernels for 38% -> 38%
where the time goes in v2:
time: 815 us; the launch traced here: 806 us
  Pallas kernels  430 us (53%)
  waiting for transfers between devices  292 us (36%)
  starting transfers between devices  51.8 us (6%)
  other arithmetic  14.9 us (2%)
  local copies, waits for them, and re-layouts  12.5 us (2%)
    ppermute x35, waiting for transfers between devices, hop(): return lax.ppermute(x, 'dp', [(i, i ^ bit) for i in range(n_dp)])  180 us
    pallas_call x7, Pallas kernels, run_grad_w(): pl.pallas_call(grad_w_kernel, out_shape=(jax.ShapeDtypeStruct((blk // 2,...  131 us
    ppermute x6, waiting for transfers between devices, hop_tp(): return lax.ppermute(x, 'tp', [(0, 1), (1, 0)])  112 us
    pallas_call x2, Pallas kernels, run_du(): pl.pallas_call(du_kernel, out_shape=jax.ShapeDtypeStruct((rows, d), jnp.f...  88.7 us
    pallas_call x1, Pallas kernels, run_logits(): pl.pallas_call(functools.partial(logits_kernel, sub=128), out_shape=(jax....  88.7 us
    pallas_call x3, Pallas kernels, run_class_e(): pl.pallas_call(functools.partial(class_e_kernel, quarter=rows // 4, slot=...  69.9 us
    ppermute x35, starting transfers between devices, hop(): return lax.ppermute(x, 'dp', [(i, i ^ bit) for i in range(n_dp)])  44.8 us
  transfers between devices with their start and end apart: 41, of which 19 were waited for; matrix products, arithmetic and copies ran while one was open for 2% of the time, Pallas kernels for 38%

profile of v2, /device:TPU:0, one launch (start us, length us, event | category | flops | bytes accessed | tf_op | source)
XLA Modules:
  0.0 805.6 jit_solution(4907410521228754476)
XLA Ops:
  2.0 9.5 %norm.1 = (bf16[4096,2048]{1,0:T(8,128)(2,1)}, f32[256,2048]{1,0:T(8,128)}, f32[256,2048]{1,0:T(8,128)}, f32[128,2048]{1,0:T(8,128)}, f32[128,2048]{1,0:T(8,128)}) custom-call(s32[1]{0:T(128)} %bitcast.2.tp_ref, bf16[1,512,2048]{2,1,0:T(8,128)(2,1)} %h_ref.2, bf16[1,512,2048]{2,1,0:T(8,128)(2,1)} %h_ref.3, f32[2,2048]{1,0:T(2,128)} %pad_maximum_fusion.1.gain_ref), custom_call_target="tpu_custom_call" | custom-call | flops 8388608000 | bytes 14680064 | tf_op jit(solution)/shard_map/norm/pallas_call | solution.py:62
  17.4 88.7 %logits.1 = (f32[1024,16128]{1,0:T(8,128)}, f32[3,1024]{1,0:T(4,128)}) custom-call(s32[2]{0:T(128)} %pad_add_fusion.start_ref, bf16[4096,2048]{1,0:T(8,128)(2,1)} %get-tuple-element.45.u_ref.refs_8_, bf16[2048,16128]{1,0:T(8,128)(2,1)} %w_ref.5, f32[1,1024]{1,0:T(1,128)} %bitcast.53), custom_call_target="tpu_custom_call" | custom-call | flops 67645734912 | bytes 132120576 | tf_op jit(solution)/shard_map/logits/pallas_call | solution.py:155
  112.0 21.7 %collective-permute-done.2 = f32[2]{0:T(128)S(1)} collective-permute-done((f32[2]{0:T(128)S(1)}, f32[2]{0:T(128)S(1)}, u32[]{:S(2)}, u32[]{:S(2)}) %collective-permute-start.2) | collective-permute-done | bytes 40 | tf_op jit(solution)/shard_map/ppermute | solution.py:416
  137.8 4.0 collective-permute-done.4
  157.3 44.3 %du.2._.refs_9_.a_ref = f32[512,2048]{1,0:T(8,128)} custom-call(s32[2]{0:T(128)} %pad_add_fusion.start_ref, f32[1024,16128]{1,0:T(8,128)} %get-tuple-element.46.z_ref.z0_ref.z1_ref, bf16[2048,16128]{1,0:T(8,128)(2,1)} %w_ref.5, f32[4,1024]{1,0:T(4,128)} %maximum_maximum_fusion.info_ref, f32[3,1024]{1,0:T(4,128)} %get-tuple-element.47._), custom_call_target="tpu_custom_call" | custom-call | flops 33822867456 | bytes 99090432 | tf_op jit(solution)/shard_map/du/pallas_call | solution.py:217
  204.6 13.5 %own_e.1.refs_7_ = bf16[4096,4096]{1,0:T(8,128)(2,1)} custom-call(s32[2]{0:T(128)} %pad_add_fusion.start_ref, f32[1024,16128]{1,0:T(8,128)} %get-tuple-element.46.z_ref.z0_ref.z1_ref, f32[1024,16128]{1,0:T(8,128)} %get-tuple-element.46.z_ref.z0_ref.z1_ref, f32[4,1024]{1,0:T(4,128)} %maximum_maximum_fusion.info_ref, f32[512,2048]{1,0:T(8,128)} %du.2._.refs_9_.a_ref), custom_call_target="tpu_custom_call" | custom-call | flops 8589934592 | bytes 25165824 | tf_op jit(solution)/shard_map/own_e/pallas_call | solution.py:248
  224.3 37.9 %collective-permute-done.10.refs_0_ = f32[256,2048]{1,0:T(8,128)} collective-permute-done((f32[256,2048]{1,0:T(8,128)S(1)}, f32[256,2048]{1,0:T(8,128)}, u32[]{:S(2)}, u32[]{:S(2)}) %collective-permute-start.10) | collective-permute-done | bytes 2097184 | tf_op jit(solution)/shard_map/ppermute | solution.py:416
  262.8 21.7 %class_e.3 = (bf16[4096,4096]{1,0:T(8,128)(2,1)}, bf16[4096,2048]{1,0:T(8,128)(2,1)}, f32[8,128]{1,0:T(8,128)}) custom-call(s32[5]{0:T(128)} %pad_add_fusion.2.start_ref, f32[256,2048]{1,0:T(8,128)} %collective-permute-done.21.refs_0_, f32[256,2048]{1,0:T(8,128)} %collective-permute-done.22.refs_1_, ...), custom_call_target="tpu_custom_call", output_to_operand_aliasing={{0}: (8, {}), {1}: (9, {})} | custom-call | flops 17179869184 | bytes 37748736 | tf_op jit(solution)/shard_map/class_e/pallas_call | solution.py:295
  288.5 4.7 collective-permute-start.15
  293.1 24.1 %class_e.4 = (bf16[4096,4096]{1,0:T(8,128)(2,1)}, bf16[4096,2048]{1,0:T(8,128)(2,1)}, f32[8,128]{1,0:T(8,128)}) custom-call(s32[5]{0:T(128)} %pad_add_fusion.2.start_ref, f32[256,2048]{1,0:T(8,128)} %copy-done, f32[256,2048]{1,0:T(8,128)} %collective-permute-done.18.refs_1_, ...), custom_call_target="tpu_custom_call", output_to_operand_aliasing={{0}: (8, {}), {1}: (9, {})} | custom-call | flops 17179869184 | bytes 37748736 | tf_op jit(solution)/shard_map/class_e/pallas_call | solution.py:295
  317.2 15.7 %collective-permute-done.17.refs_4_ = f32[128,2048]{1,0:T(8,128)} collective-permute-done((f32[128,2048]{1,0:T(8,128)S(1)}, f32[128,2048]{1,0:T(8,128)}, u32[]{:S(2)}, u32[]{:S(2)}) %collective-permute-start.17) | collective-permute-done | bytes 1048608 | tf_op jit(solution)/shard_map/ppermute | solution.py:416
  333.0 24.1 %class_e.5 = (bf16[4096,4096]{1,0:T(8,128)(2,1)}, bf16[4096,2048]{1,0:T(8,128)(2,1)}, f32[8,128]{1,0:T(8,128)}) custom-call(s32[5]{0:T(128)} %pad_add_fusion.2.start_ref, f32[256,2048]{1,0:T(8,128)} %collective-permute-done.10.refs_0_, f32[256,2048]{1,0:T(8,128)} %collective-permute-done.11.refs_1_, ...), custom_call_target="tpu_custom_call", output_to_operand_aliasing={{0}: (8, {}), {1}: (9, {})} | custom-call | flops 17179869184 | bytes 37748736 | tf_op jit(solution)/shard_map/class_e/pallas_call | solution.py:295
  357.0 16.3 %grad_w.7 = (f32[256,2048]{1,0:T(8,128)}, f32[256,2048]{1,0:T(8,128)}) custom-call(s32[2]{0:T(128)} %pad_add_fusion.5.start_ref, bf16[4096,2048]{1,0:T(8,128)(2,1)} %get-tuple-element.58.u_ref, bf16[4096,4096]{1,0:T(8,128)(2,1)} %get-tuple-element.59.e_ref, f32[8,128]{1,0:T(8,128)} %get-tuple-element.60._), custom_call_target="tpu_custom_call" | custom-call | flops 8589934592 | bytes 25165824 | tf_op jit(solution)/shard_map/grad_w/pallas_call | solution.py:343
  373.3 4.4 collective-permute-done.24.refs_1_
  379.0 17.6 %grad_w.8 = (f32[256,2048]{1,0:T(8,128)}, f32[256,2048]{1,0:T(8,128)}, f32[256,2048]{1,0:T(8,128)}) custom-call(s32[2]{0:T(128)} %pad_add_fusion.5.start_ref, bf16[4096,2048]{1,0:T(8,128)(2,1)} %get-tuple-element.58.u_ref, bf16[4096,4096]{1,0:T(8,128)(2,1)} %get-tuple-element.59.e_ref, f32[256,2048]{1,0:T(8,128)} %get-tuple-element.61._.refs_0_, ...), custom_call_target="tpu_custom_call" | custom-call | flops 8589934592 | bytes 25165824 | tf_op jit(solution)/shard_map/grad_w/pallas_call | solution.py:343
  402.3 17.6 %grad_w.9 = (f32[256,2048]{1,0:T(8,128)}, f32[256,2048]{1,0:T(8,128)}, f32[256,2048]{1,0:T(8,128)}) custom-call(s32[2]{0:T(128)} %pad_add_fusion.4.start_ref, bf16[4096,2048]{1,0:T(8,128)(2,1)} %get-tuple-element.58.u_ref, bf16[4096,4096]{1,0:T(8,128)(2,1)} %get-tuple-element.59.e_ref, f32[256,2048]{1,0:T(8,128)} %get-tuple-element.63._.refs_0_, ...), custom_call_target="tpu_custom_call" | custom-call | flops 8589934592 | bytes 25165824 | tf_op jit(solution)/shard_map/grad_w/pallas_call | solution.py:343
  420.1 44.4 %du.3._.a_ref = f32[512,2048]{1,0:T(8,128)} custom-call(s32[2]{0:T(128)} %pad_add_fusion.start_ref, f32[1024,16128]{1,0:T(8,128)} %get-tuple-element.46.z_ref.z0_ref.z1_ref, bf16[2048,16128]{1,0:T(8,128)(2,1)} %w_ref.5, f32[4,1024]{1,0:T(4,128)} %maximum_maximum_fusion.info_ref, f32[256,2048]{1,0:T(8,128)} %get-tuple-element.65._.refs_0_), custom_call_target="tpu_custom_call" | custom-call | flops 33822867456 | bytes 99090432 | tf_op jit(solution)/shard_map/du/pallas_call | solution.py:217
  465.9 17.8 %grad_w.10 = (f32[256,2048]{1,0:T(8,128)}, f32[256,2048]{1,0:T(8,128)}, f32[256,2048]{1,0:T(8,128)}) custom-call(s32[2]{0:T(128)} %pad_add_fusion.3.start_ref, bf16[4096,2048]{1,0:T(8,128)(2,1)} %get-tuple-element.58.u_ref, bf16[4096,4096]{1,0:T(8,128)(2,1)} %get-tuple-element.59.e_ref, f32[512,2048]{1,0:T(8,128)} %du.3._.a_ref, ...), custom_call_target="tpu_custom_call" | custom-call | flops 8589934592 | bytes 25165824 | tf_op jit(solution)/shard_map/grad_w/pallas_call | solution.py:343
  483.9 4.1 collective-permute-done.27.refs_1_
  489.3 17.6 %grad_w.11 = (f32[256,2048]{1,0:T(8,128)}, f32[256,2048]{1,0:T(8,128)}, f32[256,2048]{1,0:T(8,128)}) custom-call(s32[2]{0:T(128)} %pad_add_fusion.4.start_ref, bf16[4096,2048]{1,0:T(8,128)(2,1)} %get-tuple-element.58.u_ref, bf16[4096,4096]{1,0:T(8,128)(2,1)} %get-tuple-element.59.e_ref, f32[256,2048]{1,0:T(8,128)} %get-tuple-element.67._.refs_0_, ...), custom_call_target="tpu_custom_call" | custom-call | flops 8589934592 | bytes 25165824 | tf_op jit(solution)/shard_map/grad_w/pallas_call | solution.py:343
  512.6 17.6 %grad_w.12 = (f32[256,2048]{1,0:T(8,128)}, f32[256,2048]{1,0:T(8,128)}, f32[256,2048]{1,0:T(8,128)}) custom-call(s32[2]{0:T(128)} %pad_add_fusion.3.start_ref, bf16[4096,2048]{1,0:T(8,128)(2,1)} %get-tuple-element.58.u_ref, bf16[4096,4096]{1,0:T(8,128)(2,1)} %get-tuple-element.59.e_ref, f32[256,2048]{1,0:T(8,128)} %get-tuple-element.69._.refs_0_, ...), custom_call_target="tpu_custom_call" | custom-call | flops 8589934592 | bytes 25165824 | tf_op jit(solution)/shard_map/grad_w/pallas_call | solution.py:343
  537.9 26.1 %grad_w.13 = (f32[256,4096]{1,0:T(8,128)}, f32[256,4096]{1,0:T(8,128)}) custom-call(s32[2]{0:T(128)} %pad_add_fusion.1.start_ref, bf16[4096,2048]{1,0:T(8,128)(2,1)} %get-tuple-element.58.u_ref, bf16[4096,4096]{1,0:T(8,128)(2,1)} %get-tuple-element.59.e_ref, f32[256,2048]{1,0:T(8,128)} %add.69._), custom_call_target="tpu_custom_call" | custom-call | flops 17179869184 | bytes 46137344 | tf_op jit(solution)/shard_map/grad_w/pallas_call | solution.py:343
  564.4 6.2 collective-permute-start.37
  570.7 30.4 %collective-permute-done.5.b_ref = f32[512,2048]{1,0:T(8,128)} collective-permute-done((f32[512,2048]{1,0:T(8,128)}, f32[512,2048]{1,0:T(8,128)}, u32[]{:S(2)}, u32[]{:S(2)}) %collective-permute-start.5) | collective-permute-done | bytes 4194336 | tf_op jit(solution)/shard_map/ppermute | solution.py:419
  601.1 7.1 norm_back.2
  608.2 81.9 %collective-permute-done.30.b_ref = f32[512,2048]{1,0:T(8,128)} collective-permute-done((f32[512,2048]{1,0:T(8,128)}, f32[512,2048]{1,0:T(8,128)}, u32[]{:S(2)}, u32[]{:S(2)}) %collective-permute-start.30) | collective-permute-done | bytes 4194336 | tf_op jit(solution)/shard_map/ppermute | solution.py:419
  690.1 7.3 norm_back.3
  704.5 4.7 collective-permute-start.40
  711.5 43.4 %collective-permute-done.33 = f32[4224]{0:T(1024)S(1)} collective-permute-done((f32[4224]{0:T(1024)S(1)}, f32[4224]{0:T(1024)S(1)}, u32[]{:S(2)}, u32[]{:S(2)}) %collective-permute-start.33) | collective-permute-done | bytes 16928 | tf_op jit(solution)/shard_map/ppermute | solution.py:416
  759.1 11.1 %place.2.refs_2_ = f32[256,16128]{1,0:T(8,128)} custom-call(s32[5]{0:T(128)} %stack.135.at_ref, f32[256,4096]{1,0:T(8,128)} %get-tuple-element.73._.refs_0_, f32[256,4096]{1,0:T(8,128)} %collective-permute-done.36.refs_1_, f32[256,2048]{1,0:T(8,128)} %collective-permute-done.37.refs_2_, f32[256,2048]{1,0:T(8,128)} %collective-permute-done.38.refs_3_, ...), custom_call_target="tpu_custom_call" | custom-call | flops 838860800 | bytes 33554432 | tf_op jit(solution)/shard_map/place/pallas_call | solution.py:397
  770.2 24.2 %collective-permute-done.34.refs_0_ = f32[256,2048]{1,0:T(8,128)} collective-permute-done((f32[256,2048]{1,0:T(8,128)}, f32[256,2048]{1,0:T(8,128)}, u32[]{:S(2)}, u32[]{:S(2)}) %collective-permute-start.34) | collective-permute-done | bytes 2097184 | tf_op jit(solution)/shard_map/ppermute | solution.py:416
  794.4 7.0 collective-permute-done.35.refs_1_
  (151 shorter events, 85.4 us)
Async XLA Ops:
  11.4 143.8 %collective-permute-start.21 = (f32[256,2048]{1,0:T(8,128)}, f32[256,2048]{1,0:T(8,128)}, u32[]{:S(2)}, u32[]{:S(2)}) collective-permute-start(f32[256,2048]{1,0:T(8,128)} %get-tuple-element.48), channel_id=1, source_target_pairs={{0,2},{1,3},{2,0},{3,1},{4,6},{5,7},{6,4},{7,5},{8,10},{9,11},{10,... | collective-permute-start | bytes 6291464 | tf_op jit(solution)/shard_map/ppermute | solution.py:416
  14.7 141.0 %collective-permute-start.9 = (f32[256,2048]{1,0:T(8,128)}, f32[256,2048]{1,0:T(8,128)S(1)}, u32[]{:S(2)}, u32[]{:S(2)}) collective-permute-start(f32[256,2048]{1,0:T(8,128)} %get-tuple-element.48), channel_id=1, source_target_pairs={{0,4},{1,5},{2,6},{3,7},{4,0},{5,1},{6,2},{7,3},{8,12},{9,13},{10,... | collective-permute-start | bytes 6291464 | tf_op jit(solution)/shard_map/ppermute | solution.py:416
  106.1 37.8 %collective-permute-start = (f32[3,1024]{1,0:T(4,128)}, f32[3,1024]{1,0:T(4,128)S(1)}, u32[]{:S(2)}, u32[]{:S(2)}) collective-permute-start(f32[3,1024]{1,0:T(4,128)} %get-tuple-element.47._), channel_id=1, source_target_pairs={{0,8},{8,0},{1,9},{9,1},{2,10},{10,2},{3,11},{11,3},{4,12},{12,4},... | collective-permute-start | bytes 36872 | tf_op jit(solution)/shard_map/ppermute | solution.py:419
  107.8 46.9 %collective-permute-start.16 = (f32[128,2048]{1,0:T(8,128)}, f32[128,2048]{1,0:T(8,128)S(1)}, u32[]{:S(2)}, u32[]{:S(2)}) collective-permute-start(f32[128,2048]{1,0:T(8,128)} %get-tuple-element.51), channel_id=1, source_target_pairs={{0,2},{1,3},{2,0},{3,1},{4,6},{5,7},{6,4},{7,5},{8,10},{9,11},{10,... | collective-permute-start | bytes 3145736 | tf_op jit(solution)/shard_map/ppermute | solution.py:416
  110.5 23.2 %collective-permute-start.2 = (f32[2]{0:T(128)S(1)}, f32[2]{0:T(128)S(1)}, u32[]{:S(2)}, u32[]{:S(2)}) collective-permute-start(f32[2]{0:T(128)S(1)} %add.64), channel_id=1, source_target_pairs={{0,2},{1,3},{2,0},{3,1},{4,6},{5,7},{6,4},{7,5},{8,10},{9,11},{10,... | collective-permute-start | bytes 32 | tf_op jit(solution)/shard_map/ppermute | solution.py:416
  137.3 4.5 collective-permute-start.4
  149.4 4.8 collective-permute-start.8
  150.5 51.0 %collective-permute-start.23 = (f32[128,2048]{1,0:T(8,128)}, f32[128,2048]{1,0:T(8,128)}, u32[]{:S(2)}, u32[]{:S(2)}) collective-permute-start(f32[128,2048]{1,0:T(8,128)} %get-tuple-element.50), channel_id=1, source_target_pairs={{0,2},{1,3},{2,0},{3,1},{4,6},{5,7},{6,4},{7,5},{8,10},{9,11},{10,... | collective-permute-start | bytes 3145736 | tf_op jit(solution)/shard_map/ppermute | solution.py:416
  154.2 48.9 %collective-permute-start.14 = (f32[128,2048]{1,0:T(8,128)}, f32[128,2048]{1,0:T(8,128)}, u32[]{:S(2)}, u32[]{:S(2)}) collective-permute-start(f32[128,2048]{1,0:T(8,128)} %get-tuple-element.50), channel_id=1, source_target_pairs={{0,4},{1,5},{2,6},{3,7},{4,0},{5,1},{6,2},{7,3},{8,12},{9,13},{10,... | collective-permute-start | bytes 3145736 | tf_op jit(solution)/shard_map/ppermute | solution.py:416
  154.7 67.6 %collective-permute-start.12 = (f32[256,2048]{1,0:T(8,128)}, f32[256,2048]{1,0:T(8,128)}, u32[]{:S(2)}, u32[]{:S(2)}) collective-permute-start(f32[256,2048]{1,0:T(8,128)} %get-tuple-element.49), channel_id=1, source_target_pairs={{0,2},{1,3},{2,0},{3,1},{4,6},{5,7},{6,4},{7,5},{8,10},{9,11},{10,... | collective-permute-start | bytes 6291464 | tf_op jit(solution)/shard_map/ppermute | solution.py:416
  155.2 68.1 %collective-permute-start.22 = (f32[256,2048]{1,0:T(8,128)}, f32[256,2048]{1,0:T(8,128)}, u32[]{:S(2)}, u32[]{:S(2)}) collective-permute-start(f32[256,2048]{1,0:T(8,128)} %collective-permute-done.21.refs_0_), channel_id=1, source_target_pairs={{0,8},{8,0},{1,9},{9,1},{2,10},{10,2},{3,11},{11,3},{4,12},{12,4},... | collective-permute-start | bytes 6291464 | tf_op jit(solution)/shard_map/ppermute | solution.py:419
  155.7 106.6 %collective-permute-start.10 = (f32[256,2048]{1,0:T(8,128)S(1)}, f32[256,2048]{1,0:T(8,128)}, u32[]{:S(2)}, u32[]{:S(2)}) collective-permute-start(f32[256,2048]{1,0:T(8,128)S(1)} %collective-permute-done.9.refs_0_), channel_id=1, source_target_pairs={{0,2},{1,3},{2,0},{3,1},{4,6},{5,7},{6,4},{7,5},{8,10},{9,11},{10,... | collective-permute-start | bytes 6291464 | tf_op jit(solution)/shard_map/ppermute | solution.py:416
  201.6 86.9 %collective-permute-start.19 = (f32[256,2048]{1,0:T(8,128)}, f32[256,2048]{1,0:T(8,128)}, u32[]{:S(2)}, u32[]{:S(2)}) collective-permute-start(f32[256,2048]{1,0:T(8,128)} %get-tuple-element.49), channel_id=1, source_target_pairs={{0,4},{1,5},{2,6},{3,7},{4,0},{5,1},{6,2},{7,3},{8,12},{9,13},{10,... | collective-permute-start | bytes 6291464 | tf_op jit(solution)/shard_map/ppermute | solution.py:416
  203.1 90.0 %collective-permute-start.18 = (f32[256,2048]{1,0:T(8,128)S(1)}, f32[256,2048]{1,0:T(8,128)}, u32[]{:S(2)}, u32[]{:S(2)}) collective-permute-start(f32[256,2048]{1,0:T(8,128)S(1)} %collective-permute-done.9.refs_0_), channel_id=1, source_target_pairs={{0,8},{8,0},{1,9},{9,1},{2,10},{10,2},{3,11},{11,3},{4,12},{12,4},... | collective-permute-start | bytes 6291464 | tf_op jit(solution)/shard_map/ppermute | solution.py:419
  222.3 62.2 %collective-permute-start.20 = (f32[128,2048]{1,0:T(8,128)}, f32[128,2048]{1,0:T(8,128)}, u32[]{:S(2)}, u32[]{:S(2)}) collective-permute-start(f32[128,2048]{1,0:T(8,128)} %get-tuple-element.51), channel_id=1, source_target_pairs={{0,4},{1,5},{2,6},{3,7},{4,0},{5,1},{6,2},{7,3},{8,12},{9,13},{10,... | collective-permute-start | bytes 3145736 | tf_op jit(solution)/shard_map/ppermute | solution.py:416
  223.4 109.6 %collective-permute-start.13 = (f32[256,2048]{1,0:T(8,128)}, f32[256,2048]{1,0:T(8,128)}, u32[]{:S(2)}, u32[]{:S(2)}) collective-permute-start(f32[256,2048]{1,0:T(8,128)} %collective-permute-done.12.refs_2_), channel_id=1, source_target_pairs={{0,4},{1,5},{2,6},{3,7},{4,0},{5,1},{6,2},{7,3},{8,12},{9,13},{10,... | collective-permute-start | bytes 6291464 | tf_op jit(solution)/shard_map/ppermute | solution.py:416
  262.2 70.7 %collective-permute-start.11 = (f32[256,2048]{1,0:T(8,128)}, f32[256,2048]{1,0:T(8,128)}, u32[]{:S(2)}, u32[]{:S(2)}) collective-permute-start(f32[256,2048]{1,0:T(8,128)} %collective-permute-done.10.refs_0_), channel_id=1, source_target_pairs={{0,8},{8,0},{1,9},{9,1},{2,10},{10,2},{3,11},{11,3},{4,12},{12,4},... | collective-permute-start | bytes 6291464 | tf_op jit(solution)/shard_map/ppermute | solution.py:419
  284.5 48.5 %collective-permute-start.17 = (f32[128,2048]{1,0:T(8,128)S(1)}, f32[128,2048]{1,0:T(8,128)}, u32[]{:S(2)}, u32[]{:S(2)}) collective-permute-start(f32[128,2048]{1,0:T(8,128)S(1)} %copy-done.8), channel_id=1, source_target_pairs={{0,4},{1,5},{2,6},{3,7},{4,0},{5,1},{6,2},{7,3},{8,12},{9,13},{10,... | collective-permute-start | bytes 3145736 | tf_op jit(solution)/shard_map/ppermute | solution.py:416
  288.5 28.8 %collective-permute-start.15 = (f32[128,2048]{1,0:T(8,128)}, f32[128,2048]{1,0:T(8,128)}, u32[]{:S(2)}, u32[]{:S(2)}) collective-permute-start(f32[128,2048]{1,0:T(8,128)} %collective-permute-done.14.refs_3_), channel_id=1, source_target_pairs={{0,2},{1,3},{2,0},{3,1},{4,6},{5,7},{6,4},{7,5},{8,10},{9,11},{10,... | collective-permute-start | bytes 3145736 | tf_op jit(solution)/shard_map/ppermute | solution.py:416
  419.9 44.7 %collective-permute-start.26 = (f32[256,2048]{1,0:T(8,128)}, f32[256,2048]{1,0:T(8,128)S(1)}, u32[]{:S(2)}, u32[]{:S(2)}) collective-permute-start(f32[256,2048]{1,0:T(8,128)} %get-tuple-element.66), channel_id=1, source_target_pairs={{0,1},{1,0},{2,3},{3,2},{4,5},{5,4},{6,7},{7,6},{8,9},{9,8},{10,11... | collective-permute-start | bytes 6291464 | tf_op jit(solution)/shard_map/ppermute | solution.py:416
  506.9 4.4 collective-permute-start.28
  507.3 93.8 %collective-permute-start.5 = (f32[512,2048]{1,0:T(8,128)}, f32[512,2048]{1,0:T(8,128)}, u32[]{:S(2)}, u32[]{:S(2)}) collective-permute-start(f32[512,2048]{1,0:T(8,128)} %du.2._.refs_9_.a_ref), channel_id=1, source_target_pairs={{0,8},{8,0},{1,9},{9,1},{2,10},{10,2},{3,11},{11,3},{4,12},{12,4},... | collective-permute-start | bytes 12582920 | tf_op jit(solution)/shard_map/ppermute | solution.py:419
  530.2 4.4 collective-permute-start.29
  530.7 159.4 %collective-permute-start.30 = (f32[512,2048]{1,0:T(8,128)}, f32[512,2048]{1,0:T(8,128)}, u32[]{:S(2)}, u32[]{:S(2)}) collective-permute-start(f32[512,2048]{1,0:T(8,128)} %du.3._.a_ref), channel_id=1, source_target_pairs={{0,8},{8,0},{1,9},{9,1},{2,10},{10,2},{3,11},{11,3},{4,12},{12,4},... | collective-permute-start | bytes 12582920 | tf_op jit(solution)/shard_map/ppermute | solution.py:419
  564.0 195.2 %collective-permute-start.36 = (f32[256,4096]{1,0:T(8,128)}, f32[256,4096]{1,0:T(8,128)}, u32[]{:S(2)}, u32[]{:S(2)}) collective-permute-start(f32[256,4096]{1,0:T(8,128)} %get-tuple-element.79), channel_id=1, source_target_pairs={{0,1},{1,0},{2,3},{3,2},{4,5},{5,4},{6,7},{7,6},{8,9},{9,8},{10,11... | collective-permute-start | bytes 12582920 | tf_op jit(solution)/shard_map/ppermute | solution.py:416
  564.4 144.8 %collective-permute-start.37 = (f32[256,2048]{1,0:T(8,128)}, f32[256,2048]{1,0:T(8,128)}, u32[]{:S(2)}, u32[]{:S(2)}) collective-permute-start(f32[256,2048]{1,0:T(8,128)} %get-tuple-element.80), channel_id=1, source_target_pairs={{0,6},{1,7},{2,4},{3,5},{4,2},{5,3},{6,0},{7,1},{8,14},{9,15},{10,... | collective-permute-start | bytes 6291464 | tf_op jit(solution)/shard_map/ppermute | solution.py:416
  570.7 138.6 %collective-permute-start.38 = (f32[256,2048]{1,0:T(8,128)}, f32[256,2048]{1,0:T(8,128)}, u32[]{:S(2)}, u32[]{:S(2)}) collective-permute-start(f32[256,2048]{1,0:T(8,128)} %get-tuple-element.81), channel_id=1, source_target_pairs={{0,6},{1,7},{2,4},{3,5},{4,2},{5,3},{6,0},{7,1},{8,14},{9,15},{10,... | collective-permute-start | bytes 6291464 | tf_op jit(solution)/shard_map/ppermute | solution.py:416
  701.6 57.5 %collective-permute-start.39 = (f32[256,2048]{1,0:T(8,128)}, f32[256,2048]{1,0:T(8,128)}, u32[]{:S(2)}, u32[]{:S(2)}) collective-permute-start(f32[256,2048]{1,0:T(8,128)} %get-tuple-element.82), channel_id=1, source_target_pairs={{0,2},{1,3},{2,0},{3,1},{4,6},{5,7},{6,4},{7,5},{8,10},{9,11},{10,... | collective-permute-start | bytes 6291464 | tf_op jit(solution)/shard_map/ppermute | solution.py:416
  704.5 54.6 %collective-permute-start.40 = (f32[256,2048]{1,0:T(8,128)}, f32[256,2048]{1,0:T(8,128)}, u32[]{:S(2)}, u32[]{:S(2)}) collective-permute-start(f32[256,2048]{1,0:T(8,128)} %get-tuple-element.83), channel_id=1, source_target_pairs={{0,4},{1,5},{2,6},{3,7},{4,0},{5,1},{6,2},{7,3},{8,12},{9,13},{10,... | collective-permute-start | bytes 6291464 | tf_op jit(solution)/shard_map/ppermute | solution.py:416
  709.2 45.7 %collective-permute-start.33 = (f32[4224]{0:T(1024)S(1)}, f32[4224]{0:T(1024)S(1)}, u32[]{:S(2)}, u32[]{:S(2)}) collective-permute-start(f32[4224]{0:T(1024)S(1)} %add.72), channel_id=1, source_target_pairs={{0,4},{1,5},{2,6},{3,7},{4,0},{5,1},{6,2},{7,3},{8,12},{9,13},{10,... | collective-permute-start | bytes 50696 | tf_op jit(solution)/shard_map/ppermute | solution.py:416
  709.3 85.1 %collective-permute-start.34 = (f32[256,2048]{1,0:T(8,128)}, f32[256,2048]{1,0:T(8,128)}, u32[]{:S(2)}, u32[]{:S(2)}) collective-permute-start(f32[256,2048]{1,0:T(8,128)} %get-tuple-element.78), channel_id=1, source_target_pairs={{0,2},{1,3},{2,0},{3,1},{4,6},{5,7},{6,4},{7,5},{8,10},{9,11},{10,... | collective-permute-start | bytes 6291464 | tf_op jit(solution)/shard_map/ppermute | solution.py:416
  754.9 46.5 %collective-permute-start.35 = (f32[256,2048]{1,0:T(8,128)S(1)}, f32[256,2048]{1,0:T(8,128)}, u32[]{:S(2)}, u32[]{:S(2)}) collective-permute-start(f32[256,2048]{1,0:T(8,128)S(1)} %copy-done.1), channel_id=1, source_target_pairs={{0,4},{1,5},{2,6},{3,7},{4,0},{5,1},{6,2},{7,3},{8,12},{9,13},{10,... | collective-permute-start | bytes 6291464 | tf_op jit(solution)/shard_map/ppermute | solution.py:416
  (27 other events, 811.1 us)

commit v3 on v2

--- a/solution.py
+++ b/solution.py
@@ -11,12 +11,11 @@
 NORM_EPS = 1e-6
 MTP_LAMBDA = 0.3
 BLOCK_COLS = 4096
-TILE = 2304
+TILE = 1792
 L_TILE = 768
 NARROW = 256
 VMEM_LIMIT = 60 * 1024 * 1024
 CHAIN = ("60", "61", "20", "40", "21", "41", "00")
-DU1_AFTER = "20"
 NN = (((1,), (0,)), ((), ()))
 NT = (((1,), (1,)), ((), ()))
 
@@ -28,7 +27,7 @@
 HBM = pl.BlockSpec(memory_space=pl.ANY)
 
 
-def norm_kernel(tp_ref, h0_ref, h1_ref, gain_ref, u_ref, near_ref, third_ref, *last_refs):
+def norm_kernel(tp_ref, h0_ref, h1_ref, gain_ref, u_ref, near_ref, third_ref, last_ref):
     head, b = pl.program_id(0), pl.program_id(1)
 
     def rows_of(h_ref):
@@ -51,7 +50,7 @@
 
             @pl.when(b == 3)
             def _():
-                last_refs[i][...] = u
+                last_ref[...] = u
 
 
 def run_norm(tp, h0, h1, gains):
@@ -61,11 +60,11 @@
     blk = lambda f: pl.BlockSpec((q, d), f)
     return pl.pallas_call(
         norm_kernel,
-        out_shape=(jax.ShapeDtypeStruct((8 * rows, d), jnp.bfloat16), jax.ShapeDtypeStruct((2 * q, d), f32), jax.ShapeDtypeStruct((2 * q, d), f32), jax.ShapeDtypeStruct((q, d), f32), jax.ShapeDtypeStruct((q, d), f32)),
+        out_shape=(jax.ShapeDtypeStruct((8 * rows, d), jnp.bfloat16), jax.ShapeDtypeStruct((2 * q, d), f32), jax.ShapeDtypeStruct((2 * q, d), f32), jax.ShapeDtypeStruct((2 * q, d), f32)),
         grid_spec=pltpu.PrefetchScalarGridSpec(
             num_scalar_prefetch=1, grid=(2, 4),
             in_specs=[pl.BlockSpec((1, q, d), lambda h, b, s: (0, jnp.where(h == 0, b, 3), 0)), pl.BlockSpec((1, q, d), lambda h, b, s: (0, jnp.where(h == 0, 0, b), 0)), pl.BlockSpec((2, d), lambda h, b, s: (0, 0))],
-            out_specs=(blk(lambda h, b, s: (4 * h + b, 0)), blk(lambda h, b, s: (h, 0)), blk(lambda h, b, s: (h, 0)), blk(lambda h, b, s: (0, 0)), blk(lambda h, b, s: (0, 0)))),
+            out_specs=(blk(lambda h, b, s: (4 * h + b, 0)), blk(lambda h, b, s: (h, 0)), blk(lambda h, b, s: (h, 0)), blk(lambda h, b, s: (h, 0)))),
         compiler_params=params("arbitrary", "arbitrary"),
         cost_estimate=pl.CostEstimate(flops=8 * rows * d * 1000, bytes_accessed=14 * rows * d, transcendentals=rows),
         name="norm",
@@ -88,10 +87,10 @@
     out_ref[0] = gx.astype(jnp.bfloat16)
 
 
-def run_norm_back(h, a, b, gain, dep):
+def run_norm_back(h, a, b, gain, head, dep):
     _, rows, d = h.shape
     q = 128
-    row = pl.BlockSpec((q, d), lambda i: (i, 0))
+    row = pl.BlockSpec((q, d), lambda i: (head * (rows // q) + i, 0))
     row3 = pl.BlockSpec((1, q, d), lambda i: (0, i, 0))
     one = pl.BlockSpec((1, d), lambda i: (0, 0))
     return pl.pallas_call(
@@ -119,10 +118,10 @@
         off_ref[...] = label_offset(lab_ref[...], start_ref[0])
 
     base = j * tile
-    z_ref[...] = lax.dot_general(u_ref[...], w_ref[...], NN, preferred_element_type=jnp.float32)
     for i in range(rows // sub):
         r = pl.ds(i * sub, sub)
-        z = z_ref[r, :]
+        z = lax.dot_general(u_ref[r, :], w_ref[...], NN, preferred_element_type=jnp.float32)
+        z_ref[r, :] = z
         parts = [z[:, k * lanes:(k + 1) * lanes] for k in range(tile // lanes)]
         m_old = m_ref[r, :]
         m_new = m_old
@@ -153,7 +152,7 @@
     d, cols = w.shape
     full = lambda j, s: (0, 0)
     return pl.pallas_call(
-        functools.partial(logits_kernel, sub=128),
+        functools.partial(logits_kernel, sub=256),
         out_shape=(jax.ShapeDtypeStruct((rows, cols), jnp.float32), jax.ShapeDtypeStruct((3, rows), jnp.float32)),
         grid_spec=pltpu.PrefetchScalarGridSpec(
             num_scalar_prefetch=1, grid=(cols // L_TILE,),
@@ -194,74 +193,52 @@
     return [pltpu.VMEM((rows, 128), jnp.float32), pltpu.VMEM((rows, 128), jnp.float32), pltpu.VMEM((rows, 128), jnp.int32)]
 
 
-def du_kernel(start_ref, z_ref, w_ref, info_ref, _, out_ref, acc_ref, shift_ref, weight_ref, off_ref):
+def du_kernel(start_ref, z_ref, w_ref, info_ref, out_ref, e_ref, shift_ref, weight_ref, off_ref):
     j = pl.program_id(0)
+    tile = z_ref.shape[1]
 
     @pl.when(j == 0)
     def _():
-        acc_ref[...] = jnp.zeros_like(acc_ref)
+        out_ref[...] = jnp.zeros_like(out_ref)
         fill_rows(start_ref, info_ref, shift_ref, weight_ref, off_ref)
 
-    e = e_tile(z_ref[...], shift_ref[...], weight_ref[...], off_ref[...] - j * z_ref.shape[1])
-    acc_ref[...] += lax.dot_general(e, w_ref[...], NT, preferred_element_type=jnp.float32)
+    e = e_tile(z_ref[...], shift_ref[...], weight_ref[...], off_ref[...] - j * tile)
+    out_ref[...] += lax.dot_general(e, w_ref[...], NT, preferred_element_type=jnp.float32)
+
+    for k in range(tile // NARROW):
+        at = j * (tile // NARROW) + k - start_ref[1]
+
+        @pl.when((at >= 0) & (at < BLOCK_COLS // NARROW))
+        def _():
+            e_ref[:, pl.ds(pl.multiple_of(at * NARROW, NARROW), NARROW)] = e[:, k * NARROW:(k + 1) * NARROW]
 
     @pl.when(j == pl.num_programs(0) - 1)
     def _():
-        out_ref[...] = acc_ref[...].astype(jnp.bfloat16).astype(jnp.float32)
-
-
-def run_du(start, z, w, info, dep, head, rows):
+        out_ref[...] = out_ref[...].astype(jnp.bfloat16).astype(jnp.float32)
+
+
+def run_du(start, z, w, info):
     d, cols = w.shape
-    steps = cols // TILE
-    vec = pl.BlockSpec((info.shape[0], rows), lambda j, s: (0, head))
+    rows = info.shape[1]
+    full = lambda j, s: (0, 0)
+    once = pl.Buffered(1)
     return pl.pallas_call(
         du_kernel,
-        out_shape=jax.ShapeDtypeStruct((rows, d), jnp.float32),
+        out_shape=(jax.ShapeDtypeStruct((rows, d), jnp.float32), jax.ShapeDtypeStruct((4 * rows, BLOCK_COLS), jnp.bfloat16)),
         grid_spec=pltpu.PrefetchScalarGridSpec(
-            num_scalar_prefetch=1, grid=(steps,),
-            in_specs=[pl.BlockSpec((rows, TILE), lambda j, s: (head, j)), pl.BlockSpec((d, TILE), lambda j, s: (0, j)), vec, HBM],
-            out_specs=pl.BlockSpec((rows, d), lambda j, s: (0, 0)),
-            scratch_shapes=[pltpu.VMEM((rows, d), jnp.float32)] + row_scratch(rows)),
+            num_scalar_prefetch=1, grid=(cols // TILE,),
+            in_specs=[pl.BlockSpec((rows, TILE), lambda j, s: (0, j)), pl.BlockSpec((d, TILE), lambda j, s: (0, j)), pl.BlockSpec(info.shape, full)],
+            out_specs=(pl.BlockSpec((rows, d), full, pipeline_mode=once), pl.BlockSpec((rows, BLOCK_COLS), full, pipeline_mode=once)),
+            scratch_shapes=row_scratch(rows)),
         compiler_params=params("arbitrary"),
         cost_estimate=pl.CostEstimate(flops=2 * rows * d * cols, bytes_accessed=cols * (2 * d + 4 * rows), transcendentals=rows * cols),
         name="du",
-    )(start, z, w, info, dep)
-
-
-def own_e_kernel(start_ref, z0_ref, z1_ref, info_ref, _, e_ref, shift_ref, weight_ref, off_ref):
-    j = pl.program_id(0)
-
-    @pl.when(j == 0)
-    def _():
-        fill_rows(start_ref, info_ref, shift_ref, weight_ref, off_ref)
-
-    for k, z_ref in enumerate((z0_ref, z1_ref)):
-        at = (start_ref[1] + 2 * j + k) * NARROW
-        e_ref[:, k * NARROW:(k + 1) * NARROW] = e_tile(z_ref[...], shift_ref[...], weight_ref[...], off_ref[...] - at)
-
-
-def run_own_e(start, z, info, dep):
-    rows = info.shape[1]
-    vec = pl.BlockSpec(info.shape, lambda j, s: (0, 0))
-    z_even = pl.BlockSpec((rows, NARROW), lambda j, s: (0, s[1] + 2 * j))
-    z_odd = pl.BlockSpec((rows, NARROW), lambda j, s: (0, s[1] + 2 * j + 1))
-    return pl.pallas_call(
-        own_e_kernel,
-        out_shape=jax.ShapeDtypeStruct((4 * rows, BLOCK_COLS), jnp.bfloat16),
-        grid_spec=pltpu.PrefetchScalarGridSpec(
-            num_scalar_prefetch=1, grid=(BLOCK_COLS // (2 * NARROW),),
-            in_specs=[z_even, z_odd, vec, HBM],
-            out_specs=pl.BlockSpec((rows, 2 * NARROW), lambda j, s: (0, j)),
-            scratch_shapes=row_scratch(rows)),
-        compiler_params=params("arbitrary"),
-        cost_estimate=pl.CostEstimate(flops=rows * BLOCK_COLS * 2048, bytes_accessed=rows * 6 * BLOCK_COLS, transcendentals=rows * BLOCK_COLS),
-        name="own_e",
-    )(start, z, z, info, dep)
-
-
-def class_e_kernel(start_ref, *refs, quarter, slot):
-    n = len(refs) - 11
-    pieces, (w_ref, info_ref, _, _, _, e_ref, u_ref, token_ref, shift_ref, weight_ref, off_ref) = refs[:n], refs[n:]
+    )(start, z, w, info)
+
+
+def class_e_kernel(start_ref, *refs, quarter):
+    n = len(refs) - 12
+    pieces, (w_ref, info_ref, _, _, _, e_ref, u_ref, token_ref, shift_ref, weight_ref, off_ref, used_ref) = refs[:n], refs[n:]
     j = pl.program_id(0)
     rows = e_ref.shape[0]
 
@@ -273,15 +250,26 @@
             at += p.shape[0]
         fill_rows(start_ref, info_ref, shift_ref, weight_ref, off_ref)
         token_ref[...] = jnp.zeros_like(token_ref)
-
-    used = start_ref[1 + slot]
+        used_ref[0] = jnp.max(info_ref[3:4, :]).astype(jnp.int32)
+
+    used = used_ref[0]
     at = (start_ref[1] + 2 * j) * NARROW
     for count in (2, 3, 4):
         @pl.when(used == count)
         def _():
             r = slice(0, count * quarter)
-            z = lax.dot_general(u_ref[r, :], w_ref[...], NN, preferred_element_type=jnp.float32)
-            e_ref[r, :] = e_tile(z, shift_ref[r, :], weight_ref[r, :], off_ref[r, :] - at)
+
+            def columns(c, at):
+                z = lax.dot_general(u_ref[r, :], w_ref[:, c], NN, preferred_element_type=jnp.float32)
+                e_ref[r, c] = e_tile(z, shift_ref[r, :], weight_ref[r, :], off_ref[r, :] - at)
+
+            if count == 4:
+                columns(slice(0, 2 * NARROW), at)
+            else:
+                @pl.loop(0, 2)
+                def _(i):
+                    columns(pl.ds(pl.multiple_of(i * NARROW, NARROW), NARROW), at + i * NARROW)
+
             if count < 4:
                 e_ref[count * quarter:, :] = jnp.zeros((rows - count * quarter, e_ref.shape[1]), e_ref.dtype)
 
@@ -293,13 +281,13 @@
     once = pl.Buffered(1)
     n = len(pieces)
     return pl.pallas_call(
-        functools.partial(class_e_kernel, quarter=rows // 4, slot=slot),
+        functools.partial(class_e_kernel, quarter=rows // 4),
         out_shape=(jax.ShapeDtypeStruct(e_all.shape, e_all.dtype), jax.ShapeDtypeStruct(u_all.shape, u_all.dtype), jax.ShapeDtypeStruct((8, 128), jnp.float32)),
         grid_spec=pltpu.PrefetchScalarGridSpec(
             num_scalar_prefetch=1, grid=(BLOCK_COLS // (2 * NARROW),),
             in_specs=[pl.BlockSpec(p.shape, full, pipeline_mode=once) for p in pieces] + [pl.BlockSpec((pl.Element(d), pl.Element(2 * NARROW)), lambda j, s: (0, pl.multiple_of((s[1] + 2 * j) * NARROW, NARROW))), pl.BlockSpec(info.shape, full), HBM, HBM, HBM],
             out_specs=(pl.BlockSpec((rows, 2 * NARROW), lambda j, s: (slot, j)), pl.BlockSpec((rows, d), lambda j, s: (slot, 0)), pl.BlockSpec((8, 128), full)),
-            scratch_shapes=row_scratch(rows)),
+            scratch_shapes=row_scratch(rows) + [pltpu.SMEM((1,), jnp.int32)]),
         input_output_aliases={1 + n + 2: 0, 1 + n + 3: 1},
         compiler_params=params("arbitrary"),
         cost_estimate=pl.CostEstimate(flops=2 * rows * d * BLOCK_COLS, bytes_accessed=BLOCK_COLS * 2 * (d + rows) + 6 * rows * d, transcendentals=rows * BLOCK_COLS),
@@ -317,20 +305,27 @@
 
     @pl.when(pl.program_id(0) == 0)
     def _():
-        ut_ref[...] = u_ref[...].T
-
-    g = lax.dot_general(ut_ref[...], e_ref[...], NN, preferred_element_type=jnp.float32)
-    half = g.shape[0] // 2
-
-    @pl.when(start_ref[0] == 0)
-    def _():
-        keep_ref[...] = g[:half]
-        give_ref[...] = g[half:]
-
-    @pl.when(start_ref[0] == 1)
-    def _():
-        keep_ref[...] = g[half:]
-        give_ref[...] = g[:half]
+        @pl.loop(0, u_ref.shape[0] // 512)
+        def _(i):
+            r = pl.ds(pl.multiple_of(i * 512, 512), 512)
+            ut_ref[:, r] = u_ref[r, :].T
+
+    half = ut_ref.shape[0] // 2
+
+    @pl.loop(0, e_ref.shape[1] // NARROW)
+    def _(i):
+        c = pl.ds(pl.multiple_of(i * NARROW, NARROW), NARROW)
+        g = lax.dot_general(ut_ref[...], e_ref[:, c], NN, preferred_element_type=jnp.float32)
+
+        @pl.when(start_ref[0] == 0)
+        def _():
+            keep_ref[:, c] = g[:half]
+            give_ref[:, c] = g[half:]
+
+        @pl.when(start_ref[0] == 1)
+        def _():
+            keep_ref[:, c] = g[half:]
+            give_ref[:, c] = g[:half]
 
 
 def run_grad_w(where, u_all, e_all, dep, part, parts, previous=()):
@@ -442,17 +437,15 @@
         row_w = (weights * loss_coefs[:, None]).reshape(2 * rows)
         labels = labels.reshape(2 * rows).astype(jnp.float32)
 
-        u_cls, near, c0, c1a, c1b = run_norm(tp.reshape(1).astype(jnp.int32), h_main, h_mtp, gains)
+        u_cls, near, c0, c1 = run_norm(tp.reshape(1).astype(jnp.int32), h_main, h_mtp, gains)
         nx, ny = hop(near, X), hop(near, Y)
         c0x, c0y = hop(c0, X), hop(c0, Y)
-        c1ax, c1ay = hop(c1a, X), hop(c1a, Y)
-        c1bx, c1by = hop(c1b, X), hop(c1b, Y)
+        c1x, c1y = hop(c1, X), hop(c1, Y)
         nd = hop(ny, X)
         c0d = hop(c0x, Y)
-        c1ad = hop(c1ay, X)
-        c1bd = hop(c1bx, Y)
+        c1d = hop(c1, X | Y)
         zx, zy, zd = hop_tp(nx), hop_tp(ny), hop_tp(nd)
-        pieces = {X: (nx, zx, c0x, c1ax, c1bx), Y: (ny, zy, c0y, c1ay, c1by), X | Y: (nd, zd, c0d, c1ad, c1bd)}
+        pieces = {X: (nx, zx, c0x, c1x), Y: (ny, zy, c0y, c1y), X | Y: (nd, zd, c0d, c1d)}
 
         z, stats = run_logits(start, u_cls, w_out, labels[None], 2 * rows)
         other = hop_tp(stats)
@@ -469,40 +462,33 @@
         near_far = jnp.stack([jnp.where(tp == 0, a, b), jnp.where(tp == 0, b, a)], axis=1)
         info_sent = jnp.concatenate([near_far, jnp.swapaxes(v[:, :, 2:], 1, 2)], axis=1).reshape(4, 2 * rows)
         infos = {d: hop(info_sent, d) for d in (X, Y, X | Y)}
-        start_all = jnp.concatenate([start, jnp.stack([infos[d][3, 0] for d in (X, Y, X | Y)]).astype(jnp.int32)])
-
-        part0 = run_du(start, z, w_out, info, stats, 0, rows)
-        other0 = hop_tp(part0)
-        e_cls = run_own_e(start, z, info, part0)
-
-        token = part0
+
+        part, e_cls = run_du(start, z, w_out, info)
+        other = hop_tp(part)
+        token = stats
         for slot, d in enumerate((X, Y, X | Y)):
-            e_cls, u_cls, token = run_class_e(start_all, pieces[d], w_out, infos[d], e_cls, u_cls, token, slot + 1)
+            e_cls, u_cls, token = run_class_e(start, pieces[d], w_out, infos[d], e_cls, u_cls, token, slot + 1)
 
         blk = d_model // n_dp
         recv = {}
         dep, previous, send = token, (), None
         for tag in CHAIN:
-            d, part = int(tag[0]), int(tag[1])
+            d, half = int(tag[0]), int(tag[1])
             where = jnp.stack([core, chip ^ (d // 2)]).astype(jnp.int32)
             last = d == 0
-            keep, give, *total = run_grad_w(where, u_cls, e_cls, dep, part, 1 if last else 2, previous)
+            keep, give, *total = run_grad_w(where, u_cls, e_cls, dep, half, 1 if last else 2, previous)
             if send:
                 recv[send] = (hop(total[0], int(send[0])),)
             got = hop(give, CORE)
             previous, send, dep = (keep, got), tag, keep
             if last:
                 recv[tag] = (keep, got)
-            elif tag == CHAIN[-2]:
+            elif tag in (CHAIN[0], CHAIN[-2]):
                 dep = keep + got
                 recv[tag] = (hop(dep, d),)
                 previous, send = (), None
-            elif tag == DU1_AFTER:
-                part1 = run_du(start, z, w_out, info, keep, 1, rows)
-                other1 = hop_tp(part1)
-                dep = part1
-        gh0, gg0 = run_norm_back(h_main, part0, other0, gains[:1], keep)
-        gh1, gg1 = run_norm_back(h_mtp, part1, other1, gains[1:], gg0)
+        gh0, gg0 = run_norm_back(h_main, part, other, gains[:1], 0, keep)
+        gh1, gg1 = run_norm_back(h_mtp, part, other, gains[1:], 1, gg0)
         sums = jnp.concatenate([gg0.reshape(-1), gg1.reshape(-1), jnp.broadcast_to(loss_part, (128,))])
         for bit in (CORE, X, Y):
             sums = sums + hop(sums, bit)

time: 815 us -> 817 us (level)
  waiting for transfers between devices: 292 us -> 320 us
  starting transfers between devices: 51.8 us -> 41.7 us
  Pallas kernels: 430 us -> 420 us
    ppermute x35 -> x32, waiting for transfers between devices: 180 us -> 227 us  [hop(): return lax.ppermute(x, 'dp', [(i, i ^ bit) for i in range(n_dp)])]
    ppermute x6 -> x5, waiting for transfers between devices: 112 us -> 92.8 us  [hop_tp(): return lax.ppermute(x, 'tp', [(0, 1), (1, 0)])]
    pallas_call x7 -> x5, Pallas kernels: 261 us -> 244 us  [the longest x1 86.3 us: run_logits(): pl.pallas_call(functools.partial(logits_kernel, sub=256), out_shape=(jax....]
    ppermute x35 -> x32, starting transfers between devices: 44.8 us -> 37.2 us  [hop(): return lax.ppermute(x, 'dp', [(i, i ^ bit) for i in range(n_dp)])]
  transfers between devices with their start and end apart: 41 -> 37, of which waited for: 19 -> 18; matrix products, arithmetic and copies ran while one was open for 2% -> 2% of each run, Pallas kernels for 38% -> 38%
where the time goes in v3:
time: 817 us; the launch traced here: 811 us
  Pallas kernels  420 us (51%)
  waiting for transfers between devices  320 us (39%)
  starting transfers between devices  41.7 us (5%)
  other arithmetic  15.7 us (2%)
  local copies, waits for them, and re-layouts  9.75 us (1%)
    ppermute x32, waiting for transfers between devices, hop(): return lax.ppermute(x, 'dp', [(i, i ^ bit) for i in range(n_dp)])  227 us
    pallas_call x7, Pallas kernels, run_grad_w(): pl.pallas_call(grad_w_kernel, out_shape=(jax.ShapeDtypeStruct((blk // 2,...  137 us
    ppermute x5, waiting for transfers between devices, hop_tp(): return lax.ppermute(x, 'tp', [(0, 1), (1, 0)])  92.8 us
    pallas_call x1, Pallas kernels, run_logits(): pl.pallas_call(functools.partial(logits_kernel, sub=256), out_shape=(jax....  86.3 us
    pallas_call x1, Pallas kernels, run_du(): pl.pallas_call(du_kernel, out_shape=(jax.ShapeDtypeStruct((rows, d), jnp....  86 us
    pallas_call x3, Pallas kernels, run_class_e(): pl.pallas_call(functools.partial(class_e_kernel, quarter=rows // 4), out_...  71.7 us
    ppermute x32, starting transfers between devices, hop(): return lax.ppermute(x, 'dp', [(i, i ^ bit) for i in range(n_dp)])  37.2 us
  transfers between devices with their start and end apart: 37, of which 18 were waited for; matrix products, arithmetic and copies ran while one was open for 2% of the time, Pallas kernels for 38%

profile of v3, /device:TPU:0, one launch (start us, length us, event | category | flops | bytes accessed | tf_op | source)
XLA Modules:
  0.0 810.7 jit_solution(1047094641222888344)
XLA Ops:
  2.0 9.3 %norm.1 = (bf16[4096,2048]{1,0:T(8,128)(2,1)}, f32[256,2048]{1,0:T(8,128)}, f32[256,2048]{1,0:T(8,128)}, f32[256,2048]{1,0:T(8,128)}) custom-call(s32[1]{0:T(128)} %bitcast.2.tp_ref, bf16[1,512,2048]{2,1,0:T(8,128)(2,1)} %h_ref.2, bf16[1,512,2048]{2,1,0:T(8,128)(2,1)} %h_ref.3, f32[2,2048]{1,0:T(2,128)} %pad_maximum_fusion.1.gain_ref), custom_call_target="tpu_custom_call" | custom-call | flops 8388608000 | bytes 14680064 | tf_op jit(solution)/shard_map/norm/pallas_call | solution.py:61
  17.2 86.3 %logits.1 = (f32[1024,16128]{1,0:T(8,128)}, f32[3,1024]{1,0:T(4,128)}) custom-call(s32[2]{0:T(128)} %pad_add_fusion.start_ref, bf16[4096,2048]{1,0:T(8,128)(2,1)} %get-tuple-element.45.u_ref.refs_7_, bf16[2048,16128]{1,0:T(8,128)(2,1)} %refs_4_.5, f32[1,1024]{1,0:T(1,128)} %bitcast.50), custom_call_target="tpu_custom_call" | custom-call | flops 67645734912 | bytes 132120576 | tf_op jit(solution)/shard_map/logits/pallas_call | solution.py:154
  109.5 44.2 %collective-permute-done.2 = f32[2]{0:T(128)S(1)} collective-permute-done((f32[2]{0:T(128)S(1)}, f32[2]{0:T(128)S(1)}, u32[]{:S(2)}, u32[]{:S(2)}) %collective-permute-start.2) | collective-permute-done | bytes 40 | tf_op jit(solution)/shard_map/ppermute | solution.py:411
  157.7 4.0 collective-permute-done.4
  168.3 38.9 %collective-permute-done.20.refs_5_ = f32[4,1024]{1,0:T(4,128)S(1)} collective-permute-done((f32[4,1024]{1,0:T(4,128)S(1)}, f32[4,1024]{1,0:T(4,128)S(1)}, u32[]{:S(2)}, u32[]{:S(2)}) %collective-permute-start.20) | collective-permute-done | bytes 16416 | tf_op jit(solution)/shard_map/ppermute | solution.py:411
  215.7 86.0 %du.1 = (f32[1024,2048]{1,0:T(8,128)}, bf16[4096,4096]{1,0:T(8,128)(2,1)}) custom-call(s32[2]{0:T(128)} %pad_add_fusion.start_ref, f32[1024,16128]{1,0:T(8,128)} %get-tuple-element.46.z_ref, bf16[2048,16128]{1,0:T(8,128)(2,1)} %refs_4_.5, f32[4,1024]{1,0:T(4,128)} %maximum_maximum_fusion.info_ref), custom_call_target="tpu_custom_call" | custom-call | flops 67645734912 | bytes 132120576 | tf_op jit(solution)/shard_map/du/pallas_call | solution.py:225
  305.2 21.8 %class_e.3 = (bf16[4096,4096]{1,0:T(8,128)(2,1)}, bf16[4096,2048]{1,0:T(8,128)(2,1)}, f32[8,128]{1,0:T(8,128)}) custom-call(s32[2]{0:T(128)} %pad_add_fusion.start_ref, f32[256,2048]{1,0:T(8,128)} %collective-permute-done.17.refs_0_, f32[256,2048]{1,0:T(8,128)} %collective-permute-done.18.refs_1_, ...), custom_call_target="tpu_custom_call", output_to_operand_aliasing={{0}: (7, {}), {1}: (8, {})} | custom-call | flops 17179869184 | bytes 37748736 | tf_op jit(solution)/shard_map/class_e/pallas_call | solution.py:283
  327.1 3.5 collective-permute-start.12
  330.6 25.0 %class_e.4 = (bf16[4096,4096]{1,0:T(8,128)(2,1)}, bf16[4096,2048]{1,0:T(8,128)(2,1)}, f32[8,128]{1,0:T(8,128)}) custom-call(s32[2]{0:T(128)} %pad_add_fusion.start_ref, f32[256,2048]{1,0:T(8,128)} %copy-done.1, f32[256,2048]{1,0:T(8,128)} %collective-permute-done.13.refs_1_, ...), custom_call_target="tpu_custom_call", output_to_operand_aliasing={{0}: (7, {}), {1}: (8, {})} | custom-call | flops 17179869184 | bytes 37748736 | tf_op jit(solution)/shard_map/class_e/pallas_call | solution.py:283
  355.6 34.5 %collective-permute-done.10.refs_2_ = f32[256,2048]{1,0:T(8,128)} collective-permute-done((f32[256,2048]{1,0:T(8,128)}, f32[256,2048]{1,0:T(8,128)}, u32[]{:S(2)}, u32[]{:S(2)}) %collective-permute-start.10) | collective-permute-done | bytes 2097184 | tf_op jit(solution)/shard_map/ppermute | solution.py:411
  390.1 24.8 %class_e.5 = (bf16[4096,4096]{1,0:T(8,128)(2,1)}, bf16[4096,2048]{1,0:T(8,128)(2,1)}, f32[8,128]{1,0:T(8,128)}) custom-call(s32[2]{0:T(128)} %pad_add_fusion.start_ref, f32[256,2048]{1,0:T(8,128)} %collective-permute-done.7.refs_0_, f32[256,2048]{1,0:T(8,128)} %collective-permute-done.8.refs_1_, ...), custom_call_target="tpu_custom_call", output_to_operand_aliasing={{0}: (7, {}), {1}: (8, {})} | custom-call | flops 17179869184 | bytes 37748736 | tf_op jit(solution)/shard_map/class_e/pallas_call | solution.py:283
  414.9 17.2 %grad_w.7 = (f32[256,2048]{1,0:T(8,128)}, f32[256,2048]{1,0:T(8,128)}) custom-call(s32[2]{0:T(128)} %pad_add_fusion.4.start_ref, bf16[4096,2048]{1,0:T(8,128)(2,1)} %get-tuple-element.59.u_ref, bf16[4096,4096]{1,0:T(8,128)(2,1)} %get-tuple-element.60.e_ref, f32[8,128]{1,0:T(8,128)} %get-tuple-element.61._), custom_call_target="tpu_custom_call" | custom-call | flops 8589934592 | bytes 25165824 | tf_op jit(solution)/shard_map/grad_w/pallas_call | solution.py:338
  432.1 4.4 collective-permute-done.21
  439.7 17.3 %grad_w.8 = (f32[256,2048]{1,0:T(8,128)}, f32[256,2048]{1,0:T(8,128)}) custom-call(s32[2]{0:T(128)} %pad_add_fusion.4.start_ref, bf16[4096,2048]{1,0:T(8,128)(2,1)} %get-tuple-element.59.u_ref, bf16[4096,4096]{1,0:T(8,128)(2,1)} %get-tuple-element.60.e_ref, f32[256,2048]{1,0:T(8,128)} %add.72._), custom_call_target="tpu_custom_call" | custom-call | flops 8589934592 | bytes 25165824 | tf_op jit(solution)/shard_map/grad_w/pallas_call | solution.py:338
  457.8 3.5 collective-permute-done.22.refs_1_
  462.7 18.5 %grad_w.9 = (f32[256,2048]{1,0:T(8,128)}, f32[256,2048]{1,0:T(8,128)}, f32[256,2048]{1,0:T(8,128)}) custom-call(s32[2]{0:T(128)} %pad_add_fusion.3.start_ref, bf16[4096,2048]{1,0:T(8,128)(2,1)} %get-tuple-element.59.u_ref, bf16[4096,4096]{1,0:T(8,128)(2,1)} %get-tuple-element.60.e_ref, f32[256,2048]{1,0:T(8,128)} %get-tuple-element.64._.refs_0_, ...), custom_call_target="tpu_custom_call" | custom-call | flops 8589934592 | bytes 25165824 | tf_op jit(solution)/shard_map/grad_w/pallas_call | solution.py:338
  486.9 18.8 %grad_w.10 = (f32[256,2048]{1,0:T(8,128)}, f32[256,2048]{1,0:T(8,128)}, f32[256,2048]{1,0:T(8,128)}) custom-call(s32[2]{0:T(128)} %pad_add_fusion.2.start_ref, bf16[4096,2048]{1,0:T(8,128)(2,1)} %get-tuple-element.59.u_ref, bf16[4096,4096]{1,0:T(8,128)(2,1)} %get-tuple-element.60.e_ref, f32[256,2048]{1,0:T(8,128)} %get-tuple-element.66._.refs_0_, ...), custom_call_target="tpu_custom_call" | custom-call | flops 8589934592 | bytes 25165824 | tf_op jit(solution)/shard_map/grad_w/pallas_call | solution.py:338
  506.5 3.6 collective-permute-done.24.refs_1_
  511.4 18.7 %grad_w.11 = (f32[256,2048]{1,0:T(8,128)}, f32[256,2048]{1,0:T(8,128)}, f32[256,2048]{1,0:T(8,128)}) custom-call(s32[2]{0:T(128)} %pad_add_fusion.3.start_ref, bf16[4096,2048]{1,0:T(8,128)(2,1)} %get-tuple-element.59.u_ref, bf16[4096,4096]{1,0:T(8,128)(2,1)} %get-tuple-element.60.e_ref, f32[256,2048]{1,0:T(8,128)} %get-tuple-element.68._.refs_0_, ...), custom_call_target="tpu_custom_call" | custom-call | flops 8589934592 | bytes 25165824 | tf_op jit(solution)/shard_map/grad_w/pallas_call | solution.py:338
  530.5 4.0 collective-permute-done.25.refs_1_
  535.8 18.6 %grad_w.12 = (f32[256,2048]{1,0:T(8,128)}, f32[256,2048]{1,0:T(8,128)}, f32[256,2048]{1,0:T(8,128)}) custom-call(s32[2]{0:T(128)} %pad_add_fusion.2.start_ref, bf16[4096,2048]{1,0:T(8,128)(2,1)} %get-tuple-element.59.u_ref, bf16[4096,4096]{1,0:T(8,128)(2,1)} %get-tuple-element.60.e_ref, f32[256,2048]{1,0:T(8,128)} %get-tuple-element.70._.refs_0_, ...), custom_call_target="tpu_custom_call" | custom-call | flops 8589934592 | bytes 25165824 | tf_op jit(solution)/shard_map/grad_w/pallas_call | solution.py:338
  562.2 27.9 %grad_w.13 = (f32[256,4096]{1,0:T(8,128)}, f32[256,4096]{1,0:T(8,128)}) custom-call(s32[2]{0:T(128)} %pad_add_fusion.1.start_ref, bf16[4096,2048]{1,0:T(8,128)(2,1)} %get-tuple-element.59.u_ref, bf16[4096,4096]{1,0:T(8,128)(2,1)} %get-tuple-element.60.e_ref, f32[256,2048]{1,0:T(8,128)} %add.73._), custom_call_target="tpu_custom_call" | custom-call | flops 17179869184 | bytes 46137344 | tf_op jit(solution)/shard_map/grad_w/pallas_call | solution.py:338
  590.7 5.3 collective-permute-start.33
  596.1 92.8 %collective-permute-done.5.b_ref = f32[1024,2048]{1,0:T(8,128)} collective-permute-done((f32[1024,2048]{1,0:T(8,128)}, f32[1024,2048]{1,0:T(8,128)}, u32[]{:S(2)}, u32[]{:S(2)}) %collective-permute-start.5) | collective-permute-done | bytes 8388640 | tf_op jit(solution)/shard_map/ppermute | solution.py:414
  688.9 7.2 norm_back.2
  696.0 7.2 norm_back.3
  706.5 3.9 collective-permute-start.28
  716.5 43.4 %collective-permute-done.29 = f32[4224]{0:T(1024)S(1)} collective-permute-done((f32[4224]{0:T(1024)S(1)}, f32[4224]{0:T(1024)S(1)}, u32[]{:S(2)}, u32[]{:S(2)}) %collective-permute-start.29) | collective-permute-done | bytes 16928 | tf_op jit(solution)/shard_map/ppermute | solution.py:411
  764.0 11.1 %place.2.refs_2_ = f32[256,16128]{1,0:T(8,128)} custom-call(s32[5]{0:T(128)} %stack.131.at_ref, f32[256,4096]{1,0:T(8,128)} %get-tuple-element.74._.refs_0_, f32[256,4096]{1,0:T(8,128)} %collective-permute-done.32.refs_1_, f32[256,2048]{1,0:T(8,128)} %collective-permute-done.33.refs_2_, f32[256,2048]{1,0:T(8,128)} %collective-permute-done.34.refs_3_, ...), custom_call_target="tpu_custom_call" | custom-call | flops 838860800 | bytes 33554432 | tf_op jit(solution)/shard_map/place/pallas_call | solution.py:392
  775.1 27.9 %collective-permute-done.30.refs_0_ = f32[256,2048]{1,0:T(8,128)S(1)} collective-permute-done((f32[256,2048]{1,0:T(8,128)}, f32[256,2048]{1,0:T(8,128)S(1)}, u32[]{:S(2)}, u32[]{:S(2)}) %collective-permute-start.30) | collective-permute-done | bytes 2097184 | tf_op jit(solution)/shard_map/ppermute | solution.py:411
  803.0 3.6 collective-permute-done.31.refs_1_
  806.5 4.0 place.3
  (133 shorter events, 70.0 us)
Async XLA Ops:
  11.2 200.3 %collective-permute-start.17 = (f32[256,2048]{1,0:T(8,128)}, f32[256,2048]{1,0:T(8,128)}, u32[]{:S(2)}, u32[]{:S(2)}) collective-permute-start(f32[256,2048]{1,0:T(8,128)} %get-tuple-element.49), channel_id=1, source_target_pairs={{0,2},{1,3},{2,0},{3,1},{4,6},{5,7},{6,4},{7,5},{8,10},{9,11},{10,... | collective-permute-start | bytes 6291464 | tf_op jit(solution)/shard_map/ppermute | solution.py:411
  14.4 198.7 %collective-permute-start.6 = (f32[256,2048]{1,0:T(8,128)}, f32[256,2048]{1,0:T(8,128)S(1)}, u32[]{:S(2)}, u32[]{:S(2)}) collective-permute-start(f32[256,2048]{1,0:T(8,128)} %get-tuple-element.49), channel_id=1, source_target_pairs={{0,4},{1,5},{2,6},{3,7},{4,0},{5,1},{6,2},{7,3},{8,12},{9,13},{10,... | collective-permute-start | bytes 6291464 | tf_op jit(solution)/shard_map/ppermute | solution.py:411
  103.6 60.9 %collective-permute-start = (f32[3,1024]{1,0:T(4,128)}, f32[3,1024]{1,0:T(4,128)S(1)}, u32[]{:S(2)}, u32[]{:S(2)}) collective-permute-start(f32[3,1024]{1,0:T(4,128)} %get-tuple-element.47.refs_8_), channel_id=1, source_target_pairs={{0,8},{8,0},{1,9},{9,1},{2,10},{10,2},{3,11},{11,3},{4,12},{12,4},... | collective-permute-start | bytes 36872 | tf_op jit(solution)/shard_map/ppermute | solution.py:414
  105.3 108.2 %collective-permute-start.19 = (f32[256,2048]{1,0:T(8,128)}, f32[256,2048]{1,0:T(8,128)}, u32[]{:S(2)}, u32[]{:S(2)}) collective-permute-start(f32[256,2048]{1,0:T(8,128)} %get-tuple-element.51), channel_id=1, source_target_pairs={{0,2},{1,3},{2,0},{3,1},{4,6},{5,7},{6,4},{7,5},{8,10},{9,11},{10,... | collective-permute-start | bytes 6291464 | tf_op jit(solution)/shard_map/ppermute | solution.py:411
  108.1 45.6 %collective-permute-start.2 = (f32[2]{0:T(128)S(1)}, f32[2]{0:T(128)S(1)}, u32[]{:S(2)}, u32[]{:S(2)}) collective-permute-start(f32[2]{0:T(128)S(1)} %add.67), channel_id=1, source_target_pairs={{0,2},{1,3},{2,0},{3,1},{4,6},{5,7},{6,4},{7,5},{8,10},{9,11},{10,... | collective-permute-start | bytes 32 | tf_op jit(solution)/shard_map/ppermute | solution.py:411
  157.3 4.5 collective-permute-start.4
  161.7 52.4 %collective-permute-start.9 = (f32[256,2048]{1,0:T(8,128)}, f32[256,2048]{1,0:T(8,128)}, u32[]{:S(2)}, u32[]{:S(2)}) collective-permute-start(f32[256,2048]{1,0:T(8,128)} %get-tuple-element.50), channel_id=1, source_target_pairs={{0,2},{1,3},{2,0},{3,1},{4,6},{5,7},{6,4},{7,5},{8,10},{9,11},{10,... | collective-permute-start | bytes 6291464 | tf_op jit(solution)/shard_map/ppermute | solution.py:411
  166.1 41.0 %collective-permute-start.20 = (f32[4,1024]{1,0:T(4,128)S(1)}, f32[4,1024]{1,0:T(4,128)S(1)}, u32[]{:S(2)}, u32[]{:S(2)}) collective-permute-start(f32[4,1024]{1,0:T(4,128)S(1)} %reshape.155), channel_id=1, source_target_pairs={{0,2},{1,3},{2,0},{3,1},{4,6},{5,7},{6,4},{7,5},{8,10},{9,11},{10,... | collective-permute-start | bytes 49160 | tf_op jit(solution)/shard_map/ppermute | solution.py:411
  211.1 90.7 %collective-permute-start.15 = (f32[256,2048]{1,0:T(8,128)}, f32[256,2048]{1,0:T(8,128)}, u32[]{:S(2)}, u32[]{:S(2)}) collective-permute-start(f32[256,2048]{1,0:T(8,128)} %get-tuple-element.51), channel_id=1, source_target_pairs={{0,4},{1,5},{2,6},{3,7},{4,0},{5,1},{6,2},{7,3},{8,12},{9,13},{10,... | collective-permute-start | bytes 6291464 | tf_op jit(solution)/shard_map/ppermute | solution.py:411
  211.6 115.5 %collective-permute-start.14 = (f32[256,2048]{1,0:T(8,128)}, f32[256,2048]{1,0:T(8,128)}, u32[]{:S(2)}, u32[]{:S(2)}) collective-permute-start(f32[256,2048]{1,0:T(8,128)} %get-tuple-element.50), channel_id=1, source_target_pairs={{0,4},{1,5},{2,6},{3,7},{4,0},{5,1},{6,2},{7,3},{8,12},{9,13},{10,... | collective-permute-start | bytes 6291464 | tf_op jit(solution)/shard_map/ppermute | solution.py:411
  213.1 117.5 %collective-permute-start.13 = (f32[256,2048]{1,0:T(8,128)S(1)}, f32[256,2048]{1,0:T(8,128)}, u32[]{:S(2)}, u32[]{:S(2)}) collective-permute-start(f32[256,2048]{1,0:T(8,128)S(1)} %collective-permute-done.6.refs_0_), channel_id=1, source_target_pairs={{0,8},{8,0},{1,9},{9,1},{2,10},{10,2},{3,11},{11,3},{4,12},{12,4},... | collective-permute-start | bytes 6291464 | tf_op jit(solution)/shard_map/ppermute | solution.py:414
  213.5 91.2 %collective-permute-start.7 = (f32[256,2048]{1,0:T(8,128)S(1)}, f32[256,2048]{1,0:T(8,128)}, u32[]{:S(2)}, u32[]{:S(2)}) collective-permute-start(f32[256,2048]{1,0:T(8,128)S(1)} %collective-permute-done.6.refs_0_), channel_id=1, source_target_pairs={{0,2},{1,3},{2,0},{3,1},{4,6},{5,7},{6,4},{7,5},{8,10},{9,11},{10,... | collective-permute-start | bytes 6291464 | tf_op jit(solution)/shard_map/ppermute | solution.py:411
  214.1 89.2 %collective-permute-start.18 = (f32[256,2048]{1,0:T(8,128)}, f32[256,2048]{1,0:T(8,128)}, u32[]{:S(2)}, u32[]{:S(2)}) collective-permute-start(f32[256,2048]{1,0:T(8,128)} %collective-permute-done.17.refs_0_), channel_id=1, source_target_pairs={{0,8},{8,0},{1,9},{9,1},{2,10},{10,2},{3,11},{11,3},{4,12},{12,4},... | collective-permute-start | bytes 6291464 | tf_op jit(solution)/shard_map/ppermute | solution.py:414
  301.8 53.8 %collective-permute-start.11 = (f32[256,2048]{1,0:T(8,128)}, f32[256,2048]{1,0:T(8,128)}, u32[]{:S(2)}, u32[]{:S(2)}) collective-permute-start(f32[256,2048]{1,0:T(8,128)} %get-tuple-element.51), channel_id=1, source_target_pairs={{0,6},{1,7},{2,4},{3,5},{4,2},{5,3},{6,0},{7,1},{8,14},{9,15},{10,... | collective-permute-start | bytes 6291464 | tf_op jit(solution)/shard_map/ppermute | solution.py:411
  303.3 86.8 %collective-permute-start.10 = (f32[256,2048]{1,0:T(8,128)}, f32[256,2048]{1,0:T(8,128)}, u32[]{:S(2)}, u32[]{:S(2)}) collective-permute-start(f32[256,2048]{1,0:T(8,128)} %collective-permute-done.9.refs_2_), channel_id=1, source_target_pairs={{0,4},{1,5},{2,6},{3,7},{4,0},{5,1},{6,2},{7,3},{8,12},{9,13},{10,... | collective-permute-start | bytes 6291464 | tf_op jit(solution)/shard_map/ppermute | solution.py:411
  304.8 85.3 %collective-permute-start.8 = (f32[256,2048]{1,0:T(8,128)}, f32[256,2048]{1,0:T(8,128)}, u32[]{:S(2)}, u32[]{:S(2)}) collective-permute-start(f32[256,2048]{1,0:T(8,128)} %collective-permute-done.7.refs_0_), channel_id=1, source_target_pairs={{0,8},{8,0},{1,9},{9,1},{2,10},{10,2},{3,11},{11,3},{4,12},{12,4},... | collective-permute-start | bytes 6291464 | tf_op jit(solution)/shard_map/ppermute | solution.py:414
  327.1 28.5 %collective-permute-start.12 = (f32[4,1024]{1,0:T(4,128)S(1)}, f32[4,1024]{1,0:T(4,128)S(1)}, u32[]{:S(2)}, u32[]{:S(2)}) collective-permute-start(f32[4,1024]{1,0:T(4,128)S(1)} %reshape.155), channel_id=1, source_target_pairs={{0,6},{1,7},{2,4},{3,5},{4,2},{5,3},{6,0},{7,1},{8,14},{9,15},{10,... | collective-permute-start | bytes 49160 | tf_op jit(solution)/shard_map/ppermute | solution.py:411
  432.1 4.4 collective-permute-start.21
  456.9 4.4 collective-permute-start.22
  505.7 4.4 collective-permute-start.24
  506.1 182.8 %collective-permute-start.5 = (f32[1024,2048]{1,0:T(8,128)}, f32[1024,2048]{1,0:T(8,128)}, u32[]{:S(2)}, u32[]{:S(2)}) collective-permute-start(f32[1024,2048]{1,0:T(8,128)} %get-tuple-element.48.a_ref), channel_id=1, source_target_pairs={{0,8},{8,0},{1,9},{9,1},{2,10},{10,2},{3,11},{11,3},{4,12},{12,4},... | collective-permute-start | bytes 25165832 | tf_op jit(solution)/shard_map/ppermute | solution.py:414
  530.1 4.4 collective-permute-start.25
  554.5 4.5 collective-permute-start.26
  590.1 173.9 %collective-permute-start.32 = (f32[256,4096]{1,0:T(8,128)}, f32[256,4096]{1,0:T(8,128)}, u32[]{:S(2)}, u32[]{:S(2)}) collective-permute-start(f32[256,4096]{1,0:T(8,128)} %get-tuple-element.80), channel_id=1, source_target_pairs={{0,1},{1,0},{2,3},{3,2},{4,5},{5,4},{6,7},{7,6},{8,9},{9,8},{10,11... | collective-permute-start | bytes 12582920 | tf_op jit(solution)/shard_map/ppermute | solution.py:411
  590.7 123.4 %collective-permute-start.33 = (f32[256,2048]{1,0:T(8,128)S(1)}, f32[256,2048]{1,0:T(8,128)}, u32[]{:S(2)}, u32[]{:S(2)}) collective-permute-start(f32[256,2048]{1,0:T(8,128)S(1)} %copy-done), channel_id=1, source_target_pairs={{0,6},{1,7},{2,4},{3,5},{4,2},{5,3},{6,0},{7,1},{8,14},{9,15},{10,... | collective-permute-start | bytes 6291464 | tf_op jit(solution)/shard_map/ppermute | solution.py:411
  596.0 118.2 %collective-permute-start.34 = (f32[256,2048]{1,0:T(8,128)}, f32[256,2048]{1,0:T(8,128)}, u32[]{:S(2)}, u32[]{:S(2)}) collective-permute-start(f32[256,2048]{1,0:T(8,128)} %get-tuple-element.81), channel_id=1, source_target_pairs={{0,6},{1,7},{2,4},{3,5},{4,2},{5,3},{6,0},{7,1},{8,14},{9,15},{10,... | collective-permute-start | bytes 6291464 | tf_op jit(solution)/shard_map/ppermute | solution.py:411
  706.5 5.6 collective-permute-start.28
  710.4 53.6 %collective-permute-start.35 = (f32[256,2048]{1,0:T(8,128)}, f32[256,2048]{1,0:T(8,128)}, u32[]{:S(2)}, u32[]{:S(2)}) collective-permute-start(f32[256,2048]{1,0:T(8,128)} %get-tuple-element.82), channel_id=1, source_target_pairs={{0,2},{1,3},{2,0},{3,1},{4,6},{5,7},{6,4},{7,5},{8,10},{9,11},{10,... | collective-permute-start | bytes 6291464 | tf_op jit(solution)/shard_map/ppermute | solution.py:411
  712.2 51.8 %collective-permute-start.36 = (f32[256,2048]{1,0:T(8,128)}, f32[256,2048]{1,0:T(8,128)}, u32[]{:S(2)}, u32[]{:S(2)}) collective-permute-start(f32[256,2048]{1,0:T(8,128)} %get-tuple-element.83), channel_id=1, source_target_pairs={{0,4},{1,5},{2,6},{3,7},{4,0},{5,1},{6,2},{7,3},{8,12},{9,13},{10,... | collective-permute-start | bytes 6291464 | tf_op jit(solution)/shard_map/ppermute | solution.py:411
  714.2 45.7 %collective-permute-start.29 = (f32[4224]{0:T(1024)S(1)}, f32[4224]{0:T(1024)S(1)}, u32[]{:S(2)}, u32[]{:S(2)}) collective-permute-start(f32[4224]{0:T(1024)S(1)} %add.76), channel_id=1, source_target_pairs={{0,4},{1,5},{2,6},{3,7},{4,0},{5,1},{6,2},{7,3},{8,12},{9,13},{10,... | collective-permute-start | bytes 50696 | tf_op jit(solution)/shard_map/ppermute | solution.py:411
  714.2 88.7 %collective-permute-start.30 = (f32[256,2048]{1,0:T(8,128)}, f32[256,2048]{1,0:T(8,128)S(1)}, u32[]{:S(2)}, u32[]{:S(2)}) collective-permute-start(f32[256,2048]{1,0:T(8,128)} %get-tuple-element.79), channel_id=1, source_target_pairs={{0,2},{1,3},{2,0},{3,1},{4,6},{5,7},{6,4},{7,5},{8,10},{9,11},{10,... | collective-permute-start | bytes 6291464 | tf_op jit(solution)/shard_map/ppermute | solution.py:411
  759.9 46.6 %collective-permute-start.31 = (f32[256,2048]{1,0:T(8,128)}, f32[256,2048]{1,0:T(8,128)}, u32[]{:S(2)}, u32[]{:S(2)}) collective-permute-start(f32[256,2048]{1,0:T(8,128)} %add.73._), channel_id=1, source_target_pairs={{0,4},{1,5},{2,6},{3,7},{4,0},{5,1},{6,2},{7,3},{8,12},{9,13},{10,... | collective-permute-start | bytes 6291464 | tf_op jit(solution)/shard_map/ppermute | solution.py:411
  (21 other events, 763.7 us)

commit v4 on v3

--- a/solution.py
+++ b/solution.py
@@ -487,8 +487,10 @@
                 dep = keep + got
                 recv[tag] = (hop(dep, d),)
                 previous, send = (), None
-        gh0, gg0 = run_norm_back(h_main, part, other, gains[:1], 0, keep)
-        gh1, gg1 = run_norm_back(h_mtp, part, other, gains[1:], 1, gg0)
+                if tag == CHAIN[-2]:
+                    gh0, gg0 = run_norm_back(h_main, part, other, gains[:1], 0, dep)
+                    gh1, gg1 = run_norm_back(h_mtp, part, other, gains[1:], 1, gg0)
+                    dep = gg1
         sums = jnp.concatenate([gg0.reshape(-1), gg1.reshape(-1), jnp.broadcast_to(loss_part, (128,))])
         for bit in (CORE, X, Y):
             sums = sums + hop(sums, bit)
@@ -501,8 +503,8 @@
                 at.append((jnp.minimum(src * BLOCK_COLS, shard_vocab - BLOCK_COLS) + int(tag[1]) * (BLOCK_COLS // 2)) // NARROW)
             return run_place(jnp.stack(at).astype(jnp.int32), [recv[t] for t in tags], out, after, (blk, shard_vocab))
 
-        out = place(("00", "60", "61", "20", "40"), None, gg1)
-        out = place(CHAIN[-3:-1], out, gg1)
+        out = place(("00", "60", "61", "20", "40"), None, keep)
+        out = place(CHAIN[-3:-1], out, keep)
         return loss_total, gh0, gh1, out, grad_gain[0], grad_gain[1]
 
 

time: 817 us -> 907 us (1.11)
  waiting for transfers between devices: 320 us -> 412 us
    ppermute x32, waiting for transfers between devices: 227 us -> 309 us  [hop(): return lax.ppermute(x, 'dp', [(i, i ^ bit) for i in range(n_dp)])]
    ppermute x5, waiting for transfers between devices: 92.8 us -> 103 us  [hop_tp(): return lax.ppermute(x, 'tp', [(0, 1), (1, 0)])]
  transfers between devices with their start and end apart: 37 -> 37, of which waited for: 18 -> 18; matrix products, arithmetic and copies ran while one was open for 2% -> 2% of each run, Pallas kernels for 38% -> 32%
where the time goes in v4:
time: 907 us; the launch traced here: 901 us
  Pallas kernels  419 us (46%)
  waiting for transfers between devices  412 us (45%)
  starting transfers between devices  41.1 us (5%)
  other arithmetic  14.2 us (2%)
  local copies, waits for them, and re-layouts  11 us (1%)
    ppermute x32, waiting for transfers between devices, hop(): return lax.ppermute(x, 'dp', [(i, i ^ bit) for i in range(n_dp)])  309 us
    pallas_call x7, Pallas kernels, run_grad_w(): pl.pallas_call(grad_w_kernel, out_shape=(jax.ShapeDtypeStruct((blk // 2,...  137 us
    ppermute x5, waiting for transfers between devices, hop_tp(): return lax.ppermute(x, 'tp', [(0, 1), (1, 0)])  103 us
    pallas_call x1, Pallas kernels, run_logits(): pl.pallas_call(functools.partial(logits_kernel, sub=256), out_shape=(jax....  86.4 us
    pallas_call x1, Pallas kernels, run_du(): pl.pallas_call(du_kernel, out_shape=(jax.ShapeDtypeStruct((rows, d), jnp....  86 us
    pallas_call x3, Pallas kernels, run_class_e(): pl.pallas_call(functools.partial(class_e_kernel, quarter=rows // 4), out_...  71.6 us
    ppermute x32, starting transfers between devices, hop(): return lax.ppermute(x, 'dp', [(i, i ^ bit) for i in range(n_dp)])  36.6 us
  transfers between devices with their start and end apart: 37, of which 18 were waited for; matrix products, arithmetic and copies ran while one was open for 2% of the time, Pallas kernels for 32%

profile of v4, /device:TPU:0, one launch (start us, length us, event | category | flops | bytes accessed | tf_op | source)
XLA Modules:
  0.0 901.5 jit_solution(17855000482528015887)
XLA Ops:
  2.0 9.3 %norm.1 = (bf16[4096,2048]{1,0:T(8,128)(2,1)}, f32[256,2048]{1,0:T(8,128)}, f32[256,2048]{1,0:T(8,128)}, f32[256,2048]{1,0:T(8,128)}) custom-call(s32[1]{0:T(128)} %bitcast.2.tp_ref, bf16[1,512,2048]{2,1,0:T(8,128)(2,1)} %h_ref.2, bf16[1,512,2048]{2,1,0:T(8,128)(2,1)} %h_ref.3, f32[2,2048]{1,0:T(2,128)} %pad_maximum_fusion.1.gain_ref), custom_call_target="tpu_custom_call" | custom-call | flops 8388608000 | bytes 14680064 | tf_op jit(solution)/shard_map/norm/pallas_call | solution.py:61
  17.2 86.4 %logits.1 = (f32[1024,16128]{1,0:T(8,128)}, f32[3,1024]{1,0:T(4,128)}) custom-call(s32[2]{0:T(128)} %pad_add_fusion.start_ref, bf16[4096,2048]{1,0:T(8,128)(2,1)} %get-tuple-element.45.u_ref.refs_7_, bf16[2048,16128]{1,0:T(8,128)(2,1)} %refs_4_.5, f32[1,1024]{1,0:T(1,128)} %bitcast.50), custom_call_target="tpu_custom_call" | custom-call | flops 67645734912 | bytes 132120576 | tf_op jit(solution)/shard_map/logits/pallas_call | solution.py:154
  109.6 44.2 %collective-permute-done.2 = f32[2]{0:T(128)S(1)} collective-permute-done((f32[2]{0:T(128)S(1)}, f32[2]{0:T(128)S(1)}, u32[]{:S(2)}, u32[]{:S(2)}) %collective-permute-start.2) | collective-permute-done | bytes 40 | tf_op jit(solution)/shard_map/ppermute | solution.py:411
  157.8 4.0 collective-permute-done.4
  168.3 38.9 %collective-permute-done.20.refs_5_ = f32[4,1024]{1,0:T(4,128)S(1)} collective-permute-done((f32[4,1024]{1,0:T(4,128)S(1)}, f32[4,1024]{1,0:T(4,128)S(1)}, u32[]{:S(2)}, u32[]{:S(2)}) %collective-permute-start.20) | collective-permute-done | bytes 16416 | tf_op jit(solution)/shard_map/ppermute | solution.py:411
  215.7 86.0 %du.1 = (f32[1024,2048]{1,0:T(8,128)}, bf16[4096,4096]{1,0:T(8,128)(2,1)}) custom-call(s32[2]{0:T(128)} %pad_add_fusion.start_ref, f32[1024,16128]{1,0:T(8,128)} %get-tuple-element.46.z_ref, bf16[2048,16128]{1,0:T(8,128)(2,1)} %refs_4_.5, f32[4,1024]{1,0:T(4,128)} %maximum_maximum_fusion.info_ref), custom_call_target="tpu_custom_call" | custom-call | flops 67645734912 | bytes 132120576 | tf_op jit(solution)/shard_map/du/pallas_call | solution.py:225
  305.2 21.8 %class_e.3 = (bf16[4096,4096]{1,0:T(8,128)(2,1)}, bf16[4096,2048]{1,0:T(8,128)(2,1)}, f32[8,128]{1,0:T(8,128)}) custom-call(s32[2]{0:T(128)} %pad_add_fusion.start_ref, f32[256,2048]{1,0:T(8,128)} %collective-permute-done.17.refs_0_, f32[256,2048]{1,0:T(8,128)} %collective-permute-done.18.refs_1_, ...), custom_call_target="tpu_custom_call", output_to_operand_aliasing={{0}: (7, {}), {1}: (8, {})} | custom-call | flops 17179869184 | bytes 37748736 | tf_op jit(solution)/shard_map/class_e/pallas_call | solution.py:283
  330.5 25.0 %class_e.4 = (bf16[4096,4096]{1,0:T(8,128)(2,1)}, bf16[4096,2048]{1,0:T(8,128)(2,1)}, f32[8,128]{1,0:T(8,128)}) custom-call(s32[2]{0:T(128)} %pad_add_fusion.start_ref, f32[256,2048]{1,0:T(8,128)} %copy-done.1, f32[256,2048]{1,0:T(8,128)} %collective-permute-done.13.refs_1_, ...), custom_call_target="tpu_custom_call", output_to_operand_aliasing={{0}: (7, {}), {1}: (8, {})} | custom-call | flops 17179869184 | bytes 37748736 | tf_op jit(solution)/shard_map/class_e/pallas_call | solution.py:283
  355.5 34.5 %collective-permute-done.10.refs_2_ = f32[256,2048]{1,0:T(8,128)} collective-permute-done((f32[256,2048]{1,0:T(8,128)}, f32[256,2048]{1,0:T(8,128)}, u32[]{:S(2)}, u32[]{:S(2)}) %collective-permute-start.10) | collective-permute-done | bytes 2097184 | tf_op jit(solution)/shard_map/ppermute | solution.py:411
  390.0 24.8 %class_e.5 = (bf16[4096,4096]{1,0:T(8,128)(2,1)}, bf16[4096,2048]{1,0:T(8,128)(2,1)}, f32[8,128]{1,0:T(8,128)}) custom-call(s32[2]{0:T(128)} %pad_add_fusion.start_ref, f32[256,2048]{1,0:T(8,128)} %collective-permute-done.7.refs_0_, f32[256,2048]{1,0:T(8,128)} %collective-permute-done.8.refs_1_, ...), custom_call_target="tpu_custom_call", output_to_operand_aliasing={{0}: (7, {}), {1}: (8, {})} | custom-call | flops 17179869184 | bytes 37748736 | tf_op jit(solution)/shard_map/class_e/pallas_call | solution.py:283
  414.9 17.2 %grad_w.7 = (f32[256,2048]{1,0:T(8,128)}, f32[256,2048]{1,0:T(8,128)}) custom-call(s32[2]{0:T(128)} %pad_add_fusion.3.start_ref, bf16[4096,2048]{1,0:T(8,128)(2,1)} %get-tuple-element.59.u_ref, bf16[4096,4096]{1,0:T(8,128)(2,1)} %get-tuple-element.60.e_ref, f32[8,128]{1,0:T(8,128)} %get-tuple-element.61._), custom_call_target="tpu_custom_call" | custom-call | flops 8589934592 | bytes 25165824 | tf_op jit(solution)/shard_map/grad_w/pallas_call | solution.py:338
  432.0 4.4 collective-permute-done.21
  439.6 17.2 %grad_w.8 = (f32[256,2048]{1,0:T(8,128)}, f32[256,2048]{1,0:T(8,128)}) custom-call(s32[2]{0:T(128)} %pad_add_fusion.3.start_ref, bf16[4096,2048]{1,0:T(8,128)(2,1)} %get-tuple-element.59.u_ref, bf16[4096,4096]{1,0:T(8,128)(2,1)} %get-tuple-element.60.e_ref, f32[256,2048]{1,0:T(8,128)} %add.72._), custom_call_target="tpu_custom_call" | custom-call | flops 8589934592 | bytes 25165824 | tf_op jit(solution)/shard_map/grad_w/pallas_call | solution.py:338
  457.7 3.5 collective-permute-done.22.refs_1_
  462.5 18.5 %grad_w.9 = (f32[256,2048]{1,0:T(8,128)}, f32[256,2048]{1,0:T(8,128)}, f32[256,2048]{1,0:T(8,128)}) custom-call(s32[2]{0:T(128)} %pad_add_fusion.2.start_ref, bf16[4096,2048]{1,0:T(8,128)(2,1)} %get-tuple-element.59.u_ref, bf16[4096,4096]{1,0:T(8,128)(2,1)} %get-tuple-element.60.e_ref, f32[256,2048]{1,0:T(8,128)} %get-tuple-element.64._.refs_0_, ...), custom_call_target="tpu_custom_call" | custom-call | flops 8589934592 | bytes 25165824 | tf_op jit(solution)/shard_map/grad_w/pallas_call | solution.py:338
  486.7 18.7 %grad_w.10 = (f32[256,2048]{1,0:T(8,128)}, f32[256,2048]{1,0:T(8,128)}, f32[256,2048]{1,0:T(8,128)}) custom-call(s32[2]{0:T(128)} %pad_add_fusion.1.start_ref, bf16[4096,2048]{1,0:T(8,128)(2,1)} %get-tuple-element.59.u_ref, bf16[4096,4096]{1,0:T(8,128)(2,1)} %get-tuple-element.60.e_ref, f32[256,2048]{1,0:T(8,128)} %get-tuple-element.66._.refs_0_, ...), custom_call_target="tpu_custom_call" | custom-call | flops 8589934592 | bytes 25165824 | tf_op jit(solution)/shard_map/grad_w/pallas_call | solution.py:338
  505.8 4.0 collective-permute-done.24.refs_1_
  511.1 18.6 %grad_w.11 = (f32[256,2048]{1,0:T(8,128)}, f32[256,2048]{1,0:T(8,128)}, f32[256,2048]{1,0:T(8,128)}) custom-call(s32[2]{0:T(128)} %pad_add_fusion.2.start_ref, bf16[4096,2048]{1,0:T(8,128)(2,1)} %get-tuple-element.59.u_ref, bf16[4096,4096]{1,0:T(8,128)(2,1)} %get-tuple-element.60.e_ref, f32[256,2048]{1,0:T(8,128)} %get-tuple-element.68._.refs_0_, ...), custom_call_target="tpu_custom_call" | custom-call | flops 8589934592 | bytes 25165824 | tf_op jit(solution)/shard_map/grad_w/pallas_call | solution.py:338
  530.2 4.0 collective-permute-done.25.refs_1_
  535.5 18.6 %grad_w.12 = (f32[256,2048]{1,0:T(8,128)}, f32[256,2048]{1,0:T(8,128)}, f32[256,2048]{1,0:T(8,128)}) custom-call(s32[2]{0:T(128)} %pad_add_fusion.1.start_ref, bf16[4096,2048]{1,0:T(8,128)(2,1)} %get-tuple-element.59.u_ref, bf16[4096,4096]{1,0:T(8,128)(2,1)} %get-tuple-element.60.e_ref, f32[256,2048]{1,0:T(8,128)} %get-tuple-element.70._.refs_0_, ...), custom_call_target="tpu_custom_call" | custom-call | flops 8589934592 | bytes 25165824 | tf_op jit(solution)/shard_map/grad_w/pallas_call | solution.py:338
  561.7 103.1 %collective-permute-done.5.b_ref = f32[1024,2048]{1,0:T(8,128)} collective-permute-done((f32[1024,2048]{1,0:T(8,128)}, f32[1024,2048]{1,0:T(8,128)}, u32[]{:S(2)}, u32[]{:S(2)}) %collective-permute-start.5) | collective-permute-done | bytes 8388640 | tf_op jit(solution)/shard_map/ppermute | solution.py:414
  664.8 7.2 norm_back.2
  672.0 7.2 norm_back.3
  679.2 27.8 %grad_w.13 = (f32[256,4096]{1,0:T(8,128)}, f32[256,4096]{1,0:T(8,128)}) custom-call(s32[2]{0:T(128)} %pad_add_fusion.5.start_ref, bf16[4096,2048]{1,0:T(8,128)(2,1)} %get-tuple-element.59.u_ref, bf16[4096,4096]{1,0:T(8,128)(2,1)} %get-tuple-element.60.e_ref, f32[1,2048]{1,0:T(1,128)} %get-tuple-element.75._), custom_call_target="tpu_custom_call" | custom-call | flops 17179869184 | bytes 46137344 | tf_op jit(solution)/shard_map/grad_w/pallas_call | solution.py:338
  707.0 5.4 collective-permute-start.33
  714.5 3.8 collective-permute-start.28
  718.4 85.4 %collective-permute-done.28 = f32[4224]{0:T(1024)S(1)} collective-permute-done((f32[4224]{0:T(1024)S(1)}, f32[4224]{0:T(1024)S(1)}, u32[]{:S(2)}, u32[]{:S(2)}) %collective-permute-start.28) | collective-permute-done | bytes 16928 | tf_op jit(solution)/shard_map/ppermute | solution.py:411
  809.6 41.4 %collective-permute-done.29 = f32[4224]{0:T(1024)S(1)} collective-permute-done((f32[4224]{0:T(1024)S(1)}, f32[4224]{0:T(1024)S(1)}, u32[]{:S(2)}, u32[]{:S(2)}) %collective-permute-start.29) | collective-permute-done | bytes 16928 | tf_op jit(solution)/shard_map/ppermute | solution.py:411
  854.8 11.1 %place.2.refs_2_ = f32[256,16128]{1,0:T(8,128)} custom-call(s32[5]{0:T(128)} %stack.129.at_ref, f32[256,4096]{1,0:T(8,128)} %get-tuple-element.79.refs_0_.refs_6_.refs_3_, f32[256,4096]{1,0:T(8,128)} %collective-permute-done.32.refs_1_, f32[256,2048]{1,0:T(8,128)} %copy-done.2, f32[256,2048]{1,0:T(8,128)} %collective-permute-done.34.refs_3_, ...), custom_call_target="tpu_custom_call" | custom-call | flops 838860800 | bytes 33554432 | tf_op jit(solution)/shard_map/place/pallas_call | solution.py:392
  865.9 27.3 %collective-permute-done.30.refs_0_ = f32[256,2048]{1,0:T(8,128)S(1)} collective-permute-done((f32[256,2048]{1,0:T(8,128)}, f32[256,2048]{1,0:T(8,128)S(1)}, u32[]{:S(2)}, u32[]{:S(2)}) %collective-permute-start.30) | collective-permute-done | bytes 2097184 | tf_op jit(solution)/shard_map/ppermute | solution.py:411
  893.2 4.0 collective-permute-done.31.refs_1_
  897.3 4.0 place.3
  (137 shorter events, 70.6 us)
Async XLA Ops:
  11.2 200.4 %collective-permute-start.17 = (f32[256,2048]{1,0:T(8,128)}, f32[256,2048]{1,0:T(8,128)}, u32[]{:S(2)}, u32[]{:S(2)}) collective-permute-start(f32[256,2048]{1,0:T(8,128)} %get-tuple-element.49), channel_id=1, source_target_pairs={{0,2},{1,3},{2,0},{3,1},{4,6},{5,7},{6,4},{7,5},{8,10},{9,11},{10,... | collective-permute-start | bytes 6291464 | tf_op jit(solution)/shard_map/ppermute | solution.py:411
  14.4 198.7 %collective-permute-start.6 = (f32[256,2048]{1,0:T(8,128)}, f32[256,2048]{1,0:T(8,128)S(1)}, u32[]{:S(2)}, u32[]{:S(2)}) collective-permute-start(f32[256,2048]{1,0:T(8,128)} %get-tuple-element.49), channel_id=1, source_target_pairs={{0,4},{1,5},{2,6},{3,7},{4,0},{5,1},{6,2},{7,3},{8,12},{9,13},{10,... | collective-permute-start | bytes 6291464 | tf_op jit(solution)/shard_map/ppermute | solution.py:411
  103.6 60.9 %collective-permute-start = (f32[3,1024]{1,0:T(4,128)}, f32[3,1024]{1,0:T(4,128)S(1)}, u32[]{:S(2)}, u32[]{:S(2)}) collective-permute-start(f32[3,1024]{1,0:T(4,128)} %get-tuple-element.47.refs_8_), channel_id=1, source_target_pairs={{0,8},{8,0},{1,9},{9,1},{2,10},{10,2},{3,11},{11,3},{4,12},{12,4},... | collective-permute-start | bytes 36872 | tf_op jit(solution)/shard_map/ppermute | solution.py:414
  105.4 108.2 %collective-permute-start.19 = (f32[256,2048]{1,0:T(8,128)}, f32[256,2048]{1,0:T(8,128)}, u32[]{:S(2)}, u32[]{:S(2)}) collective-permute-start(f32[256,2048]{1,0:T(8,128)} %get-tuple-element.51), channel_id=1, source_target_pairs={{0,2},{1,3},{2,0},{3,1},{4,6},{5,7},{6,4},{7,5},{8,10},{9,11},{10,... | collective-permute-start | bytes 6291464 | tf_op jit(solution)/shard_map/ppermute | solution.py:411
  108.1 45.6 %collective-permute-start.2 = (f32[2]{0:T(128)S(1)}, f32[2]{0:T(128)S(1)}, u32[]{:S(2)}, u32[]{:S(2)}) collective-permute-start(f32[2]{0:T(128)S(1)} %add.67), channel_id=1, source_target_pairs={{0,2},{1,3},{2,0},{3,1},{4,6},{5,7},{6,4},{7,5},{8,10},{9,11},{10,... | collective-permute-start | bytes 32 | tf_op jit(solution)/shard_map/ppermute | solution.py:411
  157.3 4.5 collective-permute-start.4
  161.8 52.4 %collective-permute-start.9 = (f32[256,2048]{1,0:T(8,128)}, f32[256,2048]{1,0:T(8,128)}, u32[]{:S(2)}, u32[]{:S(2)}) collective-permute-start(f32[256,2048]{1,0:T(8,128)} %get-tuple-element.50), channel_id=1, source_target_pairs={{0,2},{1,3},{2,0},{3,1},{4,6},{5,7},{6,4},{7,5},{8,10},{9,11},{10,... | collective-permute-start | bytes 6291464 | tf_op jit(solution)/shard_map/ppermute | solution.py:411
  166.2 41.0 %collective-permute-start.20 = (f32[4,1024]{1,0:T(4,128)S(1)}, f32[4,1024]{1,0:T(4,128)S(1)}, u32[]{:S(2)}, u32[]{:S(2)}) collective-permute-start(f32[4,1024]{1,0:T(4,128)S(1)} %reshape.155), channel_id=1, source_target_pairs={{0,2},{1,3},{2,0},{3,1},{4,6},{5,7},{6,4},{7,5},{8,10},{9,11},{10,... | collective-permute-start | bytes 49160 | tf_op jit(solution)/shard_map/ppermute | solution.py:411
  211.1 90.6 %collective-permute-start.15 = (f32[256,2048]{1,0:T(8,128)}, f32[256,2048]{1,0:T(8,128)}, u32[]{:S(2)}, u32[]{:S(2)}) collective-permute-start(f32[256,2048]{1,0:T(8,128)} %get-tuple-element.51), channel_id=1, source_target_pairs={{0,4},{1,5},{2,6},{3,7},{4,0},{5,1},{6,2},{7,3},{8,12},{9,13},{10,... | collective-permute-start | bytes 6291464 | tf_op jit(solution)/shard_map/ppermute | solution.py:411
  211.6 115.4 %collective-permute-start.14 = (f32[256,2048]{1,0:T(8,128)}, f32[256,2048]{1,0:T(8,128)}, u32[]{:S(2)}, u32[]{:S(2)}) collective-permute-start(f32[256,2048]{1,0:T(8,128)} %get-tuple-element.50), channel_id=1, source_target_pairs={{0,4},{1,5},{2,6},{3,7},{4,0},{5,1},{6,2},{7,3},{8,12},{9,13},{10,... | collective-permute-start | bytes 6291464 | tf_op jit(solution)/shard_map/ppermute | solution.py:411
  213.1 117.4 %collective-permute-start.13 = (f32[256,2048]{1,0:T(8,128)S(1)}, f32[256,2048]{1,0:T(8,128)}, u32[]{:S(2)}, u32[]{:S(2)}) collective-permute-start(f32[256,2048]{1,0:T(8,128)S(1)} %collective-permute-done.6.refs_0_), channel_id=1, source_target_pairs={{0,8},{8,0},{1,9},{9,1},{2,10},{10,2},{3,11},{11,3},{4,12},{12,4},... | collective-permute-start | bytes 6291464 | tf_op jit(solution)/shard_map/ppermute | solution.py:414
  213.6 91.1 %collective-permute-start.7 = (f32[256,2048]{1,0:T(8,128)S(1)}, f32[256,2048]{1,0:T(8,128)}, u32[]{:S(2)}, u32[]{:S(2)}) collective-permute-start(f32[256,2048]{1,0:T(8,128)S(1)} %collective-permute-done.6.refs_0_), channel_id=1, source_target_pairs={{0,2},{1,3},{2,0},{3,1},{4,6},{5,7},{6,4},{7,5},{8,10},{9,11},{10,... | collective-permute-start | bytes 6291464 | tf_op jit(solution)/shard_map/ppermute | solution.py:411
  214.1 89.1 %collective-permute-start.18 = (f32[256,2048]{1,0:T(8,128)}, f32[256,2048]{1,0:T(8,128)}, u32[]{:S(2)}, u32[]{:S(2)}) collective-permute-start(f32[256,2048]{1,0:T(8,128)} %collective-permute-done.17.refs_0_), channel_id=1, source_target_pairs={{0,8},{8,0},{1,9},{9,1},{2,10},{10,2},{3,11},{11,3},{4,12},{12,4},... | collective-permute-start | bytes 6291464 | tf_op jit(solution)/shard_map/ppermute | solution.py:414
  301.7 53.8 %collective-permute-start.11 = (f32[256,2048]{1,0:T(8,128)}, f32[256,2048]{1,0:T(8,128)}, u32[]{:S(2)}, u32[]{:S(2)}) collective-permute-start(f32[256,2048]{1,0:T(8,128)} %get-tuple-element.51), channel_id=1, source_target_pairs={{0,6},{1,7},{2,4},{3,5},{4,2},{5,3},{6,0},{7,1},{8,14},{9,15},{10,... | collective-permute-start | bytes 6291464 | tf_op jit(solution)/shard_map/ppermute | solution.py:411
  303.2 86.8 %collective-permute-start.10 = (f32[256,2048]{1,0:T(8,128)}, f32[256,2048]{1,0:T(8,128)}, u32[]{:S(2)}, u32[]{:S(2)}) collective-permute-start(f32[256,2048]{1,0:T(8,128)} %collective-permute-done.9.refs_2_), channel_id=1, source_target_pairs={{0,4},{1,5},{2,6},{3,7},{4,0},{5,1},{6,2},{7,3},{8,12},{9,13},{10,... | collective-permute-start | bytes 6291464 | tf_op jit(solution)/shard_map/ppermute | solution.py:411
  304.7 85.3 %collective-permute-start.8 = (f32[256,2048]{1,0:T(8,128)}, f32[256,2048]{1,0:T(8,128)}, u32[]{:S(2)}, u32[]{:S(2)}) collective-permute-start(f32[256,2048]{1,0:T(8,128)} %collective-permute-done.7.refs_0_), channel_id=1, source_target_pairs={{0,8},{8,0},{1,9},{9,1},{2,10},{10,2},{3,11},{11,3},{4,12},{12,4},... | collective-permute-start | bytes 6291464 | tf_op jit(solution)/shard_map/ppermute | solution.py:414
  327.0 28.5 %collective-permute-start.12 = (f32[4,1024]{1,0:T(4,128)S(1)}, f32[4,1024]{1,0:T(4,128)S(1)}, u32[]{:S(2)}, u32[]{:S(2)}) collective-permute-start(f32[4,1024]{1,0:T(4,128)S(1)} %reshape.155), channel_id=1, source_target_pairs={{0,6},{1,7},{2,4},{3,5},{4,2},{5,3},{6,0},{7,1},{8,14},{9,15},{10,... | collective-permute-start | bytes 49160 | tf_op jit(solution)/shard_map/ppermute | solution.py:411
  432.0 4.4 collective-permute-start.21
  456.9 4.4 collective-permute-start.22
  481.9 182.9 %collective-permute-start.5 = (f32[1024,2048]{1,0:T(8,128)}, f32[1024,2048]{1,0:T(8,128)}, u32[]{:S(2)}, u32[]{:S(2)}) collective-permute-start(f32[1024,2048]{1,0:T(8,128)} %get-tuple-element.48.a_ref), channel_id=1, source_target_pairs={{0,8},{8,0},{1,9},{9,1},{2,10},{10,2},{3,11},{11,3},{4,12},{12,4},... | collective-permute-start | bytes 25165832 | tf_op jit(solution)/shard_map/ppermute | solution.py:414
  505.4 4.4 collective-permute-start.24
  529.7 4.4 collective-permute-start.25
  554.1 4.5 collective-permute-start.26
  707.0 147.8 %collective-permute-start.32 = (f32[256,4096]{1,0:T(8,128)}, f32[256,4096]{1,0:T(8,128)}, u32[]{:S(2)}, u32[]{:S(2)}) collective-permute-start(f32[256,4096]{1,0:T(8,128)} %get-tuple-element.80), channel_id=1, source_target_pairs={{0,1},{1,0},{2,3},{3,2},{4,5},{5,4},{6,7},{7,6},{8,9},{9,8},{10,11... | collective-permute-start | bytes 12582920 | tf_op jit(solution)/shard_map/ppermute | solution.py:411
  707.0 97.8 %collective-permute-start.33 = (f32[256,2048]{1,0:T(8,128)S(1)}, f32[256,2048]{1,0:T(8,128)S(1)}, u32[]{:S(2)}, u32[]{:S(2)}) collective-permute-start(f32[256,2048]{1,0:T(8,128)S(1)} %copy-done), channel_id=1, source_target_pairs={{0,6},{1,7},{2,4},{3,5},{4,2},{5,3},{6,0},{7,1},{8,14},{9,15},{10,... | collective-permute-start | bytes 6291464 | tf_op jit(solution)/shard_map/ppermute | solution.py:411
  712.4 94.8 %collective-permute-start.34 = (f32[256,2048]{1,0:T(8,128)}, f32[256,2048]{1,0:T(8,128)}, u32[]{:S(2)}, u32[]{:S(2)}) collective-permute-start(f32[256,2048]{1,0:T(8,128)} %get-tuple-element.81), channel_id=1, source_target_pairs={{0,6},{1,7},{2,4},{3,5},{4,2},{5,3},{6,0},{7,1},{8,14},{9,15},{10,... | collective-permute-start | bytes 6291464 | tf_op jit(solution)/shard_map/ppermute | solution.py:411
  714.5 89.3 %collective-permute-start.28 = (f32[4224]{0:T(1024)S(1)}, f32[4224]{0:T(1024)S(1)}, u32[]{:S(2)}, u32[]{:S(2)}) collective-permute-start(f32[4224]{0:T(1024)S(1)} %fusion.7), channel_id=1, source_target_pairs={{0,2},{1,3},{2,0},{3,1},{4,6},{5,7},{6,4},{7,5},{8,10},{9,11},{10,... | collective-permute-start | bytes 50696 | tf_op jit(solution)/shard_map/ppermute | solution.py:411
  718.3 136.5 %collective-permute-start.35 = (f32[256,2048]{1,0:T(8,128)}, f32[256,2048]{1,0:T(8,128)}, u32[]{:S(2)}, u32[]{:S(2)}) collective-permute-start(f32[256,2048]{1,0:T(8,128)} %get-tuple-element.82), channel_id=1, source_target_pairs={{0,2},{1,3},{2,0},{3,1},{4,6},{5,7},{6,4},{7,5},{8,10},{9,11},{10,... | collective-permute-start | bytes 6291464 | tf_op jit(solution)/shard_map/ppermute | solution.py:411
  803.8 51.0 %collective-permute-start.36 = (f32[256,2048]{1,0:T(8,128)}, f32[256,2048]{1,0:T(8,128)}, u32[]{:S(2)}, u32[]{:S(2)}) collective-permute-start(f32[256,2048]{1,0:T(8,128)} %get-tuple-element.83), channel_id=1, source_target_pairs={{0,4},{1,5},{2,6},{3,7},{4,0},{5,1},{6,2},{7,3},{8,12},{9,13},{10,... | collective-permute-start | bytes 6291464 | tf_op jit(solution)/shard_map/ppermute | solution.py:411
  806.1 44.9 %collective-permute-start.29 = (f32[4224]{0:T(1024)S(1)}, f32[4224]{0:T(1024)S(1)}, u32[]{:S(2)}, u32[]{:S(2)}) collective-permute-start(f32[4224]{0:T(1024)S(1)} %add.76), channel_id=1, source_target_pairs={{0,4},{1,5},{2,6},{3,7},{4,0},{5,1},{6,2},{7,3},{8,12},{9,13},{10,... | collective-permute-start | bytes 50696 | tf_op jit(solution)/shard_map/ppermute | solution.py:411
  807.2 86.1 %collective-permute-start.30 = (f32[256,2048]{1,0:T(8,128)}, f32[256,2048]{1,0:T(8,128)S(1)}, u32[]{:S(2)}, u32[]{:S(2)}) collective-permute-start(f32[256,2048]{1,0:T(8,128)} %get-tuple-element.78), channel_id=1, source_target_pairs={{0,2},{1,3},{2,0},{3,1},{4,6},{5,7},{6,4},{7,5},{8,10},{9,11},{10,... | collective-permute-start | bytes 6291464 | tf_op jit(solution)/shard_map/ppermute | solution.py:411
  851.1 46.2 %collective-permute-start.31 = (f32[256,2048]{1,0:T(8,128)}, f32[256,2048]{1,0:T(8,128)}, u32[]{:S(2)}, u32[]{:S(2)}) collective-permute-start(f32[256,2048]{1,0:T(8,128)} %add.73._), channel_id=1, source_target_pairs={{0,4},{1,5},{2,6},{3,7},{4,0},{5,1},{6,2},{7,3},{8,12},{9,13},{10,... | collective-permute-start | bytes 6291464 | tf_op jit(solution)/shard_map/ppermute | solution.py:411
  (23 other events, 824.9 us)
